TPU v7x, 256 devices: a whole 4x4x8 slice. The times are simulated.
256 devices in a mesh: seq: 64 (over y_lo, x, z), tensor: 4 (over y_hi, core).
Axes of the slice: x: 4, y: 4 (y_hi: 2, y_lo: 2; y = y_hi * 2 + y_lo), z: 8, core: 2. Of those that a mesh axis runs over, the one named last changes fastest.
Arguments:
- tokens: bfloat16 [32768, 2048], P('seq', 'tensor'), may hold values from -12 to 12
- attn_gain: float32 [2048], replicated, may hold values from 0.1 to 1.9
- w_query: bfloat16 [2048, 2048], P('seq', 'tensor'), as said below
- w_key: bfloat16 [2048, 512], P('seq', 'tensor'), as said below
- w_value: bfloat16 [2048, 512], P('seq', 'tensor'), may hold values from -0.125 to 0.125
- w_out: bfloat16 [2048, 2048], P('tensor', 'seq'), may hold values from -0.125 to 0.125
- mlp_gain: float32 [2048], replicated, may hold values from 0.1 to 1.9
- w_gate: bfloat16 [2048, 5632], P('seq', 'tensor'), may hold values from -0.125 to 0.125
- w_up: bfloat16 [2048, 5632], P('seq', 'tensor'), may hold values from -0.125 to 0.125
- w_down: bfloat16 [5632, 2048], P('tensor', 'seq'), may hold values from -0.078125 to 0.078125
Outputs:
- layer_out: bfloat16 [32768, 2048], P('seq', 'tensor')
Inputs may be any that keep to these rules, and one draw needn't show every extreme that they name: `w_query`: entries are of order 2048 to the power -1/2. `w_key`: entries are of order 2048 to the power -1/2.
All inputs are finite; a program needn't handle non-finite values.
Results may differ from a plain program's by a relative error of at most 0.013.
Values may be sent and summed in bfloat16 or wider, within the bound.
No kernel may reach another device: no remote copies, remote signals or barrier semaphores. Data moves between devices by JAX's collectives and lax.ppermute only.
A program may use at most 128 MiB of HBM per device.

v0:
```python
import jax
import jax.numpy as jnp
from jax import lax
from jax.sharding import Mesh
from jax.sharding import PartitionSpec as P

HEAD_DIM = 128
WINDOW = 1024
SEQ = ("seq_0", "seq_1", "seq_2")


def copy_for_each(value, axis):
    length = lax.axis_size(axis)
    return lax.all_to_all(
        jnp.broadcast_to(value[None], (length, *value.shape)), axis, 0, 0, tiled=True
    )


def in_order(tiles, dim):
    tiles = jnp.moveaxis(tiles, 0, dim)
    shape = tiles.shape
    return tiles.reshape(*shape[:dim], shape[dim] * shape[dim + 1], *shape[dim + 2 :])


def gathered_copies(value, axis, dim):
    tiles = copy_for_each(value, axis)
    return in_order(tiles, dim)


def sent_together(arrays, axis, dim, along):
    ends, at = ([], 0)
    for a in arrays[:-1]:
        at += a.shape[along]
        ends.append(at)
    both = jnp.concatenate(arrays, axis=along)
    return tuple(jnp.split(lax.all_gather(both, axis, axis=dim, tiled=True), ends, axis=along))


def passed_along(block, axis, distance):
    devices = range(lax.axis_size(axis))
    route = [(i - distance, i) for i in devices if i - distance in devices]
    return lax.ppermute(block, axis, route)


def in_blocks(value, dim, length):
    shape = value.shape
    tiles = value.reshape(*shape[:dim], length, shape[dim] // length, *shape[dim + 1 :])
    return jnp.moveaxis(tiles, dim, 0)


def sent_and_summed(value, axis, dim):
    length = lax.axis_size(axis)
    tiles = lax.all_to_all(in_blocks(value, dim, length), axis, 0, 0, tiled=True)
    return jnp.sum(tiles.astype(jnp.float32), axis=0)


def all_blocks(value, axes, sequence):
    tiles = value[None]
    for k in sequence:
        tiles = lax.all_gather(tiles, axes[k], axis=0, tiled=True)
    carried = [lax.axis_size(axes[k]) for k in reversed(sequence)]
    tiles = tiles.reshape(*carried, *value.shape)
    turned = sorted(range(len(sequence)), key=lambda place: sequence[len(sequence) - 1 - place])
    return tiles.transpose(*turned, *range(len(sequence), tiles.ndim)).reshape(-1, *value.shape)


def gather_axes(value, axes, sequence, dim):
    return in_order(all_blocks(value, axes, sequence), dim)


def scaled_rows(values, gain):
    values = values.astype(jnp.float32)
    mean_square = jnp.mean(values * values, axis=1, keepdims=True)
    return (values * lax.rsqrt(mean_square + 1e-06) * gain).astype(jnp.bfloat16)


def product(left, right):
    return jnp.dot(left, right, preferred_element_type=jnp.float32)


def window_attention(queries, context_keys, context_values, reach, position):
    rows = queries.shape[0]
    local_kv = context_keys.shape[1] // HEAD_DIM
    group = queries.shape[1] // (local_kv * HEAD_DIM)
    block = min(512, rows)
    span = WINDOW + block
    scale = HEAD_DIM ** (-0.5)
    start = reach * rows - WINDOW
    query_block = queries.reshape(block, local_kv, group, HEAD_DIM)
    key_block = context_keys.reshape(span, local_kv, HEAD_DIM)
    value_block = context_values.reshape(span, local_kv, HEAD_DIM)
    scores = (
        jnp.einsum("qkgd,ckd->kgqc", query_block, key_block, preferred_element_type=jnp.float32)
        * scale
    )
    query_pos = lax.broadcasted_iota(jnp.int32, (block, span), 0)
    key_pos = lax.broadcasted_iota(jnp.int32, (block, span), 1)
    distance = query_pos + WINDOW - key_pos
    first_key = (position - reach) * rows + start
    allowed = (distance >= 0) & (distance < WINDOW) & (key_pos + first_key >= 0)
    scores = jnp.where(allowed[None, None], scores, -1e30)
    highest = jnp.max(scores, axis=3, keepdims=True)
    raised = jnp.exp(scores - highest)
    weights = (raised / jnp.sum(raised, axis=3, keepdims=True)).astype(jnp.bfloat16)
    mixed = jnp.einsum("kgqc,ckd->qkgd", weights, value_block, preferred_element_type=jnp.float32)
    outputs = mixed.astype(jnp.bfloat16).reshape(block, local_kv * group * HEAD_DIM)
    return outputs


def per_device(tokens, attn_gain, w_query, w_key, w_value, w_out, mlp_gain, w_gate, w_up, w_down):
    rows = tokens.shape[0]
    whole = gathered_copies(tokens, "tensor", 1)
    normed = scaled_rows(whole, attn_gain)
    query_full, key_full, value_full = sent_together((w_query, w_key, w_value), SEQ, 0, 1)
    queries = product(normed, query_full).astype(jnp.bfloat16)
    keys = product(normed, key_full).astype(jnp.bfloat16)
    values = product(normed, value_full).astype(jnp.bfloat16)
    reach = -(-WINDOW // rows)
    earlier = []
    current = (keys, values)
    for step in range(reach):
        current = passed_along((current[0], current[1]), SEQ, 1)
        earlier.append(current)
    context_keys = jnp.concatenate(
        [earlier[reach - 1 - step][0] for step in range(reach)] + [keys], axis=0
    )
    context_values = jnp.concatenate(
        [earlier[reach - 1 - step][1] for step in range(reach)] + [values], axis=0
    )
    position = lax.axis_index(SEQ)
    attended = window_attention(queries, context_keys, context_values, reach, position)
    out_full = gathered_copies(w_out, SEQ, 1)
    head_terms = product(attended, out_full)
    attn_share = sent_and_summed(head_terms.astype(jnp.bfloat16), "tensor", 1)
    stream_share = (tokens.astype(jnp.float32) + attn_share).astype(jnp.bfloat16)
    stream_whole = gathered_copies(stream_share, "tensor", 1)
    stream_normed = scaled_rows(stream_whole, mlp_gain)
    gate_full, up_full = sent_together((w_gate, w_up), SEQ, 0, 1)
    gate = product(stream_normed, gate_full)
    upward = product(stream_normed, up_full)
    hidden = (jax.nn.silu(gate) * upward).astype(jnp.bfloat16)
    down_full = gather_axes(w_down, SEQ, (0, 1, 2), 1)
    unit_terms = product(hidden, down_full)
    mlp_share = sent_and_summed(unit_terms.astype(jnp.bfloat16), "tensor", 1)
    return (stream_share.astype(jnp.float32) + mlp_share).astype(jnp.bfloat16)


def solution(mesh):
    split = Mesh(
        mesh.devices.reshape(2, 4, 8, mesh.shape["tensor"]), ("seq_0", "seq_1", "seq_2", "tensor")
    )
    placed = (
        P(SEQ, "tensor"),
        P(),
        P(SEQ, "tensor"),
        P(SEQ, "tensor"),
        P(SEQ, "tensor"),
        P("tensor", SEQ),
        P(),
        P(SEQ, "tensor"),
        P(SEQ, "tensor"),
        P("tensor", SEQ),
    )
    return jax.shard_map(
        per_device, mesh=split, in_specs=placed, out_specs=P(SEQ, "tensor"), check_vma=False
    )
```

profile of v0, /device:TPU:1, one launch (start us, length us, event | category | flops | bytes accessed | tf_op | source)
XLA Modules:
  0.0 769.3 jit_solution(572772055486221659)
XLA Ops:
  6.5 1.5 pad_maximum_fusion.1
  8.0 0.0 all-gather.5.cloned.1.call-update
  8.0 0.0 all-gather.9.cloned.1.call-start
  8.1 5.0 all-gather
  13.1 13.0 %all_gather.18 = bf16[8,1408,32]{1,2,0:T(8,128)(2,1)} all-gather(bf16[2,1408,32]{1,2,0:T(8,128)(2,1)S(1)} %bitcast.99), channel_id=1, replica_groups=mesh['seq_0'=2,'seq_1'=4,'seq_2'=8,'tensor'=4] {'seq_1'}, dimensions={0}, use_global_device_ids=true | all-gather | bytes 901120 | tf_op jit(solution)/shard_map/all_gather | solution.py:60
  26.0 0.0 all-gather.9.cloned.1.call-update
  26.1 0.0 all-gather.7.cloned.1.call-start
  26.1 1.6 pad_maximum_fusion
  27.7 0.0 all-gather.7.cloned.1.call-update
  27.8 0.2 copy.42
  28.0 1.5 broadcast_in_dim.20
  29.5 9.4 %all-to-all-start = ((bf16[4,512,512]{1,2,0:T(8,128)(2,1)}), bf16[4,512,512]{1,2,0:T(8,128)(2,1)S(1)}, u32[]{:S(2)}, u32[]{:S(2)}) async-start(bf16[4,512,512]{1,2,0:T(8,128)(2,1)} %broadcast_in_dim.20), calls=%async_computation | async-start | bytes 4194304 | tf_op jit(solution)/shard_map/all_to_all | solution.py:14
  38.9 1.3 fusion.18
  40.2 28.7 %all-to-all-done = bf16[4,512,512]{1,2,0:T(8,128)(2,1)S(1)} async-done(((bf16[4,512,512]{1,2,0:T(8,128)(2,1)}), bf16[4,512,512]{1,2,0:T(8,128)(2,1)S(1)}, u32[]{:S(2)}, u32[]{:S(2)}) %all-to-all-start) | async-done | bytes 2097184 | tf_op jit(solution)/shard_map/all_to_all | solution.py:14
  69.0 1.6 broadcast_in_dim.23
  70.5 9.6 %all-to-all-start.1 = ((bf16[64,512,32]{1,2,0:T(8,128)(2,1)}), bf16[64,512,32]{1,2,0:T(8,128)(2,1)}, u32[]{:S(2)}, u32[]{:S(2)}) async-start(bf16[64,512,32]{1,2,0:T(8,128)(2,1)} %broadcast_in_dim.23), calls=%async_computation.1 | async-start | bytes 4194304 | tf_op jit(solution)/shard_map/all_to_all | solution.py:14
  80.1 0.5 multiply_reduce_fusion.1
  80.6 1.9 fusion.11
  82.6 194.5 %all-gather.5.cloned.1.call-done = bf16[2048,768]{1,0:T(8,128)(2,1)} async-done(((bf16[32,768]{1,0:T(8,128)(2,1)}), bf16[2048,768]{1,0:T(8,128)(2,1)}) %all-gather.5.cloned.1.call-update) | async-done | bytes 3145744 | tf_op jit(solution)/shard_map/all_gather | solution.py:36
  277.0 2.6 convolution_convert_fusion.2
  279.6 1.3 collective-permute-start.2
  280.9 2.4 convolution_convert_fusion.3
  283.4 1.8 collective-permute-start
  285.2 1.9 collective-permute-start.3
  287.2 1.3 fusion.24
  288.5 3.1 collective-permute-start.1
  291.6 2.4 fusion.1
  294.0 2.8 fusion
  296.8 4.1 fusion.27
  300.8 2.9 convolution_convert_fusion
  303.7 0.2 copy.62
  303.9 79.6 %all_to_all.25 = bf16[4,512,512]{2,1,0:T(8,128)(2,1)S(1)} all-to-all(bf16[4,512,512]{2,1,0:T(8,128)(2,1)S(1)} %bitcast.93), channel_id=1, replica_groups=mesh['seq_0'=2,'seq_1'=4,'seq_2'=8,'tensor'=4] {'tensor'}, dimensions={0} | all-to-all | bytes 4194304 | tf_op jit(solution)/shard_map/all_to_all | solution.py:53
  383.5 0.3 convert_reduce_fusion.1
  383.8 0.2 add_convert_fusion.1
  384.0 0.2 copy.47
  384.2 0.2 broadcast_in_dim.24
  384.4 34.1 %all_to_all.26 = bf16[4,512,512]{1,2,0:T(8,128)(2,1)S(1)} all-to-all(bf16[4,512,512]{1,2,0:T(8,128)(2,1)S(1)} %broadcast_in_dim.24), channel_id=1, replica_groups=mesh['seq_0'=2,'seq_1'=4,'seq_2'=8,'tensor'=4] {'tensor'}, dimensions={0} | all-to-all | bytes 4194304 | tf_op jit(solution)/shard_map/all_to_all | solution.py:14
  418.5 0.5 multiply_reduce_fusion
  419.0 0.5 fusion.9
  419.6 0.0 all-gather.9.cloned.1.call-done
  419.6 6.5 copy.49
  426.1 241.3 %all-gather.7.cloned.1.call-done = bf16[2048,2816]{1,0:T(8,128)(2,1)} async-done(((bf16[32,2816]{1,0:T(8,128)(2,1)}), bf16[2048,2816]{1,0:T(8,128)(2,1)}) %all-gather.7.cloned.1.call-update) | async-done | bytes 11534352 | tf_op jit(solution)/shard_map/all_gather | solution.py:36
  667.5 7.7 %fusion.6 = f32[512,1408]{1,0:T(8,128)} fusion(bf16[512,2048]{0,1:T(8,128)(2,1)S(1)} %fusion.9, bf16[2048,2816]{1,0:T(8,128)(2,1)} %all-gather.7.cloned.1.call-done), kind=kOutput, calls=%fused_computation.9 | convolution fusion | flops 2952790016 | bytes 10747904 | tf_op jit(solution)/shard_map/dot_general | solution.py:78
  675.2 12.8 %convolution_convert_fusion.1 = bf16[512,2048]{1,0:T(8,128)(2,1)S(1)} fusion(bf16[1408,2048]{0,1:T(8,128)(2,1)} %bitcast.96, bf16[512,2048]{0,1:T(8,128)(2,1)} %copy-done.1, bf16[2048,2816]{1,0:T(8,128)(2,1)} %all-gather.7.cloned.1.call-done, f32[512,1408]{1,0:T(8,128)} %fusion.6), kind=kOutput, calls=%fused_computation.29 | convolution fusion | flops 5910953984 | bytes 18612224 | tf_op jit(solution)/shard_map/dot_general | solution.py:78
  688.0 0.2 copy.61
  688.2 73.2 %all_to_all.27 = bf16[4,512,512]{2,1,0:T(8,128)(2,1)S(1)} all-to-all(bf16[4,512,512]{2,1,0:T(8,128)(2,1)S(1)} %bitcast.94), channel_id=1, replica_groups=mesh['seq_0'=2,'seq_1'=4,'seq_2'=8,'tensor'=4] {'tensor'}, dimensions={0} | all-to-all | bytes 4194304 | tf_op jit(solution)/shard_map/all_to_all | solution.py:53
  761.4 0.3 convert_reduce_fusion
  761.8 1.0 add_convert_fusion
  (25 shorter events, 0.1 us)
Async XLA Ops:
  6.5 21.2 %copy-start.2 = (bf16[512,512]{1,0:T(8,128)(2,1)S(1)}, bf16[512,512]{1,0:T(8,128)(2,1)}, u32[]{:S(2)}) copy-start(bf16[512,512]{1,0:T(8,128)(2,1)} %param.10) | copy-start | bytes 1572868
  6.5 270.5 %all-gather.5.cloned.1.call-start = ((), (), s32[]{:S(2)}) async-start(), calls=%async_computation.5 | async-start | bytes 3194880 | tf_op jit(solution)/shard_map/all_gather | solution.py:36
  8.0 411.6 %all-gather.9.cloned.1.call-start = ((), (), s32[]{:S(2)}) async-start(), calls=%async_computation.7 | async-start | bytes 6488064 | tf_op jit(solution)/shard_map/all_gather | solution.py:60
  26.1 641.4 %all-gather.7.cloned.1.call-start = ((), (), s32[]{:S(2)}) async-start(), calls=%async_computation.6 | async-start | bytes 11714560 | tf_op jit(solution)/shard_map/all_gather | solution.py:36
  29.5 39.5 %copy-start.3 = (bf16[512,32]{0,1:T(8,128)(2,1)S(1)}, bf16[512,32]{0,1:T(8,128)(2,1)}, u32[]{:S(2)}) copy-start(bf16[512,32]{0,1:T(8,128)(2,1)} %param.15) | copy-start | bytes 98308
  29.5 39.5 %all-to-all-start = ((bf16[4,512,512]{1,2,0:T(8,128)(2,1)}), bf16[4,512,512]{1,2,0:T(8,128)(2,1)S(1)}, u32[]{:S(2)}, u32[]{:S(2)}) async-start(bf16[4,512,512]{1,2,0:T(8,128)(2,1)} %broadcast_in_dim.20), calls=%async_computation | async-start | bytes 4194304 | tf_op jit(solution)/shard_map/all_to_all | solution.py:14
  70.5 10.1 %copy-start.4 = (f32[2048]{0:T(1024)S(1)}, f32[2048]{0:T(1024)}, u32[]{:S(2)}) copy-start(f32[2048]{0:T(1024)} %param.11) | copy-start | bytes 24580
  70.5 230.3 %all-to-all-start.1 = ((bf16[64,512,32]{1,2,0:T(8,128)(2,1)}), bf16[64,512,32]{1,2,0:T(8,128)(2,1)}, u32[]{:S(2)}, u32[]{:S(2)}) async-start(bf16[64,512,32]{1,2,0:T(8,128)(2,1)} %broadcast_in_dim.23), calls=%async_computation.1 | async-start | bytes 4194304 | tf_op jit(solution)/shard_map/all_to_all | solution.py:14
  82.6 204.6 %copy-start = (bf16[512,2048]{0,1:T(8,128)(2,1)S(1)}, bf16[512,2048]{0,1:T(8,128)(2,1)}, u32[]{:S(2)}) copy-start(bf16[512,2048]{0,1:T(8,128)(2,1)} %fusion.11) | copy-start | bytes 6291460
  277.0 10.1 %copy-start.6 = (bf16[2048,768]{1,0:T(8,128)(2,1)S(1)}, bf16[2048,768]{1,0:T(8,128)(2,1)}, u32[]{:S(2)}) copy-start(bf16[2048,768]{1,0:T(8,128)(2,1)} %all-gather.5.cloned.1.call-done) | copy-start | bytes 9437188
  279.6 5.6 collective-permute-start.2
  283.4 5.1 collective-permute-start
  285.2 6.4 collective-permute-start.3
  288.5 8.3 %collective-permute-start.1 = (bf16[512,128]{1,0:T(8,128)(2,1)S(1)}, bf16[512,128]{1,0:T(8,128)(2,1)S(1)}, u32[]{:S(2)}, u32[]{:S(2)}) collective-permute-start(bf16[512,128]{1,0:T(8,128)(2,1)S(1)} %collective-permute-done), channel_id=1, source_target_pairs={{0,4},{4,8},{8,12},{12,16},{16,20},{20,24},{24,28},{28,32},{32,36}... | collective-permute-start | bytes 393224 | tf_op jit(solution)/shard_map/ppermute | solution.py:42
  384.4 34.6 %copy-start.5 = (f32[2048]{0:T(1024)S(1)}, f32[2048]{0:T(1024)}, u32[]{:S(2)}) copy-start(f32[2048]{0:T(1024)} %param.16) | copy-start | bytes 24580
  419.6 247.9 %copy-start.1 = (bf16[512,2048]{0,1:T(8,128)(2,1)}, bf16[512,2048]{0,1:T(8,128)(2,1)S(1)}, u32[]{:S(2)}) copy-start(bf16[512,2048]{0,1:T(8,128)(2,1)S(1)} %fusion.9) | copy-start | bytes 6291460
Sparse Core Ops, SparseCore 0:
  9.1 267.8 all-gather.4
  278.8 110.4 all-gather.8
  391.1 276.3 all-gather.6
where the time goes:
time: 770 us; the launch traced here: 769 us
  waiting for transfers between devices  465 us (60%)
  blocking collectives  205 us (27%)
  matrix products  36.2 us (5%)
  starting transfers between devices  27.3 us (4%)
  between operations  13.4 us (2%)
  other arithmetic  12.4 us (2%)
  local copies, waits for them, and re-layouts  10.6 us (1%)
    all_gather x2, waiting for transfers between devices, sent_together(): lax.all_gather(both, axis, axis=dim, tiled=True)  436 us
    all_to_all x2, blocking collectives, sent_and_summed(): lax.all_to_all(in_blocks(value, dim, length), axis, 0, 0, tiled=True)  153 us
    all_to_all x1, blocking collectives, copy_for_each(): lax.all_to_all(jnp.broadcast_to(value[None], (length, *value.shape)), axi...  34.1 us
    dot_general x6, matrix products, product(): return jnp.dot(left, right, preferred_element_type=jnp.float32)  29.8 us
    all_to_all x2, waiting for transfers between devices, copy_for_each(): lax.all_to_all(jnp.broadcast_to(value[None], (length, *value.shape)), axi...  28.7 us
    all_to_all x2, starting transfers between devices, copy_for_each(): lax.all_to_all(jnp.broadcast_to(value[None], (length, *value.shape)), axi...  19 us
    all_gather x2, blocking collectives, all_blocks(): tiles = lax.all_gather(tiles, axes[k], axis=0, tiled=True)  17.9 us
  transfers between devices with their start and end apart: 9, of which 3 were waited for; matrix products, arithmetic and copies ran while one was open for 5% of the time, Pallas kernels for 0%

commit v1 on v0

v1 whole, which is shorter than its diff:
```python
import jax
import jax.numpy as jnp
from jax import lax
from jax.sharding import Mesh
from jax.sharding import PartitionSpec as P

HEAD_DIM = 128
WINDOW = 1024
SEQ = ("yl", "x", "z")
FEATURES = ("yh", "c")
PLANE = ("x", "z")


def spread(value, axis):
    length = lax.axis_size(axis)
    return lax.all_to_all(
        jnp.broadcast_to(value[None], (length, *value.shape)), axis, 0, 0, tiled=True
    )


def plane_rows(value):
    tiles = spread(value, "z")
    tiles = tiles.reshape(-1, value.shape[1])
    return spread(tiles, "x").reshape(-1, value.shape[1])


def other_core(value):
    return lax.ppermute(value, "c", [(0, 1), (1, 0)])


def column_partner(value, flip):
    return lax.ppermute(value, ("yl", "yh"), [(i, i ^ flip) for i in range(4)])


def ordered(flag, first, second):
    return jnp.where(flag == 0, first, second), jnp.where(flag == 0, second, first)


def shuffled_rows(parts):
    count = lax.axis_size("yl") * lax.axis_size("x") * lax.axis_size("z")
    core = lax.axis_index("c")
    parity = lax.axis_index("z") % 2
    received = []
    for swap, send in enumerate(ordered(parity, parts[0], parts[1])):
        route = []
        for block in range(count):
            for head in range(2):
                to_core = block % 2 if swap == 0 else 1 - block % 2
                target = (head * (count // 2) + block // 2) * 2 + to_core
                route.append((block * 2 + head, target))
        received.append(lax.ppermute(send, ("yl", "x", "z", "c"), route))
    return jnp.concatenate(ordered(core, received[0], received[1]), axis=0)


def column_tokens(share):
    yh, core = lax.axis_index("yh"), lax.axis_index("c")
    blocks = [share] + [column_partner(share, flip) for flip in (1, 2, 3)]
    mine = jnp.stack(blocks)
    theirs = other_core(mine)
    runs = []
    for run in range(2):
        pairs = []
        for half in range(2):
            pairs.append(ordered(core, mine[run * 2 + half], theirs[run * 2 + half]))
        features = []
        for core_at in range(2):
            features.append(ordered(yh, pairs[0][core_at], pairs[1][core_at]))
        runs.append(
            jnp.concatenate(
                [features[0][0], features[1][0], features[0][1], features[1][1]], axis=1
            )
        )
    return jnp.concatenate(runs, axis=0)


def scaled_rows(values, gain):
    values = values.astype(jnp.float32)
    mean_square = jnp.mean(values * values, axis=1, keepdims=True)
    return (values * lax.rsqrt(mean_square + 1e-06) * gain).astype(jnp.bfloat16)


def product(left, right):
    return jnp.dot(left, right, preferred_element_type=jnp.float32)


def product_t(left, right):
    return lax.dot_general(
        left, right, (((1,), (1,)), ((), ())), preferred_element_type=jnp.float32
    )


def column_sum(left, blocks):
    rows = left.shape[0] // 2
    mine = lax.axis_index("yh") * 2 + lax.axis_index("c")

    def term(flip):
        block = lax.dynamic_index_in_dim(blocks, mine ^ flip, 0, keepdims=False)
        return product_t(left, block)

    away = jnp.stack([term(1), term(3)]).astype(jnp.bfloat16)
    came = other_core(away).astype(jnp.float32)
    near = term(0) + came[0]
    far = term(2) + came[1]
    total = near[:rows]
    sent = (
        (far[:rows], 1),
        (near[rows:], 2),
        (far[rows:], 3),
    )
    for value, flip in sent:
        total = total + column_partner(value.astype(jnp.bfloat16), flip).astype(jnp.float32)
    return total


def window_attention(queries, keys, values, first_key):
    rows = queries.shape[1]
    span = keys.shape[1]
    scale = HEAD_DIM ** (-0.5)
    scores = jnp.einsum("rqhd,rcd->rhqc", queries, keys, preferred_element_type=jnp.float32) * scale
    query_pos = lax.broadcasted_iota(jnp.int32, (rows, span), 0)
    key_pos = lax.broadcasted_iota(jnp.int32, (rows, span), 1)
    distance = query_pos + WINDOW - key_pos
    inside = (distance >= 0) & (distance < WINDOW)
    allowed = inside[None] & (key_pos[None] + first_key[:, None, None] >= 0)
    scores = jnp.where(allowed[:, None], scores, -1e30)
    highest = jnp.max(scores, axis=3, keepdims=True)
    raised = jnp.exp(scores - highest)
    weights = (raised / jnp.sum(raised, axis=3, keepdims=True)).astype(jnp.bfloat16)
    mixed = jnp.einsum("rhqc,rcd->rqhd", weights, values, preferred_element_type=jnp.float32)
    return mixed.astype(jnp.bfloat16)


def per_device(tokens, attn_gain, w_query, w_key, w_value, w_out, mlp_gain, w_gate, w_up, w_down):
    rows = tokens.shape[0]
    yl, core = lax.axis_index("yl"), lax.axis_index("c")
    place = lax.axis_index(PLANE)
    plane = lax.axis_size("x") * lax.axis_size("z")
    out_t, down_t = w_out.T, w_down.T
    heads = w_query.shape[1] // 2
    units = w_gate.shape[1] // 2
    padded = -(-units // 128) * 128

    def half(array, h, width):
        return array[:, h * width : (h + 1) * width]

    def wide(array, h):
        return jnp.pad(half(array, h, units), ((0, 0), (0, padded - units)))

    attn_parts = [
        jnp.concatenate(
            [(w_key, w_value)[h], half(w_query, h, heads), half(out_t, h, heads)], axis=1
        )
        for h in range(2)
    ]
    mlp_parts = [
        jnp.concatenate([wide(w_gate, h), wide(w_up, h), wide(down_t, h)], axis=1)
        for h in range(2)
    ]
    attn_rows = shuffled_rows(attn_parts)
    mlp_rows = shuffled_rows(mlp_parts)
    mlp_full = lax.all_gather(mlp_rows, PLANE, axis=0, tiled=True)

    normed = scaled_rows(column_tokens(tokens), attn_gain)
    kv_width = w_key.shape[1]
    kv_full = plane_rows(attn_rows[:, :kv_width])
    fresh = product(normed, kv_full).astype(jnp.bfloat16).reshape(2, rows, kv_width)
    reach = -(-WINDOW // rows)
    context = [fresh]
    for step in range(1, reach + 1):
        came = lax.ppermute(fresh, PLANE, [(i, (i + step) % plane) for i in range(plane)])
        context.insert(0, jnp.where(place < step, came[::-1], came))
    context = jnp.concatenate(context, axis=1)
    keys, values = ordered(core, context, other_core(context))

    rest_z = spread(attn_rows[:, kv_width:], "z")
    rest_z = rest_z.reshape(-1, rest_z.shape[2])
    query_full = spread(rest_z[:, :heads], "x").reshape(-1, heads)
    out_full = spread(rest_z[:, heads:], "x")
    queries = product(normed, query_full).astype(jnp.bfloat16)
    queries = queries.reshape(2, rows, heads // HEAD_DIM, HEAD_DIM)
    runs = jnp.stack([yl, 1 - yl])
    first_key = (runs * plane + place - reach) * rows
    attended = window_attention(queries, keys, values, first_key).reshape(2 * rows, heads)
    attn_share = column_sum(attended, out_full.reshape(4, -1, heads))
    stream_share = (tokens.astype(jnp.float32) + attn_share).astype(jnp.bfloat16)

    stream_normed = scaled_rows(column_tokens(stream_share), mlp_gain)
    gate = product(stream_normed, mlp_full[:, :padded])
    upward = product(stream_normed, mlp_full[:, padded : 2 * padded])
    hidden = (jax.nn.silu(gate) * upward).astype(jnp.bfloat16)
    down_full = mlp_full[:, 2 * padded :]
    mlp_share = column_sum(hidden, down_full.reshape(4, -1, padded))
    return (stream_share.astype(jnp.float32) + mlp_share).astype(jnp.bfloat16)


def solution(mesh):
    split = Mesh(mesh.devices.reshape(2, 4, 8, 2, 2), ("yl", "x", "z", "yh", "c"))
    both = P(SEQ, FEATURES)
    down = P(FEATURES, SEQ)
    placed = (both, P(), both, both, both, down, P(), both, both, down)
    return jax.shard_map(
        per_device, mesh=split, in_specs=placed, out_specs=both, check_vma=False
    )
```

time: 770 us -> 347 us (0.45)
  waiting for transfers between devices: 465 us -> 145 us
  blocking collectives: 205 us -> 0 us
  starting transfers between devices: 27.3 us -> 78.9 us
  other arithmetic: 12.4 us -> 43.6 us
    all_gather x3 -> x1, waiting for transfers between devices: 436 us -> 0.01 us  [per_device(): mlp_full = lax.all_gather(mlp_rows, PLANE, axis=0, tiled=True)]
    all_to_all x3 -> x0, blocking collectives: 187 us -> none  [the longest x2 153 us: sent_and_summed(): lax.all_to_all(in_blocks(value, dim, length), axis, 0, 0, tiled=True)]
    ppermute x4 -> x23, waiting for transfers between devices: 0.01 us -> 134 us  [the longest x12 94.3 us: column_partner(): return lax.ppermute(value, ('yl', 'yh'), [(i, i ^ flip) for i in range(4)])]
    ppermute x4 -> x23, starting transfers between devices: 8.18 us -> 45.8 us  [the longest x4 17.1 us: shuffled_rows(): received.append(lax.ppermute(send, ('yl', 'x', 'z', 'c'), route))]
    reduce_sum x2, other arithmetic: 1.02 us -> 25.5 us  [scaled_rows(): mean_square = jnp.mean(values * values, axis=1, keepdims=True)]
    all_gather x2 -> x0, blocking collectives: 17.9 us -> none  [all_blocks(): tiles = lax.all_gather(tiles, axes[k], axis=0, tiled=True)]
    all_to_all x2 -> x5, waiting for transfers between devices: 28.7 us -> 11.4 us  [spread(): lax.all_to_all(jnp.broadcast_to(value[None], (length, *value.shape)), axi...]
    all_to_all x2 -> x5, starting transfers between devices: 19 us -> 33.1 us  [spread(): lax.all_to_all(jnp.broadcast_to(value[None], (length, *value.shape)), axi...]
  transfers between devices with their start and end apart: 9 -> 29, of which waited for: 3 -> 20; matrix products, arithmetic and copies ran while one was open for 5% -> 22% of each run, Pallas kernels for 0% -> 0%
where the time goes in v1:
time: 347 us; the launch traced here: 340 us
  waiting for transfers between devices  145 us (42%)
  starting transfers between devices  78.9 us (23%)
  other arithmetic  43.6 us (13%)
  matrix products  41.8 us (12%)
  local copies, waits for them, and re-layouts  16.3 us (5%)
  between operations  14.1 us (4%)
    ppermute x12, waiting for transfers between devices, column_partner(): return lax.ppermute(value, ('yl', 'yh'), [(i, i ^ flip) for i in range(4)])  94.3 us
    all_to_all x5, starting transfers between devices, spread(): lax.all_to_all(jnp.broadcast_to(value[None], (length, *value.shape)), axi...  33.1 us
    ppermute x2, waiting for transfers between devices, per_device(): lax.ppermute(fresh, PLANE, [(i, (i + step) % plane) for i in range(plane)])  26.8 us
    reduce_sum x2, other arithmetic, scaled_rows(): mean_square = jnp.mean(values * values, axis=1, keepdims=True)  25.5 us
    dot_general x4, matrix products, product(): return jnp.dot(left, right, preferred_element_type=jnp.float32)  20.5 us
    ppermute x4, starting transfers between devices, shuffled_rows(): received.append(lax.ppermute(send, ('yl', 'x', 'z', 'c'), route))  17.1 us
    ppermute x5, starting transfers between devices, other_core(): return lax.ppermute(value, 'c', [(0, 1), (1, 0)])  12.6 us
    ppermute x12, starting transfers between devices, column_partner(): return lax.ppermute(value, ('yl', 'yh'), [(i, i ^ flip) for i in range(4)])  12.5 us
  transfers between devices with their start and end apart: 29, of which 20 were waited for; matrix products, arithmetic and copies ran while one was open for 22% of the time, Pallas kernels for 0%

profile of v1, /device:TPU:1, one launch (start us, length us, event | category | flops | bytes accessed | tf_op | source)
XLA Modules:
  0.0 340.1 jit_solution(1689954081590783463)
XLA Ops:
  10.2 4.6 %collective-permute-start.17 = (bf16[32,2304]{1,0:T(8,128)(2,1)S(1)}, bf16[32,2304]{1,0:T(8,128)(2,1)S(1)}, u32[]{:S(2)}, u32[]{:S(2)}) collective-permute-start(bf16[32,2304]{1,0:T(8,128)(2,1)S(1)} %get-tuple-element.33), channel_id=1, source_target_pairs={{0,0},{1,128},{4,1},{5,129},{8,4},{9,132},{12,5},{13,133},{16,8},{... | collective-permute-start | bytes 442376 | tf_op jit(solution)/shard_map/ppermute | solution.py:51
  14.8 2.8 collective-permute-start.18
  18.9 2.7 collective-permute-start
  22.3 15.4 %collective-permute-done = bf16[512,512]{0,1:T(8,128)(2,1)S(1)} collective-permute-done((bf16[512,512]{0,1:T(8,128)(2,1)S(1)}, bf16[512,512]{0,1:T(8,128)(2,1)S(1)}, u32[]{:S(2)}, u32[]{:S(2)}) %collective-permute-start) | collective-permute-done | bytes 524320 | tf_op jit(solution)/shard_map/ppermute | solution.py:32
  37.7 6.9 %collective-permute-done.1 = bf16[512,512]{0,1:T(8,128)(2,1)S(1)} collective-permute-done((bf16[512,512]{0,1:T(8,128)(2,1)S(1)}, bf16[512,512]{0,1:T(8,128)(2,1)S(1)}, u32[]{:S(2)}, u32[]{:S(2)}) %collective-permute-start.1) | collective-permute-done | bytes 524320 | tf_op jit(solution)/shard_map/ppermute | solution.py:32
  44.6 1.9 collective-permute-done.2
  47.2 1.6 pad_maximum_fusion
  50.6 1.9 collective-permute-start.4
  52.6 7.8 %collective-permute-start.5 = (bf16[32,640]{1,0:T(8,128)(2,1)S(1)}, bf16[32,640]{1,0:T(8,128)(2,1)S(1)}, u32[]{:S(2)}, u32[]{:S(2)}) collective-permute-start(bf16[32,640]{1,0:T(8,128)(2,1)S(1)} %get-tuple-element.38), channel_id=1, source_target_pairs={{0,1},{1,129},{4,0},{5,128},{8,5},{9,133},{12,4},{13,132},{16,9},{... | collective-permute-start | bytes 122888 | tf_op jit(solution)/shard_map/ppermute | solution.py:51
  62.2 10.7 %all-to-all-start = ((bf16[8,64,128]{2,1,0:T(8,128)(2,1)}), bf16[8,64,128]{2,1,0:T(8,128)(2,1)S(1)}, u32[]{:S(2)}, u32[]{:S(2)}) async-start(bf16[8,64,128]{2,1,0:T(8,128)(2,1)} %broadcast_in_dim.20), calls=%async_computation | async-start | bytes 262144 | tf_op jit(solution)/shard_map/all_to_all | solution.py:16
  75.2 6.4 %all-to-all-done = bf16[8,64,128]{2,1,0:T(8,128)(2,1)S(1)} async-done(((bf16[8,64,128]{2,1,0:T(8,128)(2,1)}), bf16[8,64,128]{2,1,0:T(8,128)(2,1)S(1)}, u32[]{:S(2)}, u32[]{:S(2)}) %all-to-all-start) | async-done | bytes 131104 | tf_op jit(solution)/shard_map/all_to_all | solution.py:16
  82.5 10.5 %all-to-all-start.1 = ((bf16[4,512,128]{2,1,0:T(8,128)(2,1)}), bf16[4,512,128]{2,1,0:T(8,128)(2,1)}, u32[]{:S(2)}, u32[]{:S(2)}) async-start(bf16[4,512,128]{2,1,0:T(8,128)(2,1)} %broadcast_in_dim.22), calls=%async_computation.1 | async-start | bytes 1048576 | tf_op jit(solution)/shard_map/all_to_all | solution.py:16
  93.0 2.9 broadcast_select_fusion.28
  95.9 1.6 broadcast_select_fusion.32
  97.6 2.4 all-to-all-done.1
  100.8 3.7 %all-to-all-start.2 = ((bf16[8,64,512]{2,1,0:T(8,128)(2,1)}), bf16[8,64,512]{2,1,0:T(8,128)(2,1)S(1)}, u32[]{:S(2)}, u32[]{:S(2)}) async-start(bf16[8,64,512]{2,1,0:T(8,128)(2,1)} %broadcast_in_dim.24), calls=%async_computation.2 | async-start | bytes 1048576 | tf_op jit(solution)/shard_map/all_to_all | solution.py:16
  104.5 7.9 %fusion.2 = (f32[1024]{0:T(1024)S(1)}, bf16[1024,2048]{0,1:T(8,128)(2,1)S(1)}) fusion(bf16[512,512]{0,1:T(8,128)(2,1)} %get-tuple-element.24, bf16[512,512]{0,1:T(8,128)(2,1)} %get-tuple-element.23, bf16[512,512]{0,1:T(8,128)(2,1)} %get-tuple-element.22, bf16[512,512]{0,1:T(8,128)(2,1)} %get-tuple-element.21, bf16[512,512]{0,1:T(8,128)(2,1)} %get-tuple-element.20, ...), kind=kLoop, calls=%fused_computation.9 | loop fusion | flops 39844864 | bytes 8392704 | tf_op jit(solution)/shard_map/reduce_sum | solution.py:78
  112.5 3.4 fusion.41
  116.1 2.4 collective-permute-start.6
  121.0 4.2 %all-to-all-start.3 = ((bf16[4,512,256]{2,1,0:T(8,128)(2,1)}), bf16[4,512,256]{2,1,0:T(8,128)(2,1)}, u32[]{:S(2)}, u32[]{:S(2)}) async-start(bf16[4,512,256]{2,1,0:T(8,128)(2,1)} %broadcast_in_dim.25), calls=%async_computation.3 | async-start | bytes 2097152 | tf_op jit(solution)/shard_map/all_to_all | solution.py:16
  125.2 14.6 %collective-permute-done.6 = bf16[2,512,128]{1,2,0:T(8,128)(2,1)S(1)} collective-permute-done((bf16[2,512,128]{1,2,0:T(8,128)(2,1)S(1)}, bf16[2,512,128]{1,2,0:T(8,128)(2,1)S(1)}, u32[]{:S(2)}, u32[]{:S(2)}) %collective-permute-start.6) | collective-permute-done | bytes 262176 | tf_op jit(solution)/shard_map/ppermute | solution.py:170
  139.8 12.3 %collective-permute-done.7 = bf16[2,512,128]{1,2,0:T(8,128)(2,1)S(1)} collective-permute-done((bf16[2,512,128]{1,2,0:T(8,128)(2,1)S(1)}, bf16[2,512,128]{1,2,0:T(8,128)(2,1)S(1)}, u32[]{:S(2)}, u32[]{:S(2)}) %collective-permute-start.7) | collective-permute-done | bytes 262176 | tf_op jit(solution)/shard_map/ppermute | solution.py:170
  153.1 2.8 collective-permute-start.8
  157.0 2.5 all-to-all-done.3
  160.5 3.9 %all-to-all-start.4 = ((bf16[4,512,256]{2,1,0:T(8,128)(2,1)}), bf16[4,512,256]{2,1,0:T(8,128)(2,1)S(1)}, u32[]{:S(2)}, u32[]{:S(2)}) async-start(bf16[4,512,256]{2,1,0:T(8,128)(2,1)} %broadcast_in_dim.27), calls=%async_computation.4 | async-start | bytes 2097152 | tf_op jit(solution)/shard_map/all_to_all | solution.py:16
  164.5 5.1 %convolution_convert_fusion.4 = bf16[1024,256]{1,0:T(8,128)(2,1)} fusion(bf16[2048,256]{1,0:T(8,128)(2,1)} %bitcast.18, bf16[1024,2048]{0,1:T(8,128)(2,1)} %copy-done, f32[2048]{0:T(1024)S(1)} %copy-done.17, f32[1024]{0:T(1024)S(1)} %add_rsqrt_fusion.1), kind=kOutput, calls=%fused_computation.56 | convolution fusion | flops 1082392576 | bytes 5779456 | tf_op jit(solution)/shard_map/dot_general | solution.py:83
  169.6 2.0 reshape.91
  171.6 9.4 %fusion.124 = (f32[2,2,512]{2,1,0:T(2,128)S(1)}, f32[2,2,512,1536]{2,3,1,0:T(8,128)}) fusion(pred[2,512,1536]{1,2,0:T(8,128)(4,1)S(1)} %fusion.10, bf16[2,512,2,128]{3,2,1,0:T(2,128)(2,1)} %reshape.91, bf16[2,1536,128]{1,2,0:T(8,128)(2,1)} %collective-permute-done.8, pred[]{:T(512)S(6)} %eq.9, bf16[2,512,128]{1,2,0:T(8,128)(2,1)} %copy-done.9, ...), kind=kOutput, calls=%fused_computation.200 | convolution fusion | flops 820643328 | bytes 16261121 | tf_op jit(solution)/shard_map/sub | solution.py:127
  181.0 5.9 %fusion.35 = bf16[2,512,2,128]{1,3,2,0:T(8,128)(2,1)S(1)} fusion(f32[2,2,512,1536]{2,3,1,0:T(8,128)} %get-tuple-element.47, f32[2,2,512]{2,1,0:T(2,128)S(1)} %get-tuple-element.46, bf16[2,1536,128]{1,2,0:T(8,128)(2,1)} %collective-permute-done.8, pred[]{:T(512)S(6)} %eq.9, bf16[2,512,128]{1,2,0:T(8,128)(2,1)} %copy-done.9, ...), kind=kOutput, calls=%fused_computation.57 | convolution fusion | flops 814612480 | bytes 14688257 | tf_op jit(solution)/shard_map/rhqc,rcd->rqhd/dot_general | solution.py:129
  188.3 1.5 pad_maximum_fusion.1
  189.9 7.8 %collective-permute-start.9 = (bf16[2,1024,512]{1,2,0:T(8,128)(2,1)}, bf16[2,1024,512]{1,2,0:T(8,128)(2,1)}, u32[]{:S(2)}, u32[]{:S(2)}) collective-permute-start(bf16[2,1024,512]{1,2,0:T(8,128)(2,1)} %pad_maximum_fusion.1), channel_id=1, source_target_pairs={{0,1},{1,0},{2,3},{3,2},{4,5},{5,4},{6,7},{7,6},{8,9},{9,8},{10,11... | collective-permute-start | bytes 6291464 | tf_op jit(solution)/shard_map/ppermute | solution.py:28
  197.7 4.1 %collective-permute-done.9 = bf16[2,1024,512]{1,2,0:T(8,128)(2,1)} collective-permute-done((bf16[2,1024,512]{1,2,0:T(8,128)(2,1)}, bf16[2,1024,512]{1,2,0:T(8,128)(2,1)}, u32[]{:S(2)}, u32[]{:S(2)}) %collective-permute-start.9) | collective-permute-done | bytes 2097184 | tf_op jit(solution)/shard_map/ppermute | solution.py:28
  201.8 2.0 convert_element_type.89
  205.7 2.1 collective-permute-start.11
  207.8 11.3 %collective-permute-done.10 = bf16[512,512]{0,1:T(8,128)(2,1)S(1)} collective-permute-done((bf16[512,512]{0,1:T(8,128)(2,1)S(1)}, bf16[512,512]{0,1:T(8,128)(2,1)S(1)}, u32[]{:S(2)}, u32[]{:S(2)}) %collective-permute-start.10) | collective-permute-done | bytes 524320 | tf_op jit(solution)/shard_map/ppermute | solution.py:32
  219.2 11.9 %collective-permute-done.12 = bf16[512,512]{0,1:T(8,128)(2,1)S(1)} collective-permute-done((bf16[512,512]{0,1:T(8,128)(2,1)S(1)}, bf16[512,512]{0,1:T(8,128)(2,1)S(1)}, u32[]{:S(2)}, u32[]{:S(2)}) %collective-permute-start.12) | collective-permute-done | bytes 524320 | tf_op jit(solution)/shard_map/ppermute | solution.py:32
  232.2 2.8 collective-permute-start.15
  235.0 11.1 %collective-permute-done.13 = bf16[512,512]{0,1:T(8,128)(2,1)S(1)} collective-permute-done((bf16[512,512]{0,1:T(8,128)(2,1)S(1)}, bf16[512,512]{0,1:T(8,128)(2,1)S(1)}, u32[]{:S(2)}, u32[]{:S(2)}) %collective-permute-start.13) | collective-permute-done | bytes 524320 | tf_op jit(solution)/shard_map/ppermute | solution.py:32
  246.1 8.2 %collective-permute-done.14 = bf16[512,512]{0,1:T(8,128)(2,1)S(1)} collective-permute-done((bf16[512,512]{0,1:T(8,128)(2,1)S(1)}, bf16[512,512]{0,1:T(8,128)(2,1)S(1)}, u32[]{:S(2)}, u32[]{:S(2)}) %collective-permute-start.14) | collective-permute-done | bytes 524320 | tf_op jit(solution)/shard_map/ppermute | solution.py:32
  254.3 3.9 %collective-permute-done.15 = bf16[512,512]{0,1:T(8,128)(2,1)S(1)} collective-permute-done((bf16[512,512]{0,1:T(8,128)(2,1)S(1)}, bf16[512,512]{0,1:T(8,128)(2,1)S(1)}, u32[]{:S(2)}, u32[]{:S(2)}) %collective-permute-start.15) | collective-permute-done | bytes 524320 | tf_op jit(solution)/shard_map/ppermute | solution.py:32
  259.0 3.8 %collective-permute-done.16 = bf16[4,512,512]{1,2,0:T(8,128)(2,1)S(1)} collective-permute-done((bf16[4,512,512]{1,2,0:T(8,128)(2,1)S(1)}, bf16[4,512,512]{1,2,0:T(8,128)(2,1)S(1)}, u32[]{:S(2)}, u32[]{:S(2)}) %collective-permute-start.16) | collective-permute-done | bytes 2097184 | tf_op jit(solution)/shard_map/ppermute | solution.py:28
  263.2 17.5 %fusion.5 = (f32[1024]{0:T(1024)S(1)}, bf16[1024,2048]{0,1:T(8,128)(2,1)}) fusion(bf16[512,512]{0,1:T(8,128)(2,1)S(1)} %get-tuple-element.16, bf16[512,512]{0,1:T(8,128)(2,1)S(1)} %get-tuple-element.15, bf16[512,512]{0,1:T(8,128)(2,1)S(1)} %get-tuple-element.14, bf16[512,512]{0,1:T(8,128)(2,1)S(1)} %get-tuple-element.13, ...), kind=kLoop, calls=%fused_computation.12 | loop fusion | flops 39844864 | bytes 8392704 | tf_op jit(solution)/shard_map/reduce_sum | solution.py:78
  280.8 2.2 slice.179
  283.9 5.9 %fusion.15 = f32[1024,768]{1,0:T(8,128)S(1)} fusion(bf16[2048,2304]{1,0:T(8,128)(2,1)} %all-gather.2.cloned.1.call-done, bf16[1024,2048]{0,1:T(8,128)(2,1)S(1)} %copy-done.1, f32[2048]{0:T(1024)S(1)} %copy-done.18, f32[1024]{0:T(1024)S(1)} %add_rsqrt_fusion), kind=kOutput, calls=%fused_computation.25 | convolution fusion | flops 3229614080 | bytes 10498048 | tf_op jit(solution)/shard_map/dot_general | solution.py:83
  289.8 6.1 %multiply_convert_fusion = bf16[1024,768]{1,0:T(8,128)(2,1)S(1)} fusion(f32[1024,768]{1,0:T(8,128)S(1)} %fusion.15, bf16[2048,2304]{1,0:T(8,128)(2,1)} %all-gather.2.cloned.1.call-done, bf16[1024,2048]{0,1:T(8,128)(2,1)S(1)} %copy-done.1, f32[2048]{0:T(1024)S(1)} %copy-done.18, f32[1024]{0:T(1024)S(1)} %add_rsqrt_fusion), kind=kOutput, calls=%fused_computation.27 | convolution fusion | flops 3234332672 | bytes 12070912 | tf_op jit(solution)/shard_map/dot_general | solution.py:83
  298.6 3.8 %collective-permute-done.19 = bf16[2,1024,512]{1,2,0:T(8,128)(2,1)S(1)} collective-permute-done((bf16[2,1024,512]{1,2,0:T(8,128)(2,1)S(1)}, bf16[2,1024,512]{1,2,0:T(8,128)(2,1)S(1)}, u32[]{:S(2)}, u32[]{:S(2)}) %collective-permute-start.19) | collective-permute-done | bytes 2097184 | tf_op jit(solution)/shard_map/ppermute | solution.py:28
  307.9 11.8 %collective-permute-done.20 = bf16[512,512]{0,1:T(8,128)(2,1)S(1)} collective-permute-done((bf16[512,512]{0,1:T(8,128)(2,1)S(1)}, bf16[512,512]{0,1:T(8,128)(2,1)S(1)}, u32[]{:S(2)}, u32[]{:S(2)}) %collective-permute-start.20) | collective-permute-done | bytes 524320 | tf_op jit(solution)/shard_map/ppermute | solution.py:32
  319.7 11.9 %collective-permute-done.22 = bf16[512,512]{0,1:T(8,128)(2,1)S(1)} collective-permute-done((bf16[512,512]{0,1:T(8,128)(2,1)S(1)}, bf16[512,512]{0,1:T(8,128)(2,1)S(1)}, u32[]{:S(2)}, u32[]{:S(2)}) %collective-permute-start.22) | collective-permute-done | bytes 524320 | tf_op jit(solution)/shard_map/ppermute | solution.py:32
  (114 shorter events, 35.8 us)
Async XLA Ops:
  6.5 44.0 %copy-start.14 = (bf16[512,32]{0,1:T(8,128)(2,1)S(1)}, bf16[512,32]{0,1:T(8,128)(2,1)}, u32[]{:S(2)}) copy-start(bf16[512,32]{0,1:T(8,128)(2,1)} %param.15) | copy-start | bytes 98308
  6.5 44.0 %copy-start.13 = (bf16[32,512]{1,0:T(8,128)(2,1)S(1)}, bf16[32,512]{1,0:T(8,128)(2,1)}, u32[]{:S(2)}) copy-start(bf16[32,512]{1,0:T(8,128)(2,1)} %param.12) | copy-start | bytes 98308
  6.5 44.1 %copy-start.16 = (bf16[32,128]{1,0:T(8,128)(2,1)S(1)}, bf16[32,128]{1,0:T(8,128)(2,1)}, u32[]{:S(2)}) copy-start(bf16[32,128]{1,0:T(8,128)(2,1)} %param.13) | copy-start | bytes 24580
  6.5 44.1 %copy-start.15 = (bf16[32,128]{1,0:T(8,128)(2,1)S(1)}, bf16[32,128]{1,0:T(8,128)(2,1)}, u32[]{:S(2)}) copy-start(bf16[32,128]{1,0:T(8,128)(2,1)} %param.14) | copy-start | bytes 24580
  6.5 274.2 %all-gather.2.cloned.1.call-start = ((), (), s32[]{:S(2)}) async-start(), calls=%async_computation.5 | async-start | bytes 9732096 | tf_op jit(solution)/shard_map/all_gather | solution.py:161
  10.2 12.1 %collective-permute-start.17 = (bf16[32,2304]{1,0:T(8,128)(2,1)S(1)}, bf16[32,2304]{1,0:T(8,128)(2,1)S(1)}, u32[]{:S(2)}, u32[]{:S(2)}) collective-permute-start(bf16[32,2304]{1,0:T(8,128)(2,1)S(1)} %get-tuple-element.33), channel_id=1, source_target_pairs={{0,0},{1,128},{4,1},{5,129},{8,4},{9,132},{12,5},{13,133},{16,8},{... | collective-permute-start | bytes 442376 | tf_op jit(solution)/shard_map/ppermute | solution.py:51
  14.8 7.5 %collective-permute-start.18 = (bf16[32,2304]{1,0:T(8,128)(2,1)S(1)}, bf16[32,2304]{1,0:T(8,128)(2,1)S(1)}, u32[]{:S(2)}, u32[]{:S(2)}) collective-permute-start(bf16[32,2304]{1,0:T(8,128)(2,1)S(1)} %get-tuple-element.34), channel_id=1, source_target_pairs={{0,1},{1,129},{4,0},{5,128},{8,5},{9,133},{12,4},{13,132},{16,9},{... | collective-permute-start | bytes 442376 | tf_op jit(solution)/shard_map/ppermute | solution.py:51
  18.9 18.8 %collective-permute-start = (bf16[512,512]{0,1:T(8,128)(2,1)S(1)}, bf16[512,512]{0,1:T(8,128)(2,1)S(1)}, u32[]{:S(2)}, u32[]{:S(2)}) collective-permute-start(bf16[512,512]{0,1:T(8,128)(2,1)S(1)} %copy.32), channel_id=1, source_target_pairs={{0,2},{2,0},{128,130},{130,128},{1,3},{3,1},{129,131},{131,129},{4... | collective-permute-start | bytes 1572872 | tf_op jit(solution)/shard_map/ppermute | solution.py:32
  21.6 23.0 %collective-permute-start.1 = (bf16[512,512]{0,1:T(8,128)(2,1)S(1)}, bf16[512,512]{0,1:T(8,128)(2,1)S(1)}, u32[]{:S(2)}, u32[]{:S(2)}) collective-permute-start(bf16[512,512]{0,1:T(8,128)(2,1)S(1)} %copy.32), channel_id=1, source_target_pairs={{0,128},{2,130},{128,0},{130,2},{1,129},{3,131},{129,1},{131,3},{4... | collective-permute-start | bytes 1572872 | tf_op jit(solution)/shard_map/ppermute | solution.py:32
  21.9 24.5 %collective-permute-start.2 = (bf16[512,512]{0,1:T(8,128)(2,1)S(1)}, bf16[512,512]{0,1:T(8,128)(2,1)S(1)}, u32[]{:S(2)}, u32[]{:S(2)}) collective-permute-start(bf16[512,512]{0,1:T(8,128)(2,1)S(1)} %copy.32), channel_id=1, source_target_pairs={{0,130},{2,128},{128,2},{130,0},{1,131},{3,129},{129,3},{131,1},{4... | collective-permute-start | bytes 1572872 | tf_op jit(solution)/shard_map/ppermute | solution.py:32
  37.7 24.5 %copy-start.2 = (bf16[512,512]{0,1:T(8,128)(2,1)}, bf16[512,512]{0,1:T(8,128)(2,1)S(1)}, u32[]{:S(2)}) copy-start(bf16[512,512]{0,1:T(8,128)(2,1)S(1)} %collective-permute-done) | copy-start | bytes 1572868
  44.6 1.9 copy-start.4
  46.4 0.8 copy-start.5
  48.8 44.1 %collective-permute-start.3 = (bf16[4,512,512]{1,2,0:T(8,128)(2,1)}, bf16[4,512,512]{1,2,0:T(8,128)(2,1)S(1)}, u32[]{:S(2)}, u32[]{:S(2)}) collective-permute-start(bf16[4,512,512]{1,2,0:T(8,128)(2,1)} %pad_maximum_fusion), channel_id=1, source_target_pairs={{0,1},{1,0},{2,3},{3,2},{4,5},{5,4},{6,7},{7,6},{8,9},{9,8},{10,11... | collective-permute-start | bytes 6291464 | tf_op jit(solution)/shard_map/ppermute | solution.py:28
  50.6 9.7 %collective-permute-start.4 = (bf16[32,640]{1,0:T(8,128)(2,1)S(1)}, bf16[32,640]{1,0:T(8,128)(2,1)S(1)}, u32[]{:S(2)}, u32[]{:S(2)}) collective-permute-start(bf16[32,640]{1,0:T(8,128)(2,1)S(1)} %get-tuple-element.37), channel_id=1, source_target_pairs={{0,0},{1,128},{4,1},{5,129},{8,4},{9,132},{12,5},{13,133},{16,8},{... | collective-permute-start | bytes 122888 | tf_op jit(solution)/shard_map/ppermute | solution.py:51
  52.6 8.9 %collective-permute-start.5 = (bf16[32,640]{1,0:T(8,128)(2,1)S(1)}, bf16[32,640]{1,0:T(8,128)(2,1)S(1)}, u32[]{:S(2)}, u32[]{:S(2)}) collective-permute-start(bf16[32,640]{1,0:T(8,128)(2,1)S(1)} %get-tuple-element.38), channel_id=1, source_target_pairs={{0,1},{1,129},{4,0},{5,128},{8,5},{9,133},{12,4},{13,132},{16,9},{... | collective-permute-start | bytes 122888 | tf_op jit(solution)/shard_map/ppermute | solution.py:51
  61.5 0.7 copy-start.10
  61.5 0.7 copy-start.11
  62.2 19.4 %all-to-all-start = ((bf16[8,64,128]{2,1,0:T(8,128)(2,1)}), bf16[8,64,128]{2,1,0:T(8,128)(2,1)S(1)}, u32[]{:S(2)}, u32[]{:S(2)}) async-start(bf16[8,64,128]{2,1,0:T(8,128)(2,1)} %broadcast_in_dim.20), calls=%async_computation | async-start | bytes 262144 | tf_op jit(solution)/shard_map/all_to_all | solution.py:16
  82.5 17.5 %all-to-all-start.1 = ((bf16[4,512,128]{2,1,0:T(8,128)(2,1)}), bf16[4,512,128]{2,1,0:T(8,128)(2,1)}, u32[]{:S(2)}, u32[]{:S(2)}) async-start(bf16[4,512,128]{2,1,0:T(8,128)(2,1)} %broadcast_in_dim.22), calls=%async_computation.1 | async-start | bytes 1048576 | tf_op jit(solution)/shard_map/all_to_all | solution.py:16
  93.0 3.0 copy-start.3
  93.0 7.0 %copy-start.12 = (bf16[64,512]{1,0:T(8,128)(2,1)S(1)}, bf16[64,512]{1,0:T(8,128)(2,1)}, u32[]{:S(2)}) copy-start(bf16[64,512]{1,0:T(8,128)(2,1)} %pad_maximum_fusion.7) | copy-start | bytes 196612
  100.8 19.0 %all-to-all-start.2 = ((bf16[8,64,512]{2,1,0:T(8,128)(2,1)}), bf16[8,64,512]{2,1,0:T(8,128)(2,1)S(1)}, u32[]{:S(2)}, u32[]{:S(2)}) async-start(bf16[8,64,512]{2,1,0:T(8,128)(2,1)} %broadcast_in_dim.24), calls=%async_computation.2 | async-start | bytes 1048576 | tf_op jit(solution)/shard_map/all_to_all | solution.py:16
  104.5 8.0 %copy-start.17 = (f32[2048]{0:T(1024)S(1)}, f32[2048]{0:T(1024)}, u32[]{:S(2)}) copy-start(f32[2048]{0:T(1024)} %param.11) | copy-start | bytes 24580
  112.5 3.4 %copy-start = (bf16[1024,2048]{0,1:T(8,128)(2,1)}, bf16[1024,2048]{0,1:T(8,128)(2,1)S(1)}, u32[]{:S(2)}) copy-start(bf16[1024,2048]{0,1:T(8,128)(2,1)S(1)} %get-tuple-element.8) | copy-start | bytes 12582916
  116.1 37.0 %copy-start.9 = (bf16[2,512,128]{1,2,0:T(8,128)(2,1)}, bf16[2,512,128]{1,2,0:T(8,128)(2,1)S(1)}, u32[]{:S(2)}) copy-start(bf16[2,512,128]{1,2,0:T(8,128)(2,1)S(1)} %copy.39) | copy-start | bytes 786436
  116.1 23.7 %collective-permute-start.6 = (bf16[2,512,128]{1,2,0:T(8,128)(2,1)S(1)}, bf16[2,512,128]{1,2,0:T(8,128)(2,1)S(1)}, u32[]{:S(2)}, u32[]{:S(2)}) collective-permute-start(bf16[2,512,128]{1,2,0:T(8,128)(2,1)S(1)} %copy.39), channel_id=1, source_target_pairs={{0,8},{4,12},{8,16},{12,20},{16,24},{20,28},{24,32},{28,36},{32,40... | collective-permute-start | bytes 786440 | tf_op jit(solution)/shard_map/ppermute | solution.py:170
  118.6 33.5 %collective-permute-start.7 = (bf16[2,512,128]{1,2,0:T(8,128)(2,1)S(1)}, bf16[2,512,128]{1,2,0:T(8,128)(2,1)S(1)}, u32[]{:S(2)}, u32[]{:S(2)}) collective-permute-start(bf16[2,512,128]{1,2,0:T(8,128)(2,1)S(1)} %copy.39), channel_id=1, source_target_pairs={{0,4},{4,8},{8,12},{12,16},{16,20},{20,24},{24,28},{28,32},{32,36}... | collective-permute-start | bytes 786440 | tf_op jit(solution)/shard_map/ppermute | solution.py:170
  121.0 38.5 %all-to-all-start.3 = ((bf16[4,512,256]{2,1,0:T(8,128)(2,1)}), bf16[4,512,256]{2,1,0:T(8,128)(2,1)}, u32[]{:S(2)}, u32[]{:S(2)}) async-start(bf16[4,512,256]{2,1,0:T(8,128)(2,1)} %broadcast_in_dim.25), calls=%async_computation.3 | async-start | bytes 2097152 | tf_op jit(solution)/shard_map/all_to_all | solution.py:16
  139.8 20.7 %copy-start.6 = (bf16[2,512,128]{1,2,0:T(8,128)(2,1)}, bf16[2,512,128]{1,2,0:T(8,128)(2,1)S(1)}, u32[]{:S(2)}) copy-start(bf16[2,512,128]{1,2,0:T(8,128)(2,1)S(1)} %reverse_select_fusion.1) | copy-start | bytes 786436
  152.1 1.0 copy-start.8
  153.1 18.5 %collective-permute-start.8 = (bf16[2,1536,128]{1,2,0:T(8,128)(2,1)}, bf16[2,1536,128]{1,2,0:T(8,128)(2,1)}, u32[]{:S(2)}, u32[]{:S(2)}) collective-permute-start(bf16[2,1536,128]{1,2,0:T(8,128)(2,1)} %pad_maximum_fusion.4), channel_id=1, source_target_pairs={{0,1},{1,0},{2,3},{3,2},{4,5},{5,4},{6,7},{7,6},{8,9},{9,8},{10,11... | collective-permute-start | bytes 2359304 | tf_op jit(solution)/shard_map/ppermute | solution.py:28
  160.5 26.8 %all-to-all-start.4 = ((bf16[4,512,256]{2,1,0:T(8,128)(2,1)}), bf16[4,512,256]{2,1,0:T(8,128)(2,1)S(1)}, u32[]{:S(2)}, u32[]{:S(2)}) async-start(bf16[4,512,256]{2,1,0:T(8,128)(2,1)} %broadcast_in_dim.27), calls=%async_computation.4 | async-start | bytes 2097152 | tf_op jit(solution)/shard_map/all_to_all | solution.py:16
  164.5 7.1 %copy-start.7 = (bf16[2,512,128]{1,2,0:T(8,128)(2,1)S(1)}, bf16[2,512,128]{1,2,0:T(8,128)(2,1)}, u32[]{:S(2)}) copy-start(bf16[2,512,128]{1,2,0:T(8,128)(2,1)} %copy-done.6) | copy-start | bytes 786436
  189.9 11.9 %collective-permute-start.9 = (bf16[2,1024,512]{1,2,0:T(8,128)(2,1)}, bf16[2,1024,512]{1,2,0:T(8,128)(2,1)}, u32[]{:S(2)}, u32[]{:S(2)}) collective-permute-start(bf16[2,1024,512]{1,2,0:T(8,128)(2,1)} %pad_maximum_fusion.1), channel_id=1, source_target_pairs={{0,1},{1,0},{2,3},{3,2},{4,5},{5,4},{6,7},{7,6},{8,9},{9,8},{10,11... | collective-permute-start | bytes 6291464 | tf_op jit(solution)/shard_map/ppermute | solution.py:28
  204.4 14.7 %collective-permute-start.10 = (bf16[512,512]{0,1:T(8,128)(2,1)S(1)}, bf16[512,512]{0,1:T(8,128)(2,1)S(1)}, u32[]{:S(2)}, u32[]{:S(2)}) collective-permute-start(bf16[512,512]{0,1:T(8,128)(2,1)S(1)} %get-tuple-element.27), channel_id=1, source_target_pairs={{0,2},{2,0},{128,130},{130,128},{1,3},{3,1},{129,131},{131,129},{4... | collective-permute-start | bytes 1572872 | tf_op jit(solution)/shard_map/ppermute | solution.py:32
  205.1 25.9 %collective-permute-start.12 = (bf16[512,512]{0,1:T(8,128)(2,1)S(1)}, bf16[512,512]{0,1:T(8,128)(2,1)S(1)}, u32[]{:S(2)}, u32[]{:S(2)}) collective-permute-start(bf16[512,512]{0,1:T(8,128)(2,1)S(1)} %get-tuple-element.28), channel_id=1, source_target_pairs={{0,130},{2,128},{128,2},{130,0},{1,131},{3,129},{129,3},{131,1},{4... | collective-permute-start | bytes 1572872 | tf_op jit(solution)/shard_map/ppermute | solution.py:32
  205.7 25.3 %collective-permute-start.11 = (bf16[512,512]{0,1:T(8,128)(2,1)S(1)}, bf16[512,512]{0,1:T(8,128)(2,1)S(1)}, u32[]{:S(2)}, u32[]{:S(2)}) collective-permute-start(bf16[512,512]{0,1:T(8,128)(2,1)S(1)} %slice.336), channel_id=1, source_target_pairs={{0,128},{2,130},{128,0},{130,2},{1,129},{3,131},{129,1},{131,3},{4... | collective-permute-start | bytes 1572872 | tf_op jit(solution)/shard_map/ppermute | solution.py:32
  231.5 14.6 %collective-permute-start.13 = (bf16[512,512]{0,1:T(8,128)(2,1)S(1)}, bf16[512,512]{0,1:T(8,128)(2,1)S(1)}, u32[]{:S(2)}, u32[]{:S(2)}) collective-permute-start(bf16[512,512]{0,1:T(8,128)(2,1)S(1)} %fusion.51), channel_id=1, source_target_pairs={{0,2},{2,0},{128,130},{130,128},{1,3},{3,1},{129,131},{131,129},{4... | collective-permute-start | bytes 1572872 | tf_op jit(solution)/shard_map/ppermute | solution.py:32
  232.2 22.1 %collective-permute-start.14 = (bf16[512,512]{0,1:T(8,128)(2,1)S(1)}, bf16[512,512]{0,1:T(8,128)(2,1)S(1)}, u32[]{:S(2)}, u32[]{:S(2)}) collective-permute-start(bf16[512,512]{0,1:T(8,128)(2,1)S(1)} %fusion.51), channel_id=1, source_target_pairs={{0,128},{2,130},{128,0},{130,2},{1,129},{3,131},{129,1},{131,3},{4... | collective-permute-start | bytes 1572872 | tf_op jit(solution)/shard_map/ppermute | solution.py:32
  232.2 25.9 %collective-permute-start.15 = (bf16[512,512]{0,1:T(8,128)(2,1)S(1)}, bf16[512,512]{0,1:T(8,128)(2,1)S(1)}, u32[]{:S(2)}, u32[]{:S(2)}) collective-permute-start(bf16[512,512]{0,1:T(8,128)(2,1)S(1)} %fusion.51), channel_id=1, source_target_pairs={{0,130},{2,128},{128,2},{130,0},{1,131},{3,129},{129,3},{131,1},{4... | collective-permute-start | bytes 1572872 | tf_op jit(solution)/shard_map/ppermute | solution.py:32
  258.4 4.4 %collective-permute-start.16 = (bf16[4,512,512]{1,2,0:T(8,128)(2,1)S(1)}, bf16[4,512,512]{1,2,0:T(8,128)(2,1)S(1)}, u32[]{:S(2)}, u32[]{:S(2)}) collective-permute-start(bf16[4,512,512]{1,2,0:T(8,128)(2,1)S(1)} %pad_maximum_fusion.2), channel_id=1, source_target_pairs={{0,1},{1,0},{2,3},{3,2},{4,5},{5,4},{6,7},{7,6},{8,9},{9,8},{10,11... | collective-permute-start | bytes 6291464 | tf_op jit(solution)/shard_map/ppermute | solution.py:28
  280.7 2.3 copy-start.18
  280.7 3.2 copy-start.1
  298.2 4.2 %collective-permute-start.19 = (bf16[2,1024,512]{1,2,0:T(8,128)(2,1)S(1)}, bf16[2,1024,512]{1,2,0:T(8,128)(2,1)S(1)}, u32[]{:S(2)}, u32[]{:S(2)}) collective-permute-start(bf16[2,1024,512]{1,2,0:T(8,128)(2,1)S(1)} %pad_maximum_fusion.3), channel_id=1, source_target_pairs={{0,1},{1,0},{2,3},{3,2},{4,5},{5,4},{6,7},{7,6},{8,9},{9,8},{10,11... | collective-permute-start | bytes 6291464 | tf_op jit(solution)/shard_map/ppermute | solution.py:28
  305.0 14.7 %collective-permute-start.20 = (bf16[512,512]{0,1:T(8,128)(2,1)S(1)}, bf16[512,512]{0,1:T(8,128)(2,1)S(1)}, u32[]{:S(2)}, u32[]{:S(2)}) collective-permute-start(bf16[512,512]{0,1:T(8,128)(2,1)S(1)} %get-tuple-element.25), channel_id=1, source_target_pairs={{0,2},{2,0},{128,130},{130,128},{1,3},{3,1},{129,131},{131,129},{4... | collective-permute-start | bytes 1572872 | tf_op jit(solution)/shard_map/ppermute | solution.py:32
  305.7 25.9 %collective-permute-start.22 = (bf16[512,512]{0,1:T(8,128)(2,1)S(1)}, bf16[512,512]{0,1:T(8,128)(2,1)S(1)}, u32[]{:S(2)}, u32[]{:S(2)}) collective-permute-start(bf16[512,512]{0,1:T(8,128)(2,1)S(1)} %get-tuple-element.26), channel_id=1, source_target_pairs={{0,130},{2,128},{128,2},{130,0},{1,131},{3,129},{129,3},{131,1},{4... | collective-permute-start | bytes 1572872 | tf_op jit(solution)/shard_map/ppermute | solution.py:32
  306.7 24.9 %collective-permute-start.21 = (bf16[512,512]{0,1:T(8,128)(2,1)S(1)}, bf16[512,512]{0,1:T(8,128)(2,1)S(1)}, u32[]{:S(2)}, u32[]{:S(2)}) collective-permute-start(bf16[512,512]{0,1:T(8,128)(2,1)S(1)} %slice.335), channel_id=1, source_target_pairs={{0,128},{2,130},{128,0},{130,2},{1,129},{3,131},{129,1},{131,3},{4... | collective-permute-start | bytes 1572872 | tf_op jit(solution)/shard_map/ppermute | solution.py:32
Sparse Core Ops, SparseCore 0:
  50.7 130.7 all-gather.1

commit v2 on v1

v2 whole, which is shorter than its diff:
```python
import jax
import jax.numpy as jnp
from jax import lax
from jax.experimental import pallas as pl
from jax.experimental.pallas import tpu as pltpu
from jax.sharding import Mesh
from jax.sharding import PartitionSpec as P

HEAD_DIM = 128
WINDOW = 1024
SEQ = ("yl", "x", "z")
FEATURES = ("yh", "c")
PLANE = ("x", "z")
PARTS = 2


def other_core(value):
    return lax.ppermute(value, "c", [(0, 1), (1, 0)])


def column_partner(value, flip):
    return lax.ppermute(value, ("yl", "yh"), [(i, i ^ flip) for i in range(4)])


def ordered(flag, first, second):
    return jnp.where(flag == 0, first, second), jnp.where(flag == 0, second, first)


def column_rows(sends):
    received = [
        lax.ppermute(send, ("yl", "c"), [(yl * 2 + c, c * 2 + (yl ^ swap)) for yl in range(2) for c in range(2)])
        for swap, send in enumerate(sends)
    ]
    return jnp.stack(ordered(lax.axis_index("c"), *received))


def column_blocks(share):
    blocks = [share]
    for flip in (1, 2, 3):
        blocks.append(column_partner(share, flip))
    mine = jnp.stack(blocks)
    return mine, other_core(mine)


def call(kernel, grid, scalars, in_specs, out_specs, out_shape, scratch=(), flops=0, moved=0):
    return pl.pallas_call(
        kernel,
        grid_spec=pltpu.PrefetchScalarGridSpec(
            num_scalar_prefetch=scalars,
            grid=grid,
            in_specs=in_specs,
            out_specs=out_specs,
            scratch_shapes=scratch,
        ),
        out_shape=out_shape,
        cost_estimate=pl.CostEstimate(flops=flops, bytes_accessed=moved, transcendentals=0),
    )


def store_normed(me_ref, mine_ref, theirs_ref, gain_ref, out_ref, run, at):
    n, f = mine_ref.shape[1:]
    parts = [
        (half * 2 + other, (mine_ref, theirs_ref)[other][run * 2 + half].astype(jnp.float32))
        for half in range(2)
        for other in range(2)
    ]
    squares = sum(jnp.sum(x * x, axis=1, keepdims=True) for _, x in parts)
    scale = lax.rsqrt(squares / (len(parts) * f) + 1e-06)
    for flip, x in parts:
        column = pl.multiple_of((me_ref[0] ^ flip) * f, f)
        gain = gain_ref[:, pl.ds(column, f)]
        out_ref[pl.ds(at, n), pl.ds(column, f)] = (x * scale * gain).astype(jnp.bfloat16)


def normed_rows(me, mine, theirs, gain):
    rows, f = mine.shape[1:]
    step = min(256, rows)

    def kernel(me_ref, mine_ref, theirs_ref, gain_ref, out_ref):
        store_normed(me_ref, mine_ref, theirs_ref, gain_ref, out_ref, 0, 0)

    block = pl.BlockSpec((2, step, f), lambda run, i, me: (run, i, 0))
    tiles = rows // step
    return call(
        kernel,
        (2, tiles),
        1,
        [block, block, pl.BlockSpec((1, 4 * f), lambda run, i, me: (0, 0))],
        pl.BlockSpec((step, 4 * f), lambda run, i, me: (run * tiles + i, 0)),
        jax.ShapeDtypeStruct((2 * rows, 4 * f), jnp.bfloat16),
        flops=rows * f * 100,
        moved=rows * f * 32,
    )(me, mine, theirs, gain[None])


def unit_terms(me, mine, theirs, gain, weights):
    rows, f = mine.shape[1:]
    chips, runs, r = weights.shape[:3]
    d = chips * runs * r
    width = weights.shape[3] // 3
    step = 256
    steps = width // step

    def kernel(
        me_ref, mine_ref, theirs_ref, gain_ref, gate_ref, up_ref, down_ref, near_ref, away_ref,
        normed, total,
    ):
        j = pl.program_id(0)

        @pl.when(j == 0)
        def _():
            for run in range(2):
                store_normed(
                    me_ref, mine_ref, theirs_ref, gain_ref, normed, run, run * rows
                )

        gate = up = 0.0
        for run in range(runs):
            x = normed[:, run * chips * r : (run + 1) * chips * r]
            gate_rows = gate_ref[:, run].reshape(chips * r, step)
            gate = gate + jnp.dot(x, gate_rows, preferred_element_type=jnp.float32)
            up_rows = up_ref[:, run].reshape(chips * r, step)
            up = up + jnp.dot(x, up_rows, preferred_element_type=jnp.float32)
        hidden = (gate / (1.0 + jnp.exp(-gate)) * up).astype(jnp.bfloat16)
        for place, flip in enumerate((1, 3, 0, 2)):
            term = lax.dot_general(
                hidden,
                feature_rows(down_ref, me_ref[0] ^ flip),
                (((1,), (1,)), ((), ())),
                preferred_element_type=jnp.float32,
            )
            out = total if place < 2 else near_ref
            cols = slice(place % 2 * f, (place % 2 + 1) * f)

            @pl.when(j == 0)
            def _():
                out[:, cols] = term

            @pl.when(j > 0)
            def _():
                out[:, cols] += term

        @pl.when(j == steps - 1)
        def _():
            away_ref[...] = total[...].astype(jnp.bfloat16)

    def whole(shape):
        return pl.BlockSpec(shape, lambda j, me: (0,) * len(shape))

    def weight(part):
        return pl.BlockSpec((chips, runs, r, step), lambda j, me: (0, 0, 0, part * steps + j))

    shape = (2 * rows, 2 * f)
    return call(
        kernel,
        (steps,),
        1,
        [whole(mine.shape), whole(mine.shape), whole((1, 4 * f))]
        + [weight(part) for part in range(3)],
        [whole(shape), whole(shape)],
        [jax.ShapeDtypeStruct(shape, jnp.float32), jax.ShapeDtypeStruct(shape, jnp.bfloat16)],
        [pltpu.VMEM((2 * rows, 4 * f), jnp.bfloat16), pltpu.VMEM(shape, jnp.float32)],
        flops=2 * 2 * rows * width * (2 * d + 4 * f),
        moved=2 * weights.size + 16 * rows * f * 2,
    )(me, mine, theirs, gain[None], weights, weights, weights)


def projected(left, weights, start, width):
    n, d = left.shape
    chips, runs, r = weights.shape[:3]
    step = 512

    def kernel(x_ref, w_ref, out_ref):
        total = 0.0
        for run in range(runs):
            w = w_ref[:, run].reshape(chips * r, width)
            x = x_ref[:, run * chips * r : (run + 1) * chips * r]
            total = total + jnp.dot(x, w, preferred_element_type=jnp.float32)
        out_ref[...] = total.astype(jnp.bfloat16)

    return call(
        kernel,
        (n // step,),
        0,
        [
            pl.BlockSpec((step, d), lambda i: (i, 0)),
            pl.BlockSpec((chips, runs, r, width), lambda i: (0, 0, 0, start // width)),
        ],
        pl.BlockSpec((step, width), lambda i: (i, 0)),
        jax.ShapeDtypeStruct((n, width), jnp.bfloat16),
        flops=2 * n * d * width,
        moved=2 * (n * d + d * width + n * width),
    )(left, weights)


def feature_rows(weights_ref, block):
    chips, _, r, k = weights_ref.shape
    half = chips // 2
    at = pl.multiple_of(lax.rem(block, 2) * half, half)
    return weights_ref[pl.ds(at, half), lax.div(block, 2)].reshape(half * r, k)


def head_terms(me, attended, weights, part):
    rows, width = attended.shape[1] // PARTS, attended.shape[2]
    f = weights.shape[0] * weights.shape[1] * weights.shape[2] // 4

    def kernel(me_ref, left_ref, weights_ref, near_ref, away_ref):
        left = left_ref[...].reshape(2 * rows, width)
        for place, flip in enumerate((1, 3, 0, 2)):
            term = lax.dot_general(
                left,
                feature_rows(weights_ref, me_ref[0] ^ flip),
                (((1,), (1,)), ((), ())),
                preferred_element_type=jnp.float32,
            )
            out = away_ref if place < 2 else near_ref
            out[:, place % 2 * f : (place % 2 + 1) * f] = term.astype(out.dtype)

    shape = (2 * rows, 2 * f)
    whole = pl.BlockSpec(shape, lambda i, me: (0, 0))
    return call(
        kernel,
        (1,),
        1,
        [
            pl.BlockSpec((2, rows, width), lambda i, me: (0, part, 0)),
            pl.BlockSpec((*weights.shape[:3], width), lambda i, me: (0, 0, 0, 1)),
        ],
        [whole, whole],
        [jax.ShapeDtypeStruct(shape, jnp.float32), jax.ShapeDtypeStruct(shape, jnp.bfloat16)],
        flops=4 * rows * 4 * f * width,
        moved=8 * f * width + 24 * rows * f,
    )(me, attended, weights)


def column_sum(near, away):
    rows, f = near.shape[0] // 2, near.shape[1] // 2
    both = near + other_core(away).astype(jnp.float32)
    total = both[:rows, :f]
    sent = (
        (both[:rows, f:], 1),
        (both[rows:, :f], 2),
        (both[rows:, f:], 3),
    )
    for value, flip in sent:
        total = total + column_partner(value.astype(jnp.bfloat16), flip).astype(jnp.float32)
    return total


def window_attention(queries, keys, values, first_key):
    rows, width = queries.shape[1:]
    span = keys.shape[1]
    count = width // HEAD_DIM
    step = min(256, rows)
    seen = WINDOW + step
    scale = HEAD_DIM ** (-0.5)

    def kernel(first_ref, q_ref, k_ref, v_ref, out_ref):
        run, tile = pl.program_id(0), pl.program_id(1)
        start = pl.multiple_of(tile * step + span - rows - WINDOW, step)
        k = k_ref[0, pl.ds(start, seen), :]
        v = v_ref[0, pl.ds(start, seen), :]
        query_pos = lax.broadcasted_iota(jnp.int32, (step, seen), 0)
        key_pos = lax.broadcasted_iota(jnp.int32, (step, seen), 1)
        distance = query_pos + WINDOW - key_pos
        allowed = (distance >= 0) & (distance < WINDOW)
        allowed = allowed & (key_pos >= -first_ref[run] - start)
        for head in range(count):
            cols = slice(head * HEAD_DIM, (head + 1) * HEAD_DIM)
            scores = lax.dot_general(
                q_ref[0, :, cols], k, (((1,), (1,)), ((), ())), preferred_element_type=jnp.float32
            )
            scores = jnp.where(allowed, scores * scale, -1e30)
            raised = jnp.exp(scores - jnp.max(scores, axis=1, keepdims=True))
            total = jnp.sum(raised, axis=1, keepdims=True)
            mixed = jnp.dot(raised.astype(jnp.bfloat16), v, preferred_element_type=jnp.float32)
            out_ref[0, :, cols] = (mixed / total).astype(jnp.bfloat16)

    whole = pl.BlockSpec((1, span, HEAD_DIM), lambda run, tile, first: (run, 0, 0))
    part = pl.BlockSpec((1, step, width), lambda run, tile, first: (run, tile, 0))
    return call(
        kernel,
        (2, rows // step),
        1,
        [part, whole, whole],
        part,
        jax.ShapeDtypeStruct(queries.shape, jnp.bfloat16),
        flops=2 * rows * width * seen * 4,
        moved=2 * (2 * queries.size + keys.size + values.size),
    )(first_key, queries, keys, values)


def packed(parity, parts):
    arrays = [array for part in parts for array, *_ in part]
    rows = arrays[0].shape[0]
    width = sum(-(-size // 128) * 128 for _, _, size in parts[0])

    def kernel(parity_ref, *refs):
        ins, outs = refs[:-2], refs[-2:]
        for swap in range(2):

            @pl.when(parity_ref[0] == swap)
            def _():
                for h in range(2):
                    out = outs[h ^ swap]
                    at = 0
                    for i, (_, start, size) in enumerate(parts[h]):
                        ref = ins[h * len(parts[0]) + i]
                        out[:, at : at + size] = ref[:, start : start + size]
                        full = -(-size // 128) * 128
                        if full > size:
                            out[:, at + size : at + full] = jnp.zeros(
                                (rows, full - size), jnp.bfloat16
                            )
                        at += full

    def spec(shape):
        return pl.BlockSpec(shape, lambda i, parity: (0, 0))

    return call(
        kernel,
        (1,),
        1,
        [spec(array.shape) for array in arrays],
        [spec((rows, width))] * 2,
        [jax.ShapeDtypeStruct((rows, width), jnp.bfloat16)] * 2,
        moved=8 * rows * width,
    )(parity, *arrays)


def per_device(tokens, attn_gain, w_query, w_key, w_value, w_out, mlp_gain, w_gate, w_up, w_down):
    rows = tokens.shape[0]
    yl, yh, core = (lax.axis_index(name) for name in ("yl", "yh", "c"))
    place = lax.axis_index(PLANE)
    plane = lax.axis_size("x") * lax.axis_size("z")
    me = jnp.reshape(yh * 2 + core, (1,)).astype(jnp.int32)
    parity = jnp.reshape(yl, (1,)).astype(jnp.int32)
    out_t, down_t = w_out.T, w_down.T
    kv_width = w_key.shape[1]
    heads = w_query.shape[1] // 2
    units = w_gate.shape[1] // 2

    attn_rows = column_rows(
        packed(
            parity,
            [
                [
                    (w_query, h * heads, heads),
                    (out_t, h * heads, heads),
                    ((w_key, w_value)[h], 0, kv_width),
                ]
                for h in range(2)
            ],
        )
    )
    attn_full = lax.all_gather(attn_rows[None], "z", axis=0, tiled=True)
    mlp_rows = column_rows(
        packed(
            parity,
            [[(array, h * units, units) for array in (w_gate, w_up, down_t)] for h in range(2)],
        )
    )
    attn_full = lax.all_gather(attn_full, "x", axis=0, tiled=True)
    normed = normed_rows(me, *column_blocks(tokens), attn_gain)
    mlp_rows, attn_full, normed = lax.optimization_barrier((mlp_rows, attn_full, normed))
    mlp_full = lax.all_gather(mlp_rows[None], PLANE, axis=0, tiled=True)
    fresh = projected(normed, attn_full, 2 * heads, kv_width).reshape(2, rows, kv_width)
    reach = -(-WINDOW // rows)
    context = [fresh]
    for step in range(1, reach + 1):
        came = lax.ppermute(fresh, PLANE, [(i, (i + step) % plane) for i in range(plane)])
        context.insert(0, jnp.where(place < step, came[::-1], came))
    context = jnp.concatenate(context, axis=1)
    keys, values = ordered(core, context, other_core(context))

    queries = projected(normed, attn_full, 0, heads).reshape(2, rows, heads)
    runs = jnp.stack([yl, 1 - yl])
    first_key = ((runs * plane + place - reach) * rows).astype(jnp.int32)
    attended = window_attention(queries, keys, values, first_key)
    part = rows // PARTS
    outputs = []
    for at in range(0, rows, part):
        attn_share = column_sum(*head_terms(me, attended, attn_full, at // part))
        stream = tokens[at : at + part].astype(jnp.float32) + attn_share
        stream = stream.astype(jnp.bfloat16)
        terms = unit_terms(me, *column_blocks(stream), mlp_gain, mlp_full)
        outputs.append((stream.astype(jnp.float32) + column_sum(*terms)).astype(jnp.bfloat16))
    return jnp.concatenate(outputs, axis=0)


def solution(mesh):
    split = Mesh(mesh.devices.reshape(2, 4, 8, 2, 2), ("yl", "x", "z", "yh", "c"))
    both = P(SEQ, FEATURES)
    down = P(FEATURES, SEQ)
    placed = (both, P(), both, both, both, down, P(), both, both, down)

    return jax.shard_map(per_device, mesh=split, in_specs=placed, out_specs=both, check_vma=False)
```

time: 347 us -> 268 us (0.77); the launches traced: 340 us -> 268 us
  Pallas kernels: 0 us -> 60.1 us
  matrix products: 41.8 us -> 0 us
  waiting for transfers between devices: 145 us -> 108 us
  other arithmetic: 43.6 us -> 11.1 us
  starting transfers between devices: 78.9 us -> 49.3 us
  blocking collectives: 0 us -> 25.3 us
  local copies, waits for them, and re-layouts: 16.3 us -> 0.29 us
    pallas_call x0 -> x10, Pallas kernels: none -> 60.1 us  [the longest x2 27.7 us: unit_terms(): call(kernel, (steps,), 1, [whole(mine.shape), whole(mine.shape), whole((1...]
    all_to_all x5 -> x0, starting transfers between devices: 33.1 us -> none  [spread(): lax.all_to_all(jnp.broadcast_to(value[None], (length, *value.shape)), axi...]
    dot_general x13 -> x0, matrix products: 32.4 us -> none  [the longest x4 20.5 us: product(): return jnp.dot(left, right, preferred_element_type=jnp.float32)]
    reduce_sum x2 -> x0, other arithmetic: 25.5 us -> none  [scaled_rows(): mean_square = jnp.mean(values * values, axis=1, keepdims=True)]
    all_gather x0 -> x1, blocking collectives: none -> 25.3 us  [per_device(): attn_full = lax.all_gather(attn_rows[None], 'z', axis=0, tiled=True)]
    ppermute x12 -> x21, starting transfers between devices: 12.5 us -> 31.3 us  [column_partner(): return lax.ppermute(value, ('yl', 'yh'), [(i, i ^ flip) for i in range(4)])]
    ppermute x12 -> x21, waiting for transfers between devices: 94.3 us -> 77.1 us  [column_partner(): return lax.ppermute(value, ('yl', 'yh'), [(i, i ^ flip) for i in range(4)])]
    ppermute x5 -> x8, waiting for transfers between devices: 11.7 us -> 0.02 us  [other_core(): return lax.ppermute(value, 'c', [(0, 1), (1, 0)])]
  transfers between devices with their start and end apart: 29 -> 37, of which waited for: 20 -> 24; matrix products, arithmetic and copies ran while one was open for 22% -> 4% of each run, Pallas kernels for 0% -> 22%
where the time goes in v2:
time: 268 us
  waiting for transfers between devices  108 us (40%)
  Pallas kernels  60.1 us (22%)
  starting transfers between devices  49.3 us (18%)
  blocking collectives  25.3 us (9%)
  between operations  13.6 us (5%)
  other arithmetic  11.1 us (4%)
    ppermute x21, waiting for transfers between devices, column_partner(): return lax.ppermute(value, ('yl', 'yh'), [(i, i ^ flip) for i in range(4)])  77.1 us
    ppermute x21, starting transfers between devices, column_partner(): return lax.ppermute(value, ('yl', 'yh'), [(i, i ^ flip) for i in range(4)])  31.3 us
    pallas_call x2, Pallas kernels, unit_terms(): call(kernel, (steps,), 1, [whole(mine.shape), whole(mine.shape), whole((1...  27.7 us
    ppermute x2, waiting for transfers between devices, per_device(): lax.ppermute(fresh, PLANE, [(i, (i + step) % plane) for i in range(plane)])  25.5 us
    all_gather x1, blocking collectives, per_device(): attn_full = lax.all_gather(attn_rows[None], 'z', axis=0, tiled=True)  25.3 us
    pallas_call x1, Pallas kernels, window_attention(): call(kernel, (2, rows // step), 1, [part, whole, whole], part, jax.ShapeD...  8.41 us
    ppermute x4, starting transfers between devices, column_rows(): lax.ppermute(send, ('yl', 'c'), [(yl * 2 + c, c * 2 + (yl ^ swap)) for yl...  8.07 us
    pallas_call x2, Pallas kernels, projected(): call(kernel, (n // step,), 0, [pl.BlockSpec((step, d), lambda i: (i, 0)),...  7.83 us
  transfers between devices with their start and end apart: 37, of which 24 were waited for; matrix products, arithmetic and copies ran while one was open for 4% of the time, Pallas kernels for 22%

profile of v2, /device:TPU:1, one launch (start us, length us, event | category | flops | bytes accessed | tf_op | source)
XLA Modules:
  0.0 268.0 jit_solution(11577228534841442686)
XLA Ops:
  6.5 1.5 shard_map.101
  8.1 4.6 %collective-permute-start.2 = (bf16[32,640]{1,0:T(8,128)(2,1)}, bf16[32,640]{1,0:T(8,128)(2,1)S(1)}, u32[]{:S(2)}, u32[]{:S(2)}) collective-permute-start(bf16[32,640]{1,0:T(8,128)(2,1)} %get-tuple-element.22), channel_id=1, source_target_pairs={{0,0},{1,128},{128,1},{129,129},{2,2},{3,130},{130,3},{131,131},{4... | collective-permute-start | bytes 122888 | tf_op jit(solution)/shard_map/ppermute | solution.py:31
  12.7 1.8 collective-permute-done.2
  14.6 25.3 %all-gather = bf16[16,32,640]{2,1,0:T(8,128)(2,1)} all-gather(bf16[2,32,640]{2,1,0:T(8,128)(2,1)S(1)} %pad_maximum_fusion.6), channel_id=2, replica_groups=mesh['yl'=2,'x'=4,'z'=8,'yh'=2,'c'=2] {'z'}, dimensions={0}, use_global_device_ids=true | all-gather | bytes 737280 | tf_op jit(solution)/shard_map/all_gather | solution.py:356
  40.0 2.9 %collective-permute-start.4 = (bf16[512,512]{1,0:T(8,128)(2,1)}, bf16[512,512]{1,0:T(8,128)(2,1)S(1)}, u32[]{:S(2)}, u32[]{:S(2)}) collective-permute-start(bf16[512,512]{1,0:T(8,128)(2,1)} %param.10), channel_id=1, source_target_pairs={{0,2},{2,0},{128,130},{130,128},{1,3},{3,1},{129,131},{131,129},{4... | collective-permute-start | bytes 1572872 | tf_op jit(solution)/shard_map/ppermute | solution.py:22
  44.0 5.9 %collective-permute-done.4 = bf16[512,512]{1,0:T(8,128)(2,1)S(1)} collective-permute-done((bf16[512,512]{1,0:T(8,128)(2,1)}, bf16[512,512]{1,0:T(8,128)(2,1)S(1)}, u32[]{:S(2)}, u32[]{:S(2)}) %collective-permute-start.4) | collective-permute-done | bytes 524320 | tf_op jit(solution)/shard_map/ppermute | solution.py:22
  49.9 10.8 %collective-permute-done.5 = bf16[512,512]{1,0:T(8,128)(2,1)S(1)} collective-permute-done((bf16[512,512]{1,0:T(8,128)(2,1)}, bf16[512,512]{1,0:T(8,128)(2,1)S(1)}, u32[]{:S(2)}, u32[]{:S(2)}) %collective-permute-start.5) | collective-permute-done | bytes 524320 | tf_op jit(solution)/shard_map/ppermute | solution.py:22
  60.7 3.9 %collective-permute-done.6 = bf16[512,512]{1,0:T(8,128)(2,1)S(1)} collective-permute-done((bf16[512,512]{1,0:T(8,128)(2,1)}, bf16[512,512]{1,0:T(8,128)(2,1)S(1)}, u32[]{:S(2)}, u32[]{:S(2)}) %collective-permute-start.6) | collective-permute-done | bytes 524320 | tf_op jit(solution)/shard_map/ppermute | solution.py:22
  64.9 3.5 %collective-permute-start.7 = (bf16[4,512,512]{2,1,0:T(8,128)(2,1)S(1)}, bf16[4,512,512]{2,1,0:T(8,128)(2,1)}, u32[]{:S(2)}, u32[]{:S(2)}) collective-permute-start(bf16[4,512,512]{2,1,0:T(8,128)(2,1)S(1)} %pad_maximum_fusion.mine_ref), channel_id=1, source_target_pairs={{0,1},{1,0},{2,3},{3,2},{4,5},{5,4},{6,7},{7,6},{8,9},{9,8},{10,11... | collective-permute-start | bytes 6291464 | tf_op jit(solution)/shard_map/ppermute | solution.py:18
  68.4 1.9 shard_map.100
  70.4 3.3 %collective-permute-start = (bf16[32,2304]{1,0:T(8,128)(2,1)}, bf16[32,2304]{1,0:T(8,128)(2,1)S(1)}, u32[]{:S(2)}, u32[]{:S(2)}) collective-permute-start(bf16[32,2304]{1,0:T(8,128)(2,1)} %get-tuple-element.20), channel_id=1, source_target_pairs={{0,0},{1,128},{128,1},{129,129},{2,2},{3,130},{130,3},{131,131},{4... | collective-permute-start | bytes 442376 | tf_op jit(solution)/shard_map/ppermute | solution.py:31
  73.8 3.6 %collective-permute-done = bf16[32,2304]{1,0:T(8,128)(2,1)S(1)} collective-permute-done((bf16[32,2304]{1,0:T(8,128)(2,1)}, bf16[32,2304]{1,0:T(8,128)(2,1)S(1)}, u32[]{:S(2)}, u32[]{:S(2)}) %collective-permute-start) | collective-permute-done | bytes 147488 | tf_op jit(solution)/shard_map/ppermute | solution.py:31
  78.4 5.6 %shard_map.102.x_ref = bf16[1024,2048]{1,0:T(8,128)(2,1)} custom-call(s32[1]{0:T(128)} %bitcast.me_ref, bf16[4,512,512]{2,1,0:T(8,128)(2,1)} %copy-done, bf16[4,512,512]{2,1,0:T(8,128)(2,1)} %collective-permute-done.7.theirs_ref, f32[1,2048]{1,0:T(1,128)} %bitcast.61), custom_call_target="tpu_custom_call" | custom-call | flops 26214400 | bytes 8388608 | tf_op jit(solution)/shard_map/pallas_call | solution.py:84
  84.1 3.8 %shard_map.104 = bf16[1024,128]{1,0:T(8,128)(2,1)} custom-call(bf16[1024,2048]{1,0:T(8,128)(2,1)} %shard_map.102.x_ref, bf16[32,2,32,640]{3,2,1,0:T(8,128)(2,1)} %all-gather.5.cloned.1.call-done.w_ref.weights_ref), custom_call_target="tpu_custom_call" | custom-call | flops 536870912 | bytes 4980736 | tf_op jit(solution)/shard_map/pallas_call | solution.py:181
  87.9 1.6 collective-permute-start.8
  90.5 10.0 %collective-permute-done.8 = bf16[2,512,128]{2,1,0:T(8,128)(2,1)S(1)} collective-permute-done((bf16[2,512,128]{2,1,0:T(8,128)(2,1)}, bf16[2,512,128]{2,1,0:T(8,128)(2,1)S(1)}, u32[]{:S(2)}, u32[]{:S(2)}) %collective-permute-start.8) | collective-permute-done | bytes 262176 | tf_op jit(solution)/shard_map/ppermute | solution.py:371
  100.6 15.5 %collective-permute-done.9 = bf16[2,512,128]{2,1,0:T(8,128)(2,1)S(1)} collective-permute-done((bf16[2,512,128]{2,1,0:T(8,128)(2,1)}, bf16[2,512,128]{2,1,0:T(8,128)(2,1)S(1)}, u32[]{:S(2)}, u32[]{:S(2)}) %collective-permute-start.9) | collective-permute-done | bytes 262176 | tf_op jit(solution)/shard_map/ppermute | solution.py:371
  118.9 4.1 %shard_map.103 = bf16[1024,256]{1,0:T(8,128)(2,1)} custom-call(bf16[1024,2048]{1,0:T(8,128)(2,1)} %shard_map.102.x_ref, bf16[32,2,32,640]{3,2,1,0:T(8,128)(2,1)} %all-gather.5.cloned.1.call-done.w_ref.weights_ref), custom_call_target="tpu_custom_call" | custom-call | flops 1073741824 | bytes 5767168 | tf_op jit(solution)/shard_map/pallas_call | solution.py:181
  123.0 1.5 broadcast_select_fusion
  124.5 8.4 %shard_map.105.left_ref = bf16[2,512,256]{2,1,0:T(8,128)(2,1)} custom-call(s32[2]{0:T(128)} %add_multiply_fusion.1.first_ref, bf16[2,512,256]{2,1,0:T(8,128)(2,1)} %bitcast.45, bf16[2,1536,128]{2,1,0:T(8,128)(2,1)} %get-tuple-element.44.k_ref, bf16[2,1536,128]{2,1,0:T(8,128)(2,1)} %get-tuple-element.43.v_ref), custom_call_target="tpu_custom_call" | custom-call | flops 1342177280 | bytes 2621440 | tf_op jit(solution)/shard_map/pallas_call | solution.py:281
  132.9 3.4 %shard_map.108 = (f32[512,1024]{1,0:T(8,128)}, bf16[512,1024]{1,0:T(8,128)(2,1)}) custom-call(s32[1]{0:T(128)} %bitcast.me_ref, bf16[2,512,256]{2,1,0:T(8,128)(2,1)} %shard_map.105.left_ref, bf16[32,2,32,640]{3,2,1,0:T(8,128)(2,1)} %all-gather.5.cloned.1.call-done.w_ref.weights_ref), custom_call_target="tpu_custom_call" | custom-call | flops 536870912 | bytes 4194304 | tf_op jit(solution)/shard_map/pallas_call | solution.py:221
  136.3 3.6 %shard_map.106 = (f32[512,1024]{1,0:T(8,128)}, bf16[512,1024]{1,0:T(8,128)(2,1)}) custom-call(s32[1]{0:T(128)} %bitcast.me_ref, bf16[2,512,256]{2,1,0:T(8,128)(2,1)} %shard_map.105.left_ref, bf16[32,2,32,640]{3,2,1,0:T(8,128)(2,1)} %all-gather.5.cloned.1.call-done.w_ref.weights_ref), custom_call_target="tpu_custom_call" | custom-call | flops 536870912 | bytes 4194304 | tf_op jit(solution)/shard_map/pallas_call | solution.py:221
  140.4 1.8 fusion.20
  142.3 2.7 %collective-permute-start.24 = (bf16[256,512]{1,0:T(8,128)(2,1)S(1)}, bf16[256,512]{1,0:T(8,128)(2,1)S(1)}, u32[]{:S(2)}, u32[]{:S(2)}) collective-permute-start(bf16[256,512]{1,0:T(8,128)(2,1)S(1)} %get-tuple-element.54), channel_id=1, source_target_pairs={{0,2},{2,0},{128,130},{130,128},{1,3},{3,1},{129,131},{131,129},{4... | collective-permute-start | bytes 786440 | tf_op jit(solution)/shard_map/ppermute | solution.py:22
  145.0 1.4 collective-permute-start.25
  149.0 1.4 collective-permute-start.13
  150.4 1.3 collective-permute-done.24
  151.7 3.5 %collective-permute-start.14 = (bf16[256,512]{1,0:T(8,128)(2,1)S(1)}, bf16[256,512]{1,0:T(8,128)(2,1)S(1)}, u32[]{:S(2)}, u32[]{:S(2)}) collective-permute-start(bf16[256,512]{1,0:T(8,128)(2,1)S(1)} %get-tuple-element.49), channel_id=1, source_target_pairs={{0,130},{2,128},{128,2},{130,0},{1,131},{3,129},{129,3},{131,1},{4... | collective-permute-start | bytes 786440 | tf_op jit(solution)/shard_map/ppermute | solution.py:22
  155.2 3.3 %collective-permute-done.25 = bf16[256,512]{1,0:T(8,128)(2,1)S(1)} collective-permute-done((bf16[256,512]{1,0:T(8,128)(2,1)S(1)}, bf16[256,512]{1,0:T(8,128)(2,1)S(1)}, u32[]{:S(2)}, u32[]{:S(2)}) %collective-permute-start.25) | collective-permute-done | bytes 262176 | tf_op jit(solution)/shard_map/ppermute | solution.py:22
  158.6 4.4 %collective-permute-done.12 = bf16[256,512]{1,0:T(8,128)(2,1)S(1)} collective-permute-done((bf16[256,512]{1,0:T(8,128)(2,1)S(1)}, bf16[256,512]{1,0:T(8,128)(2,1)S(1)}, u32[]{:S(2)}, u32[]{:S(2)}) %collective-permute-start.12) | collective-permute-done | bytes 262176 | tf_op jit(solution)/shard_map/ppermute | solution.py:22
  163.0 6.9 %collective-permute-done.13 = bf16[256,512]{1,0:T(8,128)(2,1)S(1)} collective-permute-done((bf16[256,512]{1,0:T(8,128)(2,1)S(1)}, bf16[256,512]{1,0:T(8,128)(2,1)S(1)}, u32[]{:S(2)}, u32[]{:S(2)}) %collective-permute-start.13) | collective-permute-done | bytes 262176 | tf_op jit(solution)/shard_map/ppermute | solution.py:22
  170.2 1.9 collective-permute-start.15
  172.2 1.4 collective-permute-start.16
  174.2 4.7 %collective-permute-done.15 = bf16[256,512]{1,0:T(8,128)(2,1)S(1)} collective-permute-done((bf16[256,512]{1,0:T(8,128)(2,1)S(1)}, bf16[256,512]{1,0:T(8,128)(2,1)S(1)}, u32[]{:S(2)}, u32[]{:S(2)}) %collective-permute-start.15) | collective-permute-done | bytes 262176 | tf_op jit(solution)/shard_map/ppermute | solution.py:22
  178.9 6.5 %collective-permute-done.16 = bf16[256,512]{1,0:T(8,128)(2,1)S(1)} collective-permute-done((bf16[256,512]{1,0:T(8,128)(2,1)S(1)}, bf16[256,512]{1,0:T(8,128)(2,1)S(1)}, u32[]{:S(2)}, u32[]{:S(2)}) %collective-permute-start.16) | collective-permute-done | bytes 262176 | tf_op jit(solution)/shard_map/ppermute | solution.py:22
  186.7 1.8 collective-permute-start.27
  190.3 5.8 %collective-permute-done.27 = bf16[256,512]{1,0:T(8,128)(2,1)S(1)} collective-permute-done((bf16[256,512]{1,0:T(8,128)(2,1)S(1)}, bf16[256,512]{1,0:T(8,128)(2,1)S(1)}, u32[]{:S(2)}, u32[]{:S(2)}) %collective-permute-start.27) | collective-permute-done | bytes 262176 | tf_op jit(solution)/shard_map/ppermute | solution.py:22
  196.1 5.5 %collective-permute-done.28 = bf16[256,512]{1,0:T(8,128)(2,1)S(1)} collective-permute-done((bf16[256,512]{1,0:T(8,128)(2,1)S(1)}, bf16[256,512]{1,0:T(8,128)(2,1)S(1)}, u32[]{:S(2)}, u32[]{:S(2)}) %collective-permute-start.28) | collective-permute-done | bytes 262176 | tf_op jit(solution)/shard_map/ppermute | solution.py:22
  203.1 13.8 %shard_map.107 = (f32[512,1024]{1,0:T(8,128)}, bf16[512,1024]{1,0:T(8,128)(2,1)}) custom-call(s32[1]{0:T(128)} %bitcast.me_ref, bf16[4,256,512]{2,1,0:T(8,128)(2,1)} %copy-done.1, bf16[4,256,512]{2,1,0:T(8,128)(2,1)} %collective-permute-done.18.theirs_ref, f32[1,2048]{1,0:T(1,128)} %bitcast.59, bf16[32,2,32,2304]{3,2,1,0:T(8,128)(2,1)} %bitcast.31, ...), custom_call_target="tpu_custom_call" | custom-call | flops 4831838208 | bytes 13631488 | tf_op jit(solution)/shard_map/pallas_call | solution.py:154
  217.0 13.9 %shard_map.109 = (f32[512,1024]{1,0:T(8,128)}, bf16[512,1024]{1,0:T(8,128)(2,1)}) custom-call(s32[1]{0:T(128)} %bitcast.me_ref, bf16[4,256,512]{2,1,0:T(8,128)(2,1)} %copy-done.2, bf16[4,256,512]{2,1,0:T(8,128)(2,1)} %collective-permute-done.30.theirs_ref, f32[1,2048]{1,0:T(1,128)} %bitcast.60, bf16[32,2,32,2304]{3,2,1,0:T(8,128)(2,1)} %bitcast.34, ...), custom_call_target="tpu_custom_call" | custom-call | flops 4831838208 | bytes 13631488 | tf_op jit(solution)/shard_map/pallas_call | solution.py:154
  231.3 2.2 fusion.17
  233.5 1.9 collective-permute-start.20
  237.7 1.6 collective-permute-start.32
  240.5 2.4 collective-permute-done.20
  242.9 2.4 collective-permute-start.34
  245.3 3.2 %collective-permute-done.21 = bf16[256,512]{1,0:T(8,128)(2,1)S(1)} collective-permute-done((bf16[256,512]{1,0:T(8,128)(2,1)S(1)}, bf16[256,512]{1,0:T(8,128)(2,1)S(1)}, u32[]{:S(2)}, u32[]{:S(2)}) %collective-permute-start.21) | collective-permute-done | bytes 262176 | tf_op jit(solution)/shard_map/ppermute | solution.py:22
  249.5 4.7 %collective-permute-done.32 = bf16[256,512]{1,0:T(8,128)(2,1)S(1)} collective-permute-done((bf16[256,512]{1,0:T(8,128)(2,1)S(1)}, bf16[256,512]{1,0:T(8,128)(2,1)S(1)}, u32[]{:S(2)}, u32[]{:S(2)}) %collective-permute-start.32) | collective-permute-done | bytes 262176 | tf_op jit(solution)/shard_map/ppermute | solution.py:22
  254.2 5.6 %collective-permute-done.33 = bf16[256,512]{1,0:T(8,128)(2,1)S(1)} collective-permute-done((bf16[256,512]{1,0:T(8,128)(2,1)S(1)}, bf16[256,512]{1,0:T(8,128)(2,1)S(1)}, u32[]{:S(2)}, u32[]{:S(2)}) %collective-permute-start.33) | collective-permute-done | bytes 262176 | tf_op jit(solution)/shard_map/ppermute | solution.py:22
  (79 shorter events, 21.7 us)
Async XLA Ops:
  6.5 58.1 %copy-start.7 = (bf16[512,512]{1,0:T(8,128)(2,1)S(1)}, bf16[512,512]{1,0:T(8,128)(2,1)}, u32[]{:S(2)}) copy-start(bf16[512,512]{1,0:T(8,128)(2,1)} %param.10) | copy-start | bytes 1572868
  6.5 77.5 %all-gather.5.cloned.1.call-start = ((), (), s32[]{:S(2)}) async-start(), calls=%async_computation | async-start | bytes 3276800 | tf_op jit(solution)/shard_map/all_gather | solution.py:363
  8.1 6.5 %collective-permute-start.2 = (bf16[32,640]{1,0:T(8,128)(2,1)}, bf16[32,640]{1,0:T(8,128)(2,1)S(1)}, u32[]{:S(2)}, u32[]{:S(2)}) collective-permute-start(bf16[32,640]{1,0:T(8,128)(2,1)} %get-tuple-element.22), channel_id=1, source_target_pairs={{0,0},{1,128},{128,1},{129,129},{2,2},{3,130},{130,3},{131,131},{4... | collective-permute-start | bytes 122888 | tf_op jit(solution)/shard_map/ppermute | solution.py:31
  12.6 1.9 collective-permute-start.3
  39.9 163.2 %all-gather.7.cloned.1.call-start = ((), (), s32[]{:S(2)}) async-start(), calls=%async_computation.1 | async-start | bytes 9732096 | tf_op jit(solution)/shard_map/all_gather | solution.py:366
  40.0 9.9 %collective-permute-start.4 = (bf16[512,512]{1,0:T(8,128)(2,1)}, bf16[512,512]{1,0:T(8,128)(2,1)S(1)}, u32[]{:S(2)}, u32[]{:S(2)}) collective-permute-start(bf16[512,512]{1,0:T(8,128)(2,1)} %param.10), channel_id=1, source_target_pairs={{0,2},{2,0},{128,130},{130,128},{1,3},{3,1},{129,131},{131,129},{4... | collective-permute-start | bytes 1572872 | tf_op jit(solution)/shard_map/ppermute | solution.py:22
  42.8 17.9 %collective-permute-start.5 = (bf16[512,512]{1,0:T(8,128)(2,1)}, bf16[512,512]{1,0:T(8,128)(2,1)S(1)}, u32[]{:S(2)}, u32[]{:S(2)}) collective-permute-start(bf16[512,512]{1,0:T(8,128)(2,1)} %param.10), channel_id=1, source_target_pairs={{0,128},{2,130},{128,0},{130,2},{1,129},{3,131},{129,1},{131,3},{4... | collective-permute-start | bytes 1572872 | tf_op jit(solution)/shard_map/ppermute | solution.py:22
  43.6 21.0 %collective-permute-start.6 = (bf16[512,512]{1,0:T(8,128)(2,1)}, bf16[512,512]{1,0:T(8,128)(2,1)S(1)}, u32[]{:S(2)}, u32[]{:S(2)}) collective-permute-start(bf16[512,512]{1,0:T(8,128)(2,1)} %param.10), channel_id=1, source_target_pairs={{0,130},{2,128},{128,2},{130,0},{1,131},{3,129},{129,3},{131,1},{4... | collective-permute-start | bytes 1572872 | tf_op jit(solution)/shard_map/ppermute | solution.py:22
  64.9 13.5 %copy-start = (bf16[4,512,512]{2,1,0:T(8,128)(2,1)}, bf16[4,512,512]{2,1,0:T(8,128)(2,1)S(1)}, u32[]{:S(2)}) copy-start(bf16[4,512,512]{2,1,0:T(8,128)(2,1)S(1)} %pad_maximum_fusion.mine_ref) | copy-start | bytes 6291460
  64.9 13.5 %collective-permute-start.7 = (bf16[4,512,512]{2,1,0:T(8,128)(2,1)S(1)}, bf16[4,512,512]{2,1,0:T(8,128)(2,1)}, u32[]{:S(2)}, u32[]{:S(2)}) collective-permute-start(bf16[4,512,512]{2,1,0:T(8,128)(2,1)S(1)} %pad_maximum_fusion.mine_ref), channel_id=1, source_target_pairs={{0,1},{1,0},{2,3},{3,2},{4,5},{5,4},{6,7},{7,6},{8,9},{9,8},{10,11... | collective-permute-start | bytes 6291464 | tf_op jit(solution)/shard_map/ppermute | solution.py:18
  70.4 7.1 %collective-permute-start = (bf16[32,2304]{1,0:T(8,128)(2,1)}, bf16[32,2304]{1,0:T(8,128)(2,1)S(1)}, u32[]{:S(2)}, u32[]{:S(2)}) collective-permute-start(bf16[32,2304]{1,0:T(8,128)(2,1)} %get-tuple-element.20), channel_id=1, source_target_pairs={{0,0},{1,128},{128,1},{129,129},{2,2},{3,130},{130,3},{131,131},{4... | collective-permute-start | bytes 442376 | tf_op jit(solution)/shard_map/ppermute | solution.py:31
  73.7 4.0 %collective-permute-start.1 = (bf16[32,2304]{1,0:T(8,128)(2,1)}, bf16[32,2304]{1,0:T(8,128)(2,1)S(1)}, u32[]{:S(2)}, u32[]{:S(2)}) collective-permute-start(bf16[32,2304]{1,0:T(8,128)(2,1)} %get-tuple-element.21), channel_id=1, source_target_pairs={{0,1},{1,129},{128,0},{129,128},{2,3},{3,131},{130,2},{131,130},{4... | collective-permute-start | bytes 442376 | tf_op jit(solution)/shard_map/ppermute | solution.py:31
  87.9 12.7 %collective-permute-start.8 = (bf16[2,512,128]{2,1,0:T(8,128)(2,1)}, bf16[2,512,128]{2,1,0:T(8,128)(2,1)S(1)}, u32[]{:S(2)}, u32[]{:S(2)}) collective-permute-start(bf16[2,512,128]{2,1,0:T(8,128)(2,1)} %bitcast.38), channel_id=1, source_target_pairs={{0,8},{4,12},{8,16},{12,20},{16,24},{20,28},{24,32},{28,36},{32,40... | collective-permute-start | bytes 786440 | tf_op jit(solution)/shard_map/ppermute | solution.py:371
  89.5 26.6 %collective-permute-start.9 = (bf16[2,512,128]{2,1,0:T(8,128)(2,1)}, bf16[2,512,128]{2,1,0:T(8,128)(2,1)S(1)}, u32[]{:S(2)}, u32[]{:S(2)}) collective-permute-start(bf16[2,512,128]{2,1,0:T(8,128)(2,1)} %bitcast.39), channel_id=1, source_target_pairs={{0,4},{4,8},{8,12},{12,16},{16,20},{20,24},{24,28},{28,32},{32,36}... | collective-permute-start | bytes 786440 | tf_op jit(solution)/shard_map/ppermute | solution.py:371
  117.2 5.8 %collective-permute-start.10 = (bf16[2,1536,128]{2,1,0:T(8,128)(2,1)S(1)}, bf16[2,1536,128]{2,1,0:T(8,128)(2,1)S(1)}, u32[]{:S(2)}, u32[]{:S(2)}) collective-permute-start(bf16[2,1536,128]{2,1,0:T(8,128)(2,1)S(1)} %pad_maximum_fusion.3), channel_id=1, source_target_pairs={{0,1},{1,0},{2,3},{3,2},{4,5},{5,4},{6,7},{7,6},{8,9},{9,8},{10,11... | collective-permute-start | bytes 2359304 | tf_op jit(solution)/shard_map/ppermute | solution.py:18
  118.9 4.1 %copy-start.3 = (bf16[1024,128]{1,0:T(8,128)(2,1)S(1)}, bf16[1024,128]{1,0:T(8,128)(2,1)}, u32[]{:S(2)}) copy-start(bf16[1024,128]{1,0:T(8,128)(2,1)} %shard_map.104) | copy-start | bytes 786436
  136.3 4.1 %copy-start.6 = (f32[512,1024]{1,0:T(8,128)S(1)}, f32[512,1024]{1,0:T(8,128)}, u32[]{:S(2)}) copy-start(f32[512,1024]{1,0:T(8,128)} %get-tuple-element.31) | copy-start | bytes 6291460
  136.3 4.1 %collective-permute-start.23 = (bf16[512,1024]{1,0:T(8,128)(2,1)}, bf16[512,1024]{1,0:T(8,128)(2,1)}, u32[]{:S(2)}, u32[]{:S(2)}) collective-permute-start(bf16[512,1024]{1,0:T(8,128)(2,1)} %get-tuple-element.32), channel_id=1, source_target_pairs={{0,1},{1,0},{2,3},{3,2},{4,5},{5,4},{6,7},{7,6},{8,9},{9,8},{10,11... | collective-permute-start | bytes 3145736 | tf_op jit(solution)/shard_map/ppermute | solution.py:18
  139.9 7.1 %collective-permute-start.11 = (bf16[512,1024]{1,0:T(8,128)(2,1)}, bf16[512,1024]{1,0:T(8,128)(2,1)S(1)}, u32[]{:S(2)}, u32[]{:S(2)}) collective-permute-start(bf16[512,1024]{1,0:T(8,128)(2,1)} %get-tuple-element.27), channel_id=1, source_target_pairs={{0,1},{1,0},{2,3},{3,2},{4,5},{5,4},{6,7},{7,6},{8,9},{9,8},{10,11... | collective-permute-start | bytes 3145736 | tf_op jit(solution)/shard_map/ppermute | solution.py:18
  140.4 6.6 %copy-start.5 = (f32[512,1024]{1,0:T(8,128)S(1)}, f32[512,1024]{1,0:T(8,128)}, u32[]{:S(2)}) copy-start(f32[512,1024]{1,0:T(8,128)} %get-tuple-element.26) | copy-start | bytes 6291460
  142.3 9.4 %collective-permute-start.24 = (bf16[256,512]{1,0:T(8,128)(2,1)S(1)}, bf16[256,512]{1,0:T(8,128)(2,1)S(1)}, u32[]{:S(2)}, u32[]{:S(2)}) collective-permute-start(bf16[256,512]{1,0:T(8,128)(2,1)S(1)} %get-tuple-element.54), channel_id=1, source_target_pairs={{0,2},{2,0},{128,130},{130,128},{1,3},{3,1},{129,131},{131,129},{4... | collective-permute-start | bytes 786440 | tf_op jit(solution)/shard_map/ppermute | solution.py:22
  145.0 13.6 %collective-permute-start.25 = (bf16[256,512]{1,0:T(8,128)(2,1)S(1)}, bf16[256,512]{1,0:T(8,128)(2,1)S(1)}, u32[]{:S(2)}, u32[]{:S(2)}) collective-permute-start(bf16[256,512]{1,0:T(8,128)(2,1)S(1)} %get-tuple-element.56), channel_id=1, source_target_pairs={{0,128},{2,130},{128,0},{130,2},{1,129},{3,131},{129,1},{131,3},{4... | collective-permute-start | bytes 786440 | tf_op jit(solution)/shard_map/ppermute | solution.py:22
  146.4 12.1 %collective-permute-start.26 = (bf16[256,512]{1,0:T(8,128)(2,1)S(1)}, bf16[256,512]{1,0:T(8,128)(2,1)S(1)}, u32[]{:S(2)}, u32[]{:S(2)}) collective-permute-start(bf16[256,512]{1,0:T(8,128)(2,1)S(1)} %get-tuple-element.55), channel_id=1, source_target_pairs={{0,130},{2,128},{128,2},{130,0},{1,131},{3,129},{129,3},{131,1},{4... | collective-permute-start | bytes 786440 | tf_op jit(solution)/shard_map/ppermute | solution.py:22
  147.7 15.3 %collective-permute-start.12 = (bf16[256,512]{1,0:T(8,128)(2,1)S(1)}, bf16[256,512]{1,0:T(8,128)(2,1)S(1)}, u32[]{:S(2)}, u32[]{:S(2)}) collective-permute-start(bf16[256,512]{1,0:T(8,128)(2,1)S(1)} %get-tuple-element.48), channel_id=1, source_target_pairs={{0,2},{2,0},{128,130},{130,128},{1,3},{3,1},{129,131},{131,129},{4... | collective-permute-start | bytes 786440 | tf_op jit(solution)/shard_map/ppermute | solution.py:22
  149.0 20.9 %collective-permute-start.13 = (bf16[256,512]{1,0:T(8,128)(2,1)S(1)}, bf16[256,512]{1,0:T(8,128)(2,1)S(1)}, u32[]{:S(2)}, u32[]{:S(2)}) collective-permute-start(bf16[256,512]{1,0:T(8,128)(2,1)S(1)} %get-tuple-element.50), channel_id=1, source_target_pairs={{0,128},{2,130},{128,0},{130,2},{1,129},{3,131},{129,1},{131,3},{4... | collective-permute-start | bytes 786440 | tf_op jit(solution)/shard_map/ppermute | solution.py:22
  151.7 18.1 %collective-permute-start.14 = (bf16[256,512]{1,0:T(8,128)(2,1)S(1)}, bf16[256,512]{1,0:T(8,128)(2,1)S(1)}, u32[]{:S(2)}, u32[]{:S(2)}) collective-permute-start(bf16[256,512]{1,0:T(8,128)(2,1)S(1)} %get-tuple-element.49), channel_id=1, source_target_pairs={{0,130},{2,128},{128,2},{130,0},{1,131},{3,129},{129,3},{131,1},{4... | collective-permute-start | bytes 786440 | tf_op jit(solution)/shard_map/ppermute | solution.py:22
  170.2 8.7 %collective-permute-start.15 = (bf16[256,512]{1,0:T(8,128)(2,1)S(1)}, bf16[256,512]{1,0:T(8,128)(2,1)S(1)}, u32[]{:S(2)}, u32[]{:S(2)}) collective-permute-start(bf16[256,512]{1,0:T(8,128)(2,1)S(1)} %get-tuple-element.57), channel_id=1, source_target_pairs={{0,2},{2,0},{128,130},{130,128},{1,3},{3,1},{129,131},{131,129},{4... | collective-permute-start | bytes 786440 | tf_op jit(solution)/shard_map/ppermute | solution.py:22
  172.2 13.2 %collective-permute-start.16 = (bf16[256,512]{1,0:T(8,128)(2,1)S(1)}, bf16[256,512]{1,0:T(8,128)(2,1)S(1)}, u32[]{:S(2)}, u32[]{:S(2)}) collective-permute-start(bf16[256,512]{1,0:T(8,128)(2,1)S(1)} %get-tuple-element.57), channel_id=1, source_target_pairs={{0,128},{2,130},{128,0},{130,2},{1,129},{3,131},{129,1},{131,3},{4... | collective-permute-start | bytes 786440 | tf_op jit(solution)/shard_map/ppermute | solution.py:22
  173.6 12.2 %collective-permute-start.17 = (bf16[256,512]{1,0:T(8,128)(2,1)S(1)}, bf16[256,512]{1,0:T(8,128)(2,1)S(1)}, u32[]{:S(2)}, u32[]{:S(2)}) collective-permute-start(bf16[256,512]{1,0:T(8,128)(2,1)S(1)} %get-tuple-element.57), channel_id=1, source_target_pairs={{0,130},{2,128},{128,2},{130,0},{1,131},{3,129},{129,3},{131,1},{4... | collective-permute-start | bytes 786440 | tf_op jit(solution)/shard_map/ppermute | solution.py:22
  185.9 17.2 %copy-start.1 = (bf16[4,256,512]{2,1,0:T(8,128)(2,1)}, bf16[4,256,512]{2,1,0:T(8,128)(2,1)S(1)}, u32[]{:S(2)}) copy-start(bf16[4,256,512]{2,1,0:T(8,128)(2,1)S(1)} %pad_maximum_fusion.1.mine_ref) | copy-start | bytes 3145732
  185.9 17.1 %collective-permute-start.18 = (bf16[4,256,512]{2,1,0:T(8,128)(2,1)S(1)}, bf16[4,256,512]{2,1,0:T(8,128)(2,1)}, u32[]{:S(2)}, u32[]{:S(2)}) collective-permute-start(bf16[4,256,512]{2,1,0:T(8,128)(2,1)S(1)} %pad_maximum_fusion.1.mine_ref), channel_id=1, source_target_pairs={{0,1},{1,0},{2,3},{3,2},{4,5},{5,4},{6,7},{7,6},{8,9},{9,8},{10,11... | collective-permute-start | bytes 3145736 | tf_op jit(solution)/shard_map/ppermute | solution.py:18
  186.7 9.3 %collective-permute-start.27 = (bf16[256,512]{1,0:T(8,128)(2,1)S(1)}, bf16[256,512]{1,0:T(8,128)(2,1)S(1)}, u32[]{:S(2)}, u32[]{:S(2)}) collective-permute-start(bf16[256,512]{1,0:T(8,128)(2,1)S(1)} %get-tuple-element.58), channel_id=1, source_target_pairs={{0,2},{2,0},{128,130},{130,128},{1,3},{3,1},{129,131},{131,129},{4... | collective-permute-start | bytes 786440 | tf_op jit(solution)/shard_map/ppermute | solution.py:22
  188.5 13.1 %collective-permute-start.28 = (bf16[256,512]{1,0:T(8,128)(2,1)S(1)}, bf16[256,512]{1,0:T(8,128)(2,1)S(1)}, u32[]{:S(2)}, u32[]{:S(2)}) collective-permute-start(bf16[256,512]{1,0:T(8,128)(2,1)S(1)} %get-tuple-element.58), channel_id=1, source_target_pairs={{0,128},{2,130},{128,0},{130,2},{1,129},{3,131},{129,1},{131,3},{4... | collective-permute-start | bytes 786440 | tf_op jit(solution)/shard_map/ppermute | solution.py:22
  189.7 12.4 %collective-permute-start.29 = (bf16[256,512]{1,0:T(8,128)(2,1)S(1)}, bf16[256,512]{1,0:T(8,128)(2,1)S(1)}, u32[]{:S(2)}, u32[]{:S(2)}) collective-permute-start(bf16[256,512]{1,0:T(8,128)(2,1)S(1)} %get-tuple-element.58), channel_id=1, source_target_pairs={{0,130},{2,128},{128,2},{130,0},{1,131},{3,129},{129,3},{131,1},{4... | collective-permute-start | bytes 786440 | tf_op jit(solution)/shard_map/ppermute | solution.py:22
  202.2 14.7 %copy-start.2 = (bf16[4,256,512]{2,1,0:T(8,128)(2,1)}, bf16[4,256,512]{2,1,0:T(8,128)(2,1)S(1)}, u32[]{:S(2)}) copy-start(bf16[4,256,512]{2,1,0:T(8,128)(2,1)S(1)} %pad_maximum_fusion.2.mine_ref) | copy-start | bytes 3145732
  202.2 14.7 %collective-permute-start.30 = (bf16[4,256,512]{2,1,0:T(8,128)(2,1)S(1)}, bf16[4,256,512]{2,1,0:T(8,128)(2,1)}, u32[]{:S(2)}, u32[]{:S(2)}) collective-permute-start(bf16[4,256,512]{2,1,0:T(8,128)(2,1)S(1)} %pad_maximum_fusion.2.mine_ref), channel_id=1, source_target_pairs={{0,1},{1,0},{2,3},{3,2},{4,5},{5,4},{6,7},{7,6},{8,9},{9,8},{10,11... | collective-permute-start | bytes 3145736 | tf_op jit(solution)/shard_map/ppermute | solution.py:18
  216.9 14.4 %collective-permute-start.19 = (bf16[512,1024]{1,0:T(8,128)(2,1)}, bf16[512,1024]{1,0:T(8,128)(2,1)S(1)}, u32[]{:S(2)}, u32[]{:S(2)}) collective-permute-start(bf16[512,1024]{1,0:T(8,128)(2,1)} %get-tuple-element.30), channel_id=1, source_target_pairs={{0,1},{1,0},{2,3},{3,2},{4,5},{5,4},{6,7},{7,6},{8,9},{9,8},{10,11... | collective-permute-start | bytes 3145736 | tf_op jit(solution)/shard_map/ppermute | solution.py:18
  230.8 6.3 %collective-permute-start.31 = (bf16[512,1024]{1,0:T(8,128)(2,1)}, bf16[512,1024]{1,0:T(8,128)(2,1)S(1)}, u32[]{:S(2)}, u32[]{:S(2)}) collective-permute-start(bf16[512,1024]{1,0:T(8,128)(2,1)} %get-tuple-element.34), channel_id=1, source_target_pairs={{0,1},{1,0},{2,3},{3,2},{4,5},{5,4},{6,7},{7,6},{8,9},{9,8},{10,11... | collective-permute-start | bytes 3145736 | tf_op jit(solution)/shard_map/ppermute | solution.py:18
  231.3 5.8 %copy-start.4 = (f32[512,1024]{1,0:T(8,128)S(1)}, f32[512,1024]{1,0:T(8,128)}, u32[]{:S(2)}) copy-start(f32[512,1024]{1,0:T(8,128)} %get-tuple-element.33) | copy-start | bytes 6291460
  233.5 9.4 %collective-permute-start.20 = (bf16[256,512]{1,0:T(8,128)(2,1)S(1)}, bf16[256,512]{1,0:T(8,128)(2,1)S(1)}, u32[]{:S(2)}, u32[]{:S(2)}) collective-permute-start(bf16[256,512]{1,0:T(8,128)(2,1)S(1)} %get-tuple-element.45), channel_id=1, source_target_pairs={{0,2},{2,0},{128,130},{130,128},{1,3},{3,1},{129,131},{131,129},{4... | collective-permute-start | bytes 786440 | tf_op jit(solution)/shard_map/ppermute | solution.py:22
  235.4 13.2 %collective-permute-start.21 = (bf16[256,512]{1,0:T(8,128)(2,1)S(1)}, bf16[256,512]{1,0:T(8,128)(2,1)S(1)}, u32[]{:S(2)}, u32[]{:S(2)}) collective-permute-start(bf16[256,512]{1,0:T(8,128)(2,1)S(1)} %get-tuple-element.47), channel_id=1, source_target_pairs={{0,128},{2,130},{128,0},{130,2},{1,129},{3,131},{129,1},{131,3},{4... | collective-permute-start | bytes 786440 | tf_op jit(solution)/shard_map/ppermute | solution.py:22
  236.5 12.8 %collective-permute-start.22 = (bf16[256,512]{1,0:T(8,128)(2,1)S(1)}, bf16[256,512]{1,0:T(8,128)(2,1)S(1)}, u32[]{:S(2)}, u32[]{:S(2)}) collective-permute-start(bf16[256,512]{1,0:T(8,128)(2,1)S(1)} %get-tuple-element.46), channel_id=1, source_target_pairs={{0,130},{2,128},{128,2},{130,0},{1,131},{3,129},{129,3},{131,1},{4... | collective-permute-start | bytes 786440 | tf_op jit(solution)/shard_map/ppermute | solution.py:22
  237.7 16.5 %collective-permute-start.32 = (bf16[256,512]{1,0:T(8,128)(2,1)S(1)}, bf16[256,512]{1,0:T(8,128)(2,1)S(1)}, u32[]{:S(2)}, u32[]{:S(2)}) collective-permute-start(bf16[256,512]{1,0:T(8,128)(2,1)S(1)} %get-tuple-element.51), channel_id=1, source_target_pairs={{0,2},{2,0},{128,130},{130,128},{1,3},{3,1},{129,131},{131,129},{4... | collective-permute-start | bytes 786440 | tf_op jit(solution)/shard_map/ppermute | solution.py:22
  239.3 20.5 %collective-permute-start.33 = (bf16[256,512]{1,0:T(8,128)(2,1)S(1)}, bf16[256,512]{1,0:T(8,128)(2,1)S(1)}, u32[]{:S(2)}, u32[]{:S(2)}) collective-permute-start(bf16[256,512]{1,0:T(8,128)(2,1)S(1)} %get-tuple-element.53), channel_id=1, source_target_pairs={{0,128},{2,130},{128,0},{130,2},{1,129},{3,131},{129,1},{131,3},{4... | collective-permute-start | bytes 786440 | tf_op jit(solution)/shard_map/ppermute | solution.py:22
  242.9 17.3 %collective-permute-start.34 = (bf16[256,512]{1,0:T(8,128)(2,1)S(1)}, bf16[256,512]{1,0:T(8,128)(2,1)S(1)}, u32[]{:S(2)}, u32[]{:S(2)}) collective-permute-start(bf16[256,512]{1,0:T(8,128)(2,1)S(1)} %get-tuple-element.52), channel_id=1, source_target_pairs={{0,130},{2,128},{128,2},{130,0},{1,131},{3,129},{129,3},{131,1},{4... | collective-permute-start | bytes 786440 | tf_op jit(solution)/shard_map/ppermute | solution.py:22
Sparse Core Ops, SparseCore 0:
  40.0 43.1 all-gather.4
  85.8 103.1 all-gather.6

commit v3 on v2

--- a/solution.py
+++ b/solution.py
@@ -12,6 +12,13 @@
 FEATURES = ("yh", "c")
 PLANE = ("x", "z")
 PARTS = 2
+
+
+def spread(value, axis):
+    length = lax.axis_size(axis)
+    return lax.all_to_all(
+        jnp.broadcast_to(value[None], (length, *value.shape)), axis, 0, 0, tiled=True
+    )
 
 
 def other_core(value):
@@ -102,64 +109,71 @@
     steps = width // step
 
     def kernel(
-        me_ref, mine_ref, theirs_ref, gain_ref, gate_ref, up_ref, down_ref, near_ref, away_ref,
-        normed, total,
+        me_ref, mine_ref, theirs_ref, gain_ref, gate_ref, up_ref, all_ref, near_ref, away_ref,
+        normed, hidden, down_ref, arrived,
     ):
         j = pl.program_id(0)
+        fetch = pltpu.make_async_copy(all_ref.at[:, :, :, 2 * width :], down_ref, arrived)
 
         @pl.when(j == 0)
         def _():
+            fetch.start()
             for run in range(2):
                 store_normed(
                     me_ref, mine_ref, theirs_ref, gain_ref, normed, run, run * rows
                 )
 
-        gate = up = 0.0
-        for run in range(runs):
-            x = normed[:, run * chips * r : (run + 1) * chips * r]
-            gate_rows = gate_ref[:, run].reshape(chips * r, step)
-            gate = gate + jnp.dot(x, gate_rows, preferred_element_type=jnp.float32)
-            up_rows = up_ref[:, run].reshape(chips * r, step)
-            up = up + jnp.dot(x, up_rows, preferred_element_type=jnp.float32)
-        hidden = (gate / (1.0 + jnp.exp(-gate)) * up).astype(jnp.bfloat16)
-        for place, flip in enumerate((1, 3, 0, 2)):
-            term = lax.dot_general(
-                hidden,
-                feature_rows(down_ref, me_ref[0] ^ flip),
-                (((1,), (1,)), ((), ())),
-                preferred_element_type=jnp.float32,
-            )
-            out = total if place < 2 else near_ref
-            cols = slice(place % 2 * f, (place % 2 + 1) * f)
-
-            @pl.when(j == 0)
-            def _():
-                out[:, cols] = term
-
-            @pl.when(j > 0)
-            def _():
-                out[:, cols] += term
-
-        @pl.when(j == steps - 1)
+        @pl.when(j < steps)
         def _():
-            away_ref[...] = total[...].astype(jnp.bfloat16)
+            gate = up = 0.0
+            for run in range(runs):
+                x = normed[:, run * chips * r : (run + 1) * chips * r]
+                gate_rows = gate_ref[:, run].reshape(chips * r, step)
+                gate = gate + jnp.dot(x, gate_rows, preferred_element_type=jnp.float32)
+                up_rows = up_ref[:, run].reshape(chips * r, step)
+                up = up + jnp.dot(x, up_rows, preferred_element_type=jnp.float32)
+            hidden[j] = (gate / (1.0 + jnp.exp(-gate)) * up).astype(jnp.bfloat16)
+
+        @pl.when(j == steps)
+        def _():
+            fetch.wait()
+
+        @pl.when(j >= steps)
+        def _():
+            left = jnp.concatenate([hidden[i] for i in range(steps)], axis=1)
+            for out, flip in ((away_ref, 2 * (j - steps) + 1), (near_ref, 2 * (j - steps))):
+                term = lax.dot_general(
+                    left,
+                    feature_rows(down_ref, me_ref[0] ^ flip),
+                    (((1,), (1,)), ((), ())),
+                    preferred_element_type=jnp.float32,
+                )
+                out[...] = term.astype(out.dtype)
 
     def whole(shape):
         return pl.BlockSpec(shape, lambda j, me: (0,) * len(shape))
 
     def weight(part):
-        return pl.BlockSpec((chips, runs, r, step), lambda j, me: (0, 0, 0, part * steps + j))
+        return pl.BlockSpec(
+            (chips, runs, r, step),
+            lambda j, me: (0, 0, 0, part * steps + jnp.minimum(j, steps - 1)),
+        )
 
     shape = (2 * rows, 2 * f)
     return call(
         kernel,
-        (steps,),
+        (steps + 2,),
         1,
         [whole(mine.shape), whole(mine.shape), whole((1, 4 * f))]
-        + [weight(part) for part in range(3)],
-        [whole(shape), whole(shape)],
+        + [weight(0), weight(1), pl.BlockSpec(memory_space=pl.ANY)],
+        [pl.BlockSpec((2 * rows, f), lambda j, me: (0, jnp.maximum(j - steps, 0)))] * 2,
         [jax.ShapeDtypeStruct(shape, jnp.float32), jax.ShapeDtypeStruct(shape, jnp.bfloat16)],
-        [pltpu.VMEM((2 * rows, 4 * f), jnp.bfloat16), pltpu.VMEM(shape, jnp.float32)],
+        [
+            pltpu.VMEM((2 * rows, 4 * f), jnp.bfloat16),
+            pltpu.VMEM((steps, 2 * rows, step), jnp.bfloat16),
+            pltpu.VMEM((chips, runs, r, width), jnp.bfloat16),
+            pltpu.SemaphoreType.DMA,
+        ],
         flops=2 * 2 * rows * width * (2 * d + 4 * f),
         moved=2 * weights.size + 16 * rows * f * 2,
     )(me, mine, theirs, gain[None], weights, weights, weights)
@@ -200,33 +214,32 @@
     return weights_ref[pl.ds(at, half), lax.div(block, 2)].reshape(half * r, k)
 
 
-def head_terms(me, attended, weights, part):
-    rows, width = attended.shape[1] // PARTS, attended.shape[2]
+def head_terms(me, attended, weights):
+    rows, width = attended.shape[1:]
     f = weights.shape[0] * weights.shape[1] * weights.shape[2] // 4
 
     def kernel(me_ref, left_ref, weights_ref, near_ref, away_ref):
         left = left_ref[...].reshape(2 * rows, width)
-        for place, flip in enumerate((1, 3, 0, 2)):
+        at = 2 * pl.program_id(0)
+        for out, flip in ((away_ref, at + 1), (near_ref, at)):
             term = lax.dot_general(
                 left,
                 feature_rows(weights_ref, me_ref[0] ^ flip),
                 (((1,), (1,)), ((), ())),
                 preferred_element_type=jnp.float32,
             )
-            out = away_ref if place < 2 else near_ref
-            out[:, place % 2 * f : (place % 2 + 1) * f] = term.astype(out.dtype)
+            out[...] = term.astype(out.dtype)
 
     shape = (2 * rows, 2 * f)
-    whole = pl.BlockSpec(shape, lambda i, me: (0, 0))
-    return call(
-        kernel,
-        (1,),
+    return call(
+        kernel,
+        (2,),
         1,
         [
-            pl.BlockSpec((2, rows, width), lambda i, me: (0, part, 0)),
-            pl.BlockSpec((*weights.shape[:3], width), lambda i, me: (0, 0, 0, 1)),
+            pl.BlockSpec((2, rows, width), lambda i, me: (0, 0, 0)),
+            pl.BlockSpec((*weights.shape[:3], width), lambda i, me: (0, 0, 0, 0)),
         ],
-        [whole, whole],
+        [pl.BlockSpec((2 * rows, f), lambda i, me: (0, i))] * 2,
         [jax.ShapeDtypeStruct(shape, jnp.float32), jax.ShapeDtypeStruct(shape, jnp.bfloat16)],
         flops=4 * rows * 4 * f * width,
         moved=8 * f * width + 24 * rows * f,
@@ -243,23 +256,24 @@
         (both[rows:, f:], 3),
     )
     for value, flip in sent:
-        total = total + column_partner(value.astype(jnp.bfloat16), flip).astype(jnp.float32)
+        came = column_partner(value.astype(jnp.bfloat16), flip)
+        total = total + came.astype(jnp.float32)
     return total
 
 
-def window_attention(queries, keys, values, first_key):
+def window_attention(queries, keys, values, first_key, part):
     rows, width = queries.shape[1:]
     span = keys.shape[1]
     count = width // HEAD_DIM
-    step = min(256, rows)
+    step = rows // PARTS
     seen = WINDOW + step
+    start = part * step + span - rows - WINDOW
     scale = HEAD_DIM ** (-0.5)
 
     def kernel(first_ref, q_ref, k_ref, v_ref, out_ref):
-        run, tile = pl.program_id(0), pl.program_id(1)
-        start = pl.multiple_of(tile * step + span - rows - WINDOW, step)
-        k = k_ref[0, pl.ds(start, seen), :]
-        v = v_ref[0, pl.ds(start, seen), :]
+        run = pl.program_id(0)
+        k = k_ref[0, start : start + seen, :]
+        v = v_ref[0, start : start + seen, :]
         query_pos = lax.broadcasted_iota(jnp.int32, (step, seen), 0)
         key_pos = lax.broadcasted_iota(jnp.int32, (step, seen), 1)
         distance = query_pos + WINDOW - key_pos
@@ -276,17 +290,16 @@
             mixed = jnp.dot(raised.astype(jnp.bfloat16), v, preferred_element_type=jnp.float32)
             out_ref[0, :, cols] = (mixed / total).astype(jnp.bfloat16)
 
-    whole = pl.BlockSpec((1, span, HEAD_DIM), lambda run, tile, first: (run, 0, 0))
-    part = pl.BlockSpec((1, step, width), lambda run, tile, first: (run, tile, 0))
-    return call(
-        kernel,
-        (2, rows // step),
+    whole = pl.BlockSpec((1, span, HEAD_DIM), lambda run, first: (run, 0, 0))
+    return call(
+        kernel,
+        (2,),
         1,
-        [part, whole, whole],
-        part,
-        jax.ShapeDtypeStruct(queries.shape, jnp.bfloat16),
-        flops=2 * rows * width * seen * 4,
-        moved=2 * (2 * queries.size + keys.size + values.size),
+        [pl.BlockSpec((1, step, width), lambda run, first: (run, part, 0)), whole, whole],
+        pl.BlockSpec((1, step, width), lambda run, first: (run, 0, 0)),
+        jax.ShapeDtypeStruct((2, step, width), jnp.bfloat16),
+        flops=2 * step * width * seen * 4,
+        moved=2 * (2 * queries.size // PARTS + keys.size + values.size),
     )(first_key, queries, keys, values)
 
 
@@ -346,14 +359,16 @@
             [
                 [
                     (w_query, h * heads, heads),
+                    ((w_key, w_value)[h], 0, kv_width),
                     (out_t, h * heads, heads),
-                    ((w_key, w_value)[h], 0, kv_width),
                 ]
                 for h in range(2)
             ],
         )
     )
-    attn_full = lax.all_gather(attn_rows[None], "z", axis=0, tiled=True)
+    split = heads + kv_width
+    attn_full = spread(attn_rows, "z")
+    attn_full, out_full = attn_full[..., :split], attn_full[..., split:]
     mlp_rows = column_rows(
         packed(
             parity,
@@ -364,7 +379,9 @@
     normed = normed_rows(me, *column_blocks(tokens), attn_gain)
     mlp_rows, attn_full, normed = lax.optimization_barrier((mlp_rows, attn_full, normed))
     mlp_full = lax.all_gather(mlp_rows[None], PLANE, axis=0, tiled=True)
-    fresh = projected(normed, attn_full, 2 * heads, kv_width).reshape(2, rows, kv_width)
+    out_full = spread(out_full, "x")
+    out_full = out_full.reshape(-1, *out_full.shape[2:])
+    fresh = projected(normed, attn_full, heads, kv_width).reshape(2, rows, kv_width)
     reach = -(-WINDOW // rows)
     context = [fresh]
     for step in range(1, reach + 1):
@@ -376,15 +393,19 @@
     queries = projected(normed, attn_full, 0, heads).reshape(2, rows, heads)
     runs = jnp.stack([yl, 1 - yl])
     first_key = ((runs * plane + place - reach) * rows).astype(jnp.int32)
-    attended = window_attention(queries, keys, values, first_key)
     part = rows // PARTS
     outputs = []
-    for at in range(0, rows, part):
-        attn_share = column_sum(*head_terms(me, attended, attn_full, at // part))
-        stream = tokens[at : at + part].astype(jnp.float32) + attn_share
-        stream = stream.astype(jnp.bfloat16)
-        terms = unit_terms(me, *column_blocks(stream), mlp_gain, mlp_full)
-        outputs.append((stream.astype(jnp.float32) + column_sum(*terms)).astype(jnp.bfloat16))
+    for i in range(PARTS):
+        attended = window_attention(queries, keys, values, first_key, i)
+        attn_share = column_sum(*head_terms(me, attended, out_full))
+        residual = tokens[i * part : (i + 1) * part]
+        if i > 0:
+            residual, stream = lax.optimization_barrier((residual, stream))
+        stream = (residual.astype(jnp.float32) + attn_share).astype(jnp.bfloat16)
+        blocks = column_blocks(stream)
+        terms = unit_terms(me, *blocks, mlp_gain, mlp_full)
+        mlp_share = column_sum(*terms)
+        outputs.append((stream.astype(jnp.float32) + mlp_share).astype(jnp.bfloat16))
     return jnp.concatenate(outputs, axis=0)
 
 

time: 268 us -> 261 us (0.974); the launches traced: 268 us -> 258 us
  blocking collectives: 25.3 us -> 0 us
  starting transfers between devices: 49.3 us -> 63.1 us
  local copies, waits for them, and re-layouts: 0.29 us -> 4.96 us
  other arithmetic: 11.1 us -> 15.4 us
  Pallas kernels: 60.1 us -> 56.1 us
  waiting for transfers between devices: 108 us -> 105 us
    all_gather x1 -> x0, blocking collectives: 25.3 us -> none  [per_device(): attn_full = lax.all_gather(attn_rows[None], 'z', axis=0, tiled=True)]
    all_to_all x0 -> x2, waiting for transfers between devices: none -> 18.8 us  [spread(): lax.all_to_all(jnp.broadcast_to(value[None], (length, *value.shape)), axi...]
    ppermute x21, waiting for transfers between devices: 77.1 us -> 64.4 us  [column_partner(): return lax.ppermute(value, ('yl', 'yh'), [(i, i ^ flip) for i in range(4)])]
    all_to_all x0 -> x2, starting transfers between devices: none -> 11.7 us  [spread(): lax.all_to_all(jnp.broadcast_to(value[None], (length, *value.shape)), axi...]
    ppermute x2, waiting for transfers between devices: 25.5 us -> 14.8 us  [per_device(): lax.ppermute(fresh, PLANE, [(i, (i + step) % plane) for i in range(plane)])]
    ppermute x8, starting transfers between devices: 7.24 us -> 14.2 us  [other_core(): return lax.ppermute(value, 'c', [(0, 1), (1, 0)])]
    ppermute x21, starting transfers between devices: 31.3 us -> 26.5 us  [column_partner(): return lax.ppermute(value, ('yl', 'yh'), [(i, i ^ flip) for i in range(4)])]
    pallas_call x5 -> x6, Pallas kernels: 43.2 us -> 39.2 us  [the longest x2 21.6 us: unit_terms(): call(kernel, (steps + 2,), 1, [whole(mine.shape), whole(mine.shape), whol...]
  transfers between devices with their start and end apart: 37 -> 39, of which waited for: 24 -> 24; matrix products, arithmetic and copies ran while one was open for 4% -> 6% of each run, Pallas kernels for 22% -> 21%
where the time goes in v3:
time: 261 us; the launch traced here: 258 us
  waiting for transfers between devices  105 us (40%)
  starting transfers between devices  63.1 us (24%)
  Pallas kernels  56.1 us (21%)
  other arithmetic  15.4 us (6%)
  between operations  13.7 us (5%)
  local copies, waits for them, and re-layouts  4.96 us (2%)
    ppermute x21, waiting for transfers between devices, column_partner(): return lax.ppermute(value, ('yl', 'yh'), [(i, i ^ flip) for i in range(4)])  64.4 us
    ppermute x21, starting transfers between devices, column_partner(): return lax.ppermute(value, ('yl', 'yh'), [(i, i ^ flip) for i in range(4)])  26.5 us
    pallas_call x2, Pallas kernels, unit_terms(): call(kernel, (steps + 2,), 1, [whole(mine.shape), whole(mine.shape), whol...  21.6 us
    all_to_all x2, waiting for transfers between devices, spread(): lax.all_to_all(jnp.broadcast_to(value[None], (length, *value.shape)), axi...  18.8 us
    ppermute x2, waiting for transfers between devices, per_device(): lax.ppermute(fresh, PLANE, [(i, (i + step) % plane) for i in range(plane)])  14.8 us
    ppermute x8, starting transfers between devices, other_core(): return lax.ppermute(value, 'c', [(0, 1), (1, 0)])  14.2 us
    all_to_all x2, starting transfers between devices, spread(): lax.all_to_all(jnp.broadcast_to(value[None], (length, *value.shape)), axi...  11.7 us
    pallas_call x2, Pallas kernels, window_attention(): call(kernel, (2,), 1, [pl.BlockSpec((1, step, width), lambda run, first:...  10.8 us
  transfers between devices with their start and end apart: 39, of which 24 were waited for; matrix products, arithmetic and copies ran while one was open for 6% of the time, Pallas kernels for 21%

profile of v3, /device:TPU:1, one launch (start us, length us, event | category | flops | bytes accessed | tf_op | source)
XLA Modules:
  0.0 257.9 jit_solution(2522601369993886029)
XLA Ops:
  8.1 4.6 %collective-permute-start.2 = (bf16[32,640]{1,0:T(8,128)(2,1)}, bf16[32,640]{1,0:T(8,128)(2,1)S(1)}, u32[]{:S(2)}, u32[]{:S(2)}) collective-permute-start(bf16[32,640]{1,0:T(8,128)(2,1)} %get-tuple-element.23), channel_id=1, source_target_pairs={{0,0},{1,128},{128,1},{129,129},{2,2},{3,130},{130,3},{131,131},{4... | collective-permute-start | bytes 122888 | tf_op jit(solution)/shard_map/ppermute | solution.py:38
  15.5 8.2 %all-to-all-start = ((bf16[8,2,32,640]{3,2,1,0:T(8,128)(2,1)}), bf16[8,2,32,640]{3,2,1,0:T(8,128)(2,1)S(1)}, u32[]{:S(2)}, u32[]{:S(2)}) async-start(bf16[8,2,32,640]{3,2,1,0:T(8,128)(2,1)} %broadcast_in_dim.10), calls=%async_computation | async-start | bytes 1310720 | tf_op jit(solution)/shard_map/all_to_all | solution.py:19
  23.8 3.1 %collective-permute-start.6 = (bf16[512,512]{1,0:T(8,128)(2,1)S(1)}, bf16[512,512]{1,0:T(8,128)(2,1)S(1)}, u32[]{:S(2)}, u32[]{:S(2)}) collective-permute-start(bf16[512,512]{1,0:T(8,128)(2,1)S(1)} %copy-done.7), channel_id=1, source_target_pairs={{0,130},{2,128},{128,2},{130,0},{1,131},{3,129},{129,3},{131,1},{4... | collective-permute-start | bytes 1572872 | tf_op jit(solution)/shard_map/ppermute | solution.py:29
  28.2 16.3 %all-to-all-done = bf16[8,2,32,640]{3,2,1,0:T(8,128)(2,1)S(1)} async-done(((bf16[8,2,32,640]{3,2,1,0:T(8,128)(2,1)}), bf16[8,2,32,640]{3,2,1,0:T(8,128)(2,1)S(1)}, u32[]{:S(2)}, u32[]{:S(2)}) %all-to-all-start) | async-done | bytes 655392 | tf_op jit(solution)/shard_map/all_to_all | solution.py:19
  45.4 4.8 %collective-permute-done.4 = bf16[512,512]{1,0:T(8,128)(2,1)S(1)} collective-permute-done((bf16[512,512]{1,0:T(8,128)(2,1)S(1)}, bf16[512,512]{1,0:T(8,128)(2,1)S(1)}, u32[]{:S(2)}, u32[]{:S(2)}) %collective-permute-start.4) | collective-permute-done | bytes 524320 | tf_op jit(solution)/shard_map/ppermute | solution.py:29
  52.6 2.2 collective-permute-start.7
  54.8 2.0 shard_map.100
  56.8 2.3 collective-permute-start
  59.2 4.6 %collective-permute-done = bf16[32,2304]{1,0:T(8,128)(2,1)S(1)} collective-permute-done((bf16[32,2304]{1,0:T(8,128)(2,1)}, bf16[32,2304]{1,0:T(8,128)(2,1)S(1)}, u32[]{:S(2)}, u32[]{:S(2)}) %collective-permute-start) | collective-permute-done | bytes 147488 | tf_op jit(solution)/shard_map/ppermute | solution.py:38
  65.5 5.7 %shard_map.102.x_ref = bf16[1024,2048]{1,0:T(8,128)(2,1)} custom-call(s32[1]{0:T(128)} %bitcast.me_ref, bf16[4,512,512]{2,1,0:T(8,128)(2,1)} %copy-done, bf16[4,512,512]{2,1,0:T(8,128)(2,1)} %collective-permute-done.7.theirs_ref, f32[1,2048]{1,0:T(1,128)} %bitcast.63), custom_call_target="tpu_custom_call" | custom-call | flops 26214400 | bytes 8388608 | tf_op jit(solution)/shard_map/pallas_call | solution.py:91
  71.2 3.8 %shard_map.104 = bf16[1024,128]{1,0:T(8,128)(2,1)} custom-call(bf16[1024,2048]{1,0:T(8,128)(2,1)} %shard_map.102.x_ref, bf16[32,2,32,384]{3,2,1,0:T(8,128)(2,1)} %all-gather.4.cloned.1.call-done.w_ref), custom_call_target="tpu_custom_call" | custom-call | flops 536870912 | bytes 4980736 | tf_op jit(solution)/shard_map/pallas_call | solution.py:195
  76.4 2.1 collective-permute-start.8
  78.6 6.0 %collective-permute-done.9 = bf16[2,512,128]{2,1,0:T(8,128)(2,1)S(1)} collective-permute-done((bf16[2,512,128]{2,1,0:T(8,128)(2,1)}, bf16[2,512,128]{2,1,0:T(8,128)(2,1)S(1)}, u32[]{:S(2)}, u32[]{:S(2)}) %collective-permute-start.9) | collective-permute-done | bytes 262176 | tf_op jit(solution)/shard_map/ppermute | solution.py:388
  84.6 8.9 %collective-permute-done.8 = bf16[2,512,128]{2,1,0:T(8,128)(2,1)S(1)} collective-permute-done((bf16[2,512,128]{2,1,0:T(8,128)(2,1)}, bf16[2,512,128]{2,1,0:T(8,128)(2,1)S(1)}, u32[]{:S(2)}, u32[]{:S(2)}) %collective-permute-start.8) | collective-permute-done | bytes 262176 | tf_op jit(solution)/shard_map/ppermute | solution.py:388
  93.5 1.9 pad_maximum_fusion.3
  95.4 6.0 %collective-permute-start.10 = (bf16[2,1536,128]{2,1,0:T(8,128)(2,1)}, bf16[2,1536,128]{2,1,0:T(8,128)(2,1)}, u32[]{:S(2)}, u32[]{:S(2)}) collective-permute-start(bf16[2,1536,128]{2,1,0:T(8,128)(2,1)} %pad_maximum_fusion.3), channel_id=1, source_target_pairs={{0,1},{1,0},{2,3},{3,2},{4,5},{5,4},{6,7},{7,6},{8,9},{9,8},{10,11... | collective-permute-start | bytes 2359304 | tf_op jit(solution)/shard_map/ppermute | solution.py:25
  102.5 3.5 %all-to-all-start.1 = ((bf16[4,8,2,32,256]{4,3,2,1,0:T(8,128)(2,1)}), bf16[4,8,2,32,256]{4,3,2,1,0:T(8,128)(2,1)S(1)}, u32[]{:S(2)}, u32[]{:S(2)}) async-start(bf16[4,8,2,32,256]{4,3,2,1,0:T(8,128)(2,1)} %broadcast_in_dim.24), calls=%async_computation.1 | async-start | bytes 2097152 | tf_op jit(solution)/shard_map/all_to_all | solution.py:19
  106.7 4.0 %shard_map.103 = bf16[1024,256]{1,0:T(8,128)(2,1)} custom-call(bf16[1024,2048]{1,0:T(8,128)(2,1)} %shard_map.102.x_ref, bf16[32,2,32,384]{3,2,1,0:T(8,128)(2,1)} %all-gather.4.cloned.1.call-done.w_ref), custom_call_target="tpu_custom_call" | custom-call | flops 1073741824 | bytes 5767168 | tf_op jit(solution)/shard_map/pallas_call | solution.py:195
  110.7 2.6 %broadcast_select_fusion = (bf16[2,1536,128]{2,1,0:T(8,128)(2,1)}, bf16[2,1536,128]{2,1,0:T(8,128)(2,1)}) fusion(bf16[2,1536,128]{2,1,0:T(8,128)(2,1)} %collective-permute-done.10, pred[]{:T(512)S(6)} %eq.2, bf16[2,512,128]{2,1,0:T(8,128)(2,1)S(1)} %bitcast.42, bf16[2,512,128]{2,1,0:T(8,128)(2,1)S(1)} %reverse_select_fusion, ...), kind=kLoop, calls=%fused_computation.8 | loop fusion | flops 3145728 | bytes 3145729 | tf_op jit(solution)/shard_map/jit(_where)/select_n | solution.py:33
  113.3 5.3 %shard_map.105.left_ref = bf16[2,256,256]{2,1,0:T(8,128)(2,1)} custom-call(s32[2]{0:T(128)} %add_multiply_fusion.1.first_ref, bf16[2,512,256]{2,1,0:T(8,128)(2,1)} %bitcast.46, bf16[2,1536,128]{2,1,0:T(8,128)(2,1)} %get-tuple-element.46.k_ref, bf16[2,1536,128]{2,1,0:T(8,128)(2,1)} %get-tuple-element.45.v_ref), custom_call_target="tpu_custom_call" | custom-call | flops 671088640 | bytes 2097152 | tf_op jit(solution)/shard_map/pallas_call | solution.py:294
  118.7 2.5 all-to-all-done.1
  122.2 3.3 %shard_map.106 = (f32[512,1024]{1,0:T(8,128)}, bf16[512,1024]{1,0:T(8,128)(2,1)}) custom-call(s32[1]{0:T(128)} %bitcast.me_ref, bf16[2,256,256]{2,1,0:T(8,128)(2,1)} %shard_map.105.left_ref, bf16[32,2,32,256]{3,2,1,0:T(8,128)(2,1)} %bitcast.44), custom_call_target="tpu_custom_call" | custom-call | flops 536870912 | bytes 4194304 | tf_op jit(solution)/shard_map/pallas_call | solution.py:234
  126.4 5.5 %shard_map.108.left_ref = bf16[2,256,256]{2,1,0:T(8,128)(2,1)} custom-call(s32[2]{0:T(128)} %add_multiply_fusion.1.first_ref, bf16[2,512,256]{2,1,0:T(8,128)(2,1)} %bitcast.47, bf16[2,1536,128]{2,1,0:T(8,128)(2,1)} %get-tuple-element.46.k_ref, bf16[2,1536,128]{2,1,0:T(8,128)(2,1)} %get-tuple-element.45.v_ref), custom_call_target="tpu_custom_call" | custom-call | flops 671088640 | bytes 2097152 | tf_op jit(solution)/shard_map/pallas_call | solution.py:294
  131.9 3.4 %shard_map.109 = (f32[512,1024]{1,0:T(8,128)}, bf16[512,1024]{1,0:T(8,128)(2,1)}) custom-call(s32[1]{0:T(128)} %bitcast.me_ref, bf16[2,256,256]{2,1,0:T(8,128)(2,1)} %shard_map.108.left_ref, bf16[32,2,32,256]{3,2,1,0:T(8,128)(2,1)} %bitcast.45), custom_call_target="tpu_custom_call" | custom-call | flops 536870912 | bytes 4194304 | tf_op jit(solution)/shard_map/pallas_call | solution.py:234
  137.5 2.3 collective-permute-start.14
  142.0 2.3 collective-permute-start.26
  144.3 2.1 collective-permute-done.14
  146.5 2.0 collective-permute-start.24
  148.5 4.5 %collective-permute-done.12 = bf16[256,512]{1,0:T(8,128)(2,1)S(1)} collective-permute-done((bf16[256,512]{1,0:T(8,128)(2,1)S(1)}, bf16[256,512]{1,0:T(8,128)(2,1)S(1)}, u32[]{:S(2)}, u32[]{:S(2)}) %collective-permute-start.12) | collective-permute-done | bytes 262176 | tf_op jit(solution)/shard_map/ppermute | solution.py:29
  153.1 4.6 %collective-permute-done.26 = bf16[256,512]{1,0:T(8,128)(2,1)S(1)} collective-permute-done((bf16[256,512]{1,0:T(8,128)(2,1)S(1)}, bf16[256,512]{1,0:T(8,128)(2,1)S(1)}, u32[]{:S(2)}, u32[]{:S(2)}) %collective-permute-start.26) | collective-permute-done | bytes 262176 | tf_op jit(solution)/shard_map/ppermute | solution.py:29
  158.3 5.8 %collective-permute-done.24 = bf16[256,512]{1,0:T(8,128)(2,1)S(1)} collective-permute-done((bf16[256,512]{1,0:T(8,128)(2,1)S(1)}, bf16[256,512]{1,0:T(8,128)(2,1)S(1)}, u32[]{:S(2)}, u32[]{:S(2)}) %collective-permute-start.24) | collective-permute-done | bytes 262176 | tf_op jit(solution)/shard_map/ppermute | solution.py:29
  164.4 2.2 collective-permute-start.29
  168.3 3.9 %collective-permute-done.29 = bf16[256,512]{1,0:T(8,128)(2,1)S(1)} collective-permute-done((bf16[256,512]{1,0:T(8,128)(2,1)S(1)}, bf16[256,512]{1,0:T(8,128)(2,1)S(1)}, u32[]{:S(2)}, u32[]{:S(2)}) %collective-permute-start.29) | collective-permute-done | bytes 262176 | tf_op jit(solution)/shard_map/ppermute | solution.py:29
  172.7 6.0 %collective-permute-done.27 = bf16[256,512]{1,0:T(8,128)(2,1)S(1)} collective-permute-done((bf16[256,512]{1,0:T(8,128)(2,1)S(1)}, bf16[256,512]{1,0:T(8,128)(2,1)S(1)}, u32[]{:S(2)}, u32[]{:S(2)}) %collective-permute-start.27) | collective-permute-done | bytes 262176 | tf_op jit(solution)/shard_map/ppermute | solution.py:29
  178.8 2.6 %collective-permute-start.30 = (bf16[4,256,512]{2,1,0:T(8,128)(2,1)S(1)}, bf16[4,256,512]{2,1,0:T(8,128)(2,1)}, u32[]{:S(2)}, u32[]{:S(2)}) collective-permute-start(bf16[4,256,512]{2,1,0:T(8,128)(2,1)S(1)} %pad_maximum_fusion.2.mine_ref), channel_id=1, source_target_pairs={{0,1},{1,0},{2,3},{3,2},{4,5},{5,4},{6,7},{7,6},{8,9},{9,8},{10,11... | collective-permute-start | bytes 3145736 | tf_op jit(solution)/shard_map/ppermute | solution.py:25
  181.4 2.1 collective-permute-start.17
  185.3 5.1 %collective-permute-done.17 = bf16[256,512]{1,0:T(8,128)(2,1)S(1)} collective-permute-done((bf16[256,512]{1,0:T(8,128)(2,1)S(1)}, bf16[256,512]{1,0:T(8,128)(2,1)S(1)}, u32[]{:S(2)}, u32[]{:S(2)}) %collective-permute-start.17) | collective-permute-done | bytes 262176 | tf_op jit(solution)/shard_map/ppermute | solution.py:29
  191.0 5.9 %collective-permute-done.15 = bf16[256,512]{1,0:T(8,128)(2,1)S(1)} collective-permute-done((bf16[256,512]{1,0:T(8,128)(2,1)S(1)}, bf16[256,512]{1,0:T(8,128)(2,1)S(1)}, u32[]{:S(2)}, u32[]{:S(2)}) %collective-permute-start.15) | collective-permute-done | bytes 262176 | tf_op jit(solution)/shard_map/ppermute | solution.py:29
  198.6 10.8 %shard_map.110 = (f32[512,1024]{1,0:T(8,128)}, bf16[512,1024]{1,0:T(8,128)(2,1)}) custom-call(s32[1]{0:T(128)} %bitcast.me_ref, bf16[4,256,512]{2,1,0:T(8,128)(2,1)} %copy-done.1, bf16[4,256,512]{2,1,0:T(8,128)(2,1)} %collective-permute-done.30.theirs_ref, f32[1,2048]{1,0:T(1,128)} %bitcast.61, bf16[32,2,32,2304]{3,2,1,0:T(8,128)(2,1)} %bitcast.31, ...), custom_call_target="tpu_custom_call" | custom-call | flops 4831838208 | bytes 13631488 | tf_op jit(solution)/shard_map/pallas_call | solution.py:163
  209.6 10.8 %shard_map.107 = (f32[512,1024]{1,0:T(8,128)}, bf16[512,1024]{1,0:T(8,128)(2,1)}) custom-call(s32[1]{0:T(128)} %bitcast.me_ref, bf16[4,256,512]{2,1,0:T(8,128)(2,1)} %copy-done.2, bf16[4,256,512]{2,1,0:T(8,128)(2,1)} %collective-permute-done.18.theirs_ref, f32[1,2048]{1,0:T(1,128)} %bitcast.62, bf16[32,2,32,2304]{3,2,1,0:T(8,128)(2,1)} %bitcast.34, ...), custom_call_target="tpu_custom_call" | custom-call | flops 4831838208 | bytes 13631488 | tf_op jit(solution)/shard_map/pallas_call | solution.py:163
  220.9 2.2 fusion.18
  223.1 2.1 collective-permute-start.34
  225.3 1.8 collective-permute-start.32
  227.7 2.1 collective-permute-start.22
  229.9 2.4 collective-permute-done.34
  232.8 6.0 %collective-permute-done.32 = bf16[256,512]{1,0:T(8,128)(2,1)S(1)} collective-permute-done((bf16[256,512]{1,0:T(8,128)(2,1)S(1)}, bf16[256,512]{1,0:T(8,128)(2,1)S(1)}, u32[]{:S(2)}, u32[]{:S(2)}) %collective-permute-start.32) | collective-permute-done | bytes 262176 | tf_op jit(solution)/shard_map/ppermute | solution.py:29
  239.0 4.5 %collective-permute-done.22 = bf16[256,512]{1,0:T(8,128)(2,1)S(1)} collective-permute-done((bf16[256,512]{1,0:T(8,128)(2,1)S(1)}, bf16[256,512]{1,0:T(8,128)(2,1)S(1)}, u32[]{:S(2)}, u32[]{:S(2)}) %collective-permute-start.22) | collective-permute-done | bytes 262176 | tf_op jit(solution)/shard_map/ppermute | solution.py:29
  244.1 6.0 %collective-permute-done.20 = bf16[256,512]{1,0:T(8,128)(2,1)S(1)} collective-permute-done((bf16[256,512]{1,0:T(8,128)(2,1)S(1)}, bf16[256,512]{1,0:T(8,128)(2,1)S(1)}, u32[]{:S(2)}, u32[]{:S(2)}) %collective-permute-start.20) | collective-permute-done | bytes 262176 | tf_op jit(solution)/shard_map/ppermute | solution.py:29
  (97 shorter events, 31.4 us)
Async XLA Ops:
  6.5 17.2 %copy-start.7 = (bf16[512,512]{1,0:T(8,128)(2,1)S(1)}, bf16[512,512]{1,0:T(8,128)(2,1)}, u32[]{:S(2)}) copy-start(bf16[512,512]{1,0:T(8,128)(2,1)} %param.10) | copy-start | bytes 1572868
  8.1 6.5 %collective-permute-start.2 = (bf16[32,640]{1,0:T(8,128)(2,1)}, bf16[32,640]{1,0:T(8,128)(2,1)S(1)}, u32[]{:S(2)}, u32[]{:S(2)}) collective-permute-start(bf16[32,640]{1,0:T(8,128)(2,1)} %get-tuple-element.23), channel_id=1, source_target_pairs={{0,0},{1,128},{128,1},{129,129},{2,2},{3,130},{130,3},{131,131},{4... | collective-permute-start | bytes 122888 | tf_op jit(solution)/shard_map/ppermute | solution.py:38
  12.7 1.9 collective-permute-start.3
  15.5 28.9 %all-to-all-start = ((bf16[8,2,32,640]{3,2,1,0:T(8,128)(2,1)}), bf16[8,2,32,640]{3,2,1,0:T(8,128)(2,1)S(1)}, u32[]{:S(2)}, u32[]{:S(2)}) async-start(bf16[8,2,32,640]{3,2,1,0:T(8,128)(2,1)} %broadcast_in_dim.10), calls=%async_computation | async-start | bytes 1310720 | tf_op jit(solution)/shard_map/all_to_all | solution.py:19
  23.7 47.5 %all-gather.4.cloned.1.call-start = ((), (), s32[]{:S(2)}) async-start(), calls=%async_computation.2 | async-start | bytes 1966080 | tf_op jit(solution)/shard_map/all_gather | solution.py:378
  23.8 21.6 %collective-permute-start.6 = (bf16[512,512]{1,0:T(8,128)(2,1)S(1)}, bf16[512,512]{1,0:T(8,128)(2,1)S(1)}, u32[]{:S(2)}, u32[]{:S(2)}) collective-permute-start(bf16[512,512]{1,0:T(8,128)(2,1)S(1)} %copy-done.7), channel_id=1, source_target_pairs={{0,130},{2,128},{128,2},{130,0},{1,131},{3,129},{129,3},{131,1},{4... | collective-permute-start | bytes 1572872 | tf_op jit(solution)/shard_map/ppermute | solution.py:29
  26.9 18.5 %collective-permute-start.5 = (bf16[512,512]{1,0:T(8,128)(2,1)S(1)}, bf16[512,512]{1,0:T(8,128)(2,1)S(1)}, u32[]{:S(2)}, u32[]{:S(2)}) collective-permute-start(bf16[512,512]{1,0:T(8,128)(2,1)S(1)} %copy-done.7), channel_id=1, source_target_pairs={{0,128},{2,130},{128,0},{130,2},{1,129},{3,131},{129,1},{131,3},{4... | collective-permute-start | bytes 1572872 | tf_op jit(solution)/shard_map/ppermute | solution.py:29
  26.9 23.3 %collective-permute-start.4 = (bf16[512,512]{1,0:T(8,128)(2,1)S(1)}, bf16[512,512]{1,0:T(8,128)(2,1)S(1)}, u32[]{:S(2)}, u32[]{:S(2)}) collective-permute-start(bf16[512,512]{1,0:T(8,128)(2,1)S(1)} %copy-done.7), channel_id=1, source_target_pairs={{0,2},{2,0},{128,130},{130,128},{1,3},{3,1},{129,131},{131,129},{4... | collective-permute-start | bytes 1572872 | tf_op jit(solution)/shard_map/ppermute | solution.py:29
  45.3 153.3 %all-gather.6.cloned.1.call-start = ((), (), s32[]{:S(2)}) async-start(), calls=%async_computation.3 | async-start | bytes 9732096 | tf_op jit(solution)/shard_map/all_gather | solution.py:381
  45.4 4.8 %copy-start.9 = (bf16[512,512]{1,0:T(8,128)(2,1)}, bf16[512,512]{1,0:T(8,128)(2,1)S(1)}, u32[]{:S(2)}) copy-start(bf16[512,512]{1,0:T(8,128)(2,1)S(1)} %collective-permute-done.6) | copy-start | bytes 1572868
  45.4 4.8 %copy-start.10 = (bf16[512,512]{1,0:T(8,128)(2,1)}, bf16[512,512]{1,0:T(8,128)(2,1)S(1)}, u32[]{:S(2)}) copy-start(bf16[512,512]{1,0:T(8,128)(2,1)S(1)} %collective-permute-done.5) | copy-start | bytes 1572868
  52.6 12.9 %copy-start = (bf16[4,512,512]{2,1,0:T(8,128)(2,1)}, bf16[4,512,512]{2,1,0:T(8,128)(2,1)S(1)}, u32[]{:S(2)}) copy-start(bf16[4,512,512]{2,1,0:T(8,128)(2,1)S(1)} %pad_maximum_fusion.mine_ref) | copy-start | bytes 6291460
  52.6 12.9 %collective-permute-start.7 = (bf16[4,512,512]{2,1,0:T(8,128)(2,1)S(1)}, bf16[4,512,512]{2,1,0:T(8,128)(2,1)}, u32[]{:S(2)}, u32[]{:S(2)}) collective-permute-start(bf16[4,512,512]{2,1,0:T(8,128)(2,1)S(1)} %pad_maximum_fusion.mine_ref), channel_id=1, source_target_pairs={{0,1},{1,0},{2,3},{3,2},{4,5},{5,4},{6,7},{7,6},{8,9},{9,8},{10,11... | collective-permute-start | bytes 6291464 | tf_op jit(solution)/shard_map/ppermute | solution.py:25
  56.8 7.1 %collective-permute-start = (bf16[32,2304]{1,0:T(8,128)(2,1)}, bf16[32,2304]{1,0:T(8,128)(2,1)S(1)}, u32[]{:S(2)}, u32[]{:S(2)}) collective-permute-start(bf16[32,2304]{1,0:T(8,128)(2,1)} %get-tuple-element.21), channel_id=1, source_target_pairs={{0,0},{1,128},{128,1},{129,129},{2,2},{3,130},{130,3},{131,131},{4... | collective-permute-start | bytes 442376 | tf_op jit(solution)/shard_map/ppermute | solution.py:38
  59.1 4.7 %collective-permute-start.1 = (bf16[32,2304]{1,0:T(8,128)(2,1)}, bf16[32,2304]{1,0:T(8,128)(2,1)}, u32[]{:S(2)}, u32[]{:S(2)}) collective-permute-start(bf16[32,2304]{1,0:T(8,128)(2,1)} %get-tuple-element.22), channel_id=1, source_target_pairs={{0,1},{1,129},{128,0},{129,128},{2,3},{3,131},{130,2},{131,130},{4... | collective-permute-start | bytes 442376 | tf_op jit(solution)/shard_map/ppermute | solution.py:38
  75.0 9.5 %collective-permute-start.9 = (bf16[2,512,128]{2,1,0:T(8,128)(2,1)}, bf16[2,512,128]{2,1,0:T(8,128)(2,1)S(1)}, u32[]{:S(2)}, u32[]{:S(2)}) collective-permute-start(bf16[2,512,128]{2,1,0:T(8,128)(2,1)} %bitcast.39), channel_id=1, source_target_pairs={{0,4},{4,8},{8,12},{12,16},{16,20},{20,24},{24,28},{28,32},{32,36}... | collective-permute-start | bytes 786440 | tf_op jit(solution)/shard_map/ppermute | solution.py:388
  76.4 17.0 %collective-permute-start.8 = (bf16[2,512,128]{2,1,0:T(8,128)(2,1)}, bf16[2,512,128]{2,1,0:T(8,128)(2,1)S(1)}, u32[]{:S(2)}, u32[]{:S(2)}) collective-permute-start(bf16[2,512,128]{2,1,0:T(8,128)(2,1)} %bitcast.40), channel_id=1, source_target_pairs={{0,8},{4,12},{8,16},{12,20},{16,24},{20,28},{24,32},{28,36},{32,40... | collective-permute-start | bytes 786440 | tf_op jit(solution)/shard_map/ppermute | solution.py:388
  95.4 15.3 %collective-permute-start.10 = (bf16[2,1536,128]{2,1,0:T(8,128)(2,1)}, bf16[2,1536,128]{2,1,0:T(8,128)(2,1)}, u32[]{:S(2)}, u32[]{:S(2)}) collective-permute-start(bf16[2,1536,128]{2,1,0:T(8,128)(2,1)} %pad_maximum_fusion.3), channel_id=1, source_target_pairs={{0,1},{1,0},{2,3},{3,2},{4,5},{5,4},{6,7},{7,6},{8,9},{9,8},{10,11... | collective-permute-start | bytes 2359304 | tf_op jit(solution)/shard_map/ppermute | solution.py:25
  102.5 18.7 %all-to-all-start.1 = ((bf16[4,8,2,32,256]{4,3,2,1,0:T(8,128)(2,1)}), bf16[4,8,2,32,256]{4,3,2,1,0:T(8,128)(2,1)S(1)}, u32[]{:S(2)}, u32[]{:S(2)}) async-start(bf16[4,8,2,32,256]{4,3,2,1,0:T(8,128)(2,1)} %broadcast_in_dim.24), calls=%async_computation.1 | async-start | bytes 2097152 | tf_op jit(solution)/shard_map/all_to_all | solution.py:19
  125.5 10.1 %copy-start.6 = (f32[512,1024]{1,0:T(8,128)S(1)}, f32[512,1024]{1,0:T(8,128)}, u32[]{:S(2)}) copy-start(f32[512,1024]{1,0:T(8,128)} %get-tuple-element.27) | copy-start | bytes 6291460
  125.5 10.0 %collective-permute-start.11 = (bf16[512,1024]{1,0:T(8,128)(2,1)}, bf16[512,1024]{1,0:T(8,128)(2,1)}, u32[]{:S(2)}, u32[]{:S(2)}) collective-permute-start(bf16[512,1024]{1,0:T(8,128)(2,1)} %get-tuple-element.28), channel_id=1, source_target_pairs={{0,1},{1,0},{2,3},{3,2},{4,5},{5,4},{6,7},{7,6},{8,9},{9,8},{10,11... | collective-permute-start | bytes 3145736 | tf_op jit(solution)/shard_map/ppermute | solution.py:25
  135.3 6.1 %collective-permute-start.23 = (bf16[512,1024]{1,0:T(8,128)(2,1)}, bf16[512,1024]{1,0:T(8,128)(2,1)S(1)}, u32[]{:S(2)}, u32[]{:S(2)}) collective-permute-start(bf16[512,1024]{1,0:T(8,128)(2,1)} %get-tuple-element.34), channel_id=1, source_target_pairs={{0,1},{1,0},{2,3},{3,2},{4,5},{5,4},{6,7},{7,6},{8,9},{9,8},{10,11... | collective-permute-start | bytes 3145736 | tf_op jit(solution)/shard_map/ppermute | solution.py:25
  135.6 5.8 %copy-start.5 = (f32[512,1024]{1,0:T(8,128)S(1)}, f32[512,1024]{1,0:T(8,128)}, u32[]{:S(2)}) copy-start(f32[512,1024]{1,0:T(8,128)} %get-tuple-element.33) | copy-start | bytes 6291460
  137.5 9.0 %collective-permute-start.14 = (bf16[256,512]{1,0:T(8,128)(2,1)S(1)}, bf16[256,512]{1,0:T(8,128)(2,1)S(1)}, u32[]{:S(2)}, u32[]{:S(2)}) collective-permute-start(bf16[256,512]{1,0:T(8,128)(2,1)S(1)} %get-tuple-element.54), channel_id=1, source_target_pairs={{0,130},{2,128},{128,2},{130,0},{1,131},{3,129},{129,3},{131,1},{4... | collective-permute-start | bytes 786440 | tf_op jit(solution)/shard_map/ppermute | solution.py:29
  139.8 8.7 %collective-permute-start.13 = (bf16[256,512]{1,0:T(8,128)(2,1)S(1)}, bf16[256,512]{1,0:T(8,128)(2,1)S(1)}, u32[]{:S(2)}, u32[]{:S(2)}) collective-permute-start(bf16[256,512]{1,0:T(8,128)(2,1)S(1)} %get-tuple-element.55), channel_id=1, source_target_pairs={{0,128},{2,130},{128,0},{130,2},{1,129},{3,131},{129,1},{131,3},{4... | collective-permute-start | bytes 786440 | tf_op jit(solution)/shard_map/ppermute | solution.py:29
  140.4 12.6 %collective-permute-start.12 = (bf16[256,512]{1,0:T(8,128)(2,1)S(1)}, bf16[256,512]{1,0:T(8,128)(2,1)S(1)}, u32[]{:S(2)}, u32[]{:S(2)}) collective-permute-start(bf16[256,512]{1,0:T(8,128)(2,1)S(1)} %get-tuple-element.53), channel_id=1, source_target_pairs={{0,2},{2,0},{128,130},{130,128},{1,3},{3,1},{129,131},{131,129},{4... | collective-permute-start | bytes 786440 | tf_op jit(solution)/shard_map/ppermute | solution.py:29
  142.0 15.7 %collective-permute-start.26 = (bf16[256,512]{1,0:T(8,128)(2,1)S(1)}, bf16[256,512]{1,0:T(8,128)(2,1)S(1)}, u32[]{:S(2)}, u32[]{:S(2)}) collective-permute-start(bf16[256,512]{1,0:T(8,128)(2,1)S(1)} %get-tuple-element.57), channel_id=1, source_target_pairs={{0,130},{2,128},{128,2},{130,0},{1,131},{3,129},{129,3},{131,1},{4... | collective-permute-start | bytes 786440 | tf_op jit(solution)/shard_map/ppermute | solution.py:29
  144.3 14.0 %collective-permute-start.25 = (bf16[256,512]{1,0:T(8,128)(2,1)S(1)}, bf16[256,512]{1,0:T(8,128)(2,1)S(1)}, u32[]{:S(2)}, u32[]{:S(2)}) collective-permute-start(bf16[256,512]{1,0:T(8,128)(2,1)S(1)} %get-tuple-element.58), channel_id=1, source_target_pairs={{0,128},{2,130},{128,0},{130,2},{1,129},{3,131},{129,1},{131,3},{4... | collective-permute-start | bytes 786440 | tf_op jit(solution)/shard_map/ppermute | solution.py:29
  146.5 17.7 %collective-permute-start.24 = (bf16[256,512]{1,0:T(8,128)(2,1)S(1)}, bf16[256,512]{1,0:T(8,128)(2,1)S(1)}, u32[]{:S(2)}, u32[]{:S(2)}) collective-permute-start(bf16[256,512]{1,0:T(8,128)(2,1)S(1)} %get-tuple-element.56), channel_id=1, source_target_pairs={{0,2},{2,0},{128,130},{130,128},{1,3},{3,1},{129,131},{131,129},{4... | collective-permute-start | bytes 786440 | tf_op jit(solution)/shard_map/ppermute | solution.py:29
  164.4 7.9 %collective-permute-start.29 = (bf16[256,512]{1,0:T(8,128)(2,1)S(1)}, bf16[256,512]{1,0:T(8,128)(2,1)S(1)}, u32[]{:S(2)}, u32[]{:S(2)}) collective-permute-start(bf16[256,512]{1,0:T(8,128)(2,1)S(1)} %fusion.7), channel_id=1, source_target_pairs={{0,130},{2,128},{128,2},{130,0},{1,131},{3,129},{129,3},{131,1},{4... | collective-permute-start | bytes 786440 | tf_op jit(solution)/shard_map/ppermute | solution.py:29
  166.5 6.2 %collective-permute-start.28 = (bf16[256,512]{1,0:T(8,128)(2,1)S(1)}, bf16[256,512]{1,0:T(8,128)(2,1)S(1)}, u32[]{:S(2)}, u32[]{:S(2)}) collective-permute-start(bf16[256,512]{1,0:T(8,128)(2,1)S(1)} %fusion.7), channel_id=1, source_target_pairs={{0,128},{2,130},{128,0},{130,2},{1,129},{3,131},{129,1},{131,3},{4... | collective-permute-start | bytes 786440 | tf_op jit(solution)/shard_map/ppermute | solution.py:29
  166.5 12.1 %collective-permute-start.27 = (bf16[256,512]{1,0:T(8,128)(2,1)S(1)}, bf16[256,512]{1,0:T(8,128)(2,1)S(1)}, u32[]{:S(2)}, u32[]{:S(2)}) collective-permute-start(bf16[256,512]{1,0:T(8,128)(2,1)S(1)} %fusion.7), channel_id=1, source_target_pairs={{0,2},{2,0},{128,130},{130,128},{1,3},{3,1},{129,131},{131,129},{4... | collective-permute-start | bytes 786440 | tf_op jit(solution)/shard_map/ppermute | solution.py:29
  178.8 19.8 %copy-start.1 = (bf16[4,256,512]{2,1,0:T(8,128)(2,1)}, bf16[4,256,512]{2,1,0:T(8,128)(2,1)S(1)}, u32[]{:S(2)}) copy-start(bf16[4,256,512]{2,1,0:T(8,128)(2,1)S(1)} %pad_maximum_fusion.2.mine_ref) | copy-start | bytes 3145732
  178.8 19.8 %collective-permute-start.30 = (bf16[4,256,512]{2,1,0:T(8,128)(2,1)S(1)}, bf16[4,256,512]{2,1,0:T(8,128)(2,1)}, u32[]{:S(2)}, u32[]{:S(2)}) collective-permute-start(bf16[4,256,512]{2,1,0:T(8,128)(2,1)S(1)} %pad_maximum_fusion.2.mine_ref), channel_id=1, source_target_pairs={{0,1},{1,0},{2,3},{3,2},{4,5},{5,4},{6,7},{7,6},{8,9},{9,8},{10,11... | collective-permute-start | bytes 3145736 | tf_op jit(solution)/shard_map/ppermute | solution.py:25
  181.4 9.0 %collective-permute-start.17 = (bf16[256,512]{1,0:T(8,128)(2,1)S(1)}, bf16[256,512]{1,0:T(8,128)(2,1)S(1)}, u32[]{:S(2)}, u32[]{:S(2)}) collective-permute-start(bf16[256,512]{1,0:T(8,128)(2,1)S(1)} %fusion.15), channel_id=1, source_target_pairs={{0,130},{2,128},{128,2},{130,0},{1,131},{3,129},{129,3},{131,1},{4... | collective-permute-start | bytes 786440 | tf_op jit(solution)/shard_map/ppermute | solution.py:29
  183.5 7.5 %collective-permute-start.16 = (bf16[256,512]{1,0:T(8,128)(2,1)S(1)}, bf16[256,512]{1,0:T(8,128)(2,1)S(1)}, u32[]{:S(2)}, u32[]{:S(2)}) collective-permute-start(bf16[256,512]{1,0:T(8,128)(2,1)S(1)} %fusion.15), channel_id=1, source_target_pairs={{0,128},{2,130},{128,0},{130,2},{1,129},{3,131},{129,1},{131,3},{4... | collective-permute-start | bytes 786440 | tf_op jit(solution)/shard_map/ppermute | solution.py:29
  183.5 13.4 %collective-permute-start.15 = (bf16[256,512]{1,0:T(8,128)(2,1)S(1)}, bf16[256,512]{1,0:T(8,128)(2,1)S(1)}, u32[]{:S(2)}, u32[]{:S(2)}) collective-permute-start(bf16[256,512]{1,0:T(8,128)(2,1)S(1)} %fusion.15), channel_id=1, source_target_pairs={{0,2},{2,0},{128,130},{130,128},{1,3},{3,1},{129,131},{131,129},{4... | collective-permute-start | bytes 786440 | tf_op jit(solution)/shard_map/ppermute | solution.py:29
  197.0 12.4 %copy-start.2 = (bf16[4,256,512]{2,1,0:T(8,128)(2,1)}, bf16[4,256,512]{2,1,0:T(8,128)(2,1)S(1)}, u32[]{:S(2)}) copy-start(bf16[4,256,512]{2,1,0:T(8,128)(2,1)S(1)} %pad_maximum_fusion.1.mine_ref) | copy-start | bytes 3145732
  197.0 12.5 %collective-permute-start.18 = (bf16[4,256,512]{2,1,0:T(8,128)(2,1)S(1)}, bf16[4,256,512]{2,1,0:T(8,128)(2,1)}, u32[]{:S(2)}, u32[]{:S(2)}) collective-permute-start(bf16[4,256,512]{2,1,0:T(8,128)(2,1)S(1)} %pad_maximum_fusion.1.mine_ref), channel_id=1, source_target_pairs={{0,1},{1,0},{2,3},{3,2},{4,5},{5,4},{6,7},{7,6},{8,9},{9,8},{10,11... | collective-permute-start | bytes 3145736 | tf_op jit(solution)/shard_map/ppermute | solution.py:25
  209.4 11.5 %collective-permute-start.31 = (bf16[512,1024]{1,0:T(8,128)(2,1)}, bf16[512,1024]{1,0:T(8,128)(2,1)S(1)}, u32[]{:S(2)}, u32[]{:S(2)}) collective-permute-start(bf16[512,1024]{1,0:T(8,128)(2,1)} %get-tuple-element.36), channel_id=1, source_target_pairs={{0,1},{1,0},{2,3},{3,2},{4,5},{5,4},{6,7},{7,6},{8,9},{9,8},{10,11... | collective-permute-start | bytes 3145736 | tf_op jit(solution)/shard_map/ppermute | solution.py:25
  220.3 6.7 %collective-permute-start.19 = (bf16[512,1024]{1,0:T(8,128)(2,1)}, bf16[512,1024]{1,0:T(8,128)(2,1)S(1)}, u32[]{:S(2)}, u32[]{:S(2)}) collective-permute-start(bf16[512,1024]{1,0:T(8,128)(2,1)} %get-tuple-element.31), channel_id=1, source_target_pairs={{0,1},{1,0},{2,3},{3,2},{4,5},{5,4},{6,7},{7,6},{8,9},{9,8},{10,11... | collective-permute-start | bytes 3145736 | tf_op jit(solution)/shard_map/ppermute | solution.py:25
  220.9 6.2 %copy-start.4 = (f32[512,1024]{1,0:T(8,128)S(1)}, f32[512,1024]{1,0:T(8,128)}, u32[]{:S(2)}) copy-start(f32[512,1024]{1,0:T(8,128)} %get-tuple-element.30) | copy-start | bytes 6291460
  223.1 9.1 %collective-permute-start.34 = (bf16[256,512]{1,0:T(8,128)(2,1)S(1)}, bf16[256,512]{1,0:T(8,128)(2,1)S(1)}, u32[]{:S(2)}, u32[]{:S(2)}) collective-permute-start(bf16[256,512]{1,0:T(8,128)(2,1)S(1)} %get-tuple-element.51), channel_id=1, source_target_pairs={{0,130},{2,128},{128,2},{130,0},{1,131},{3,129},{129,3},{131,1},{4... | collective-permute-start | bytes 786440 | tf_op jit(solution)/shard_map/ppermute | solution.py:29
  225.3 7.5 %collective-permute-start.33 = (bf16[256,512]{1,0:T(8,128)(2,1)S(1)}, bf16[256,512]{1,0:T(8,128)(2,1)S(1)}, u32[]{:S(2)}, u32[]{:S(2)}) collective-permute-start(bf16[256,512]{1,0:T(8,128)(2,1)S(1)} %get-tuple-element.52), channel_id=1, source_target_pairs={{0,128},{2,130},{128,0},{130,2},{1,129},{3,131},{129,1},{131,3},{4... | collective-permute-start | bytes 786440 | tf_op jit(solution)/shard_map/ppermute | solution.py:29
  225.3 13.5 %collective-permute-start.32 = (bf16[256,512]{1,0:T(8,128)(2,1)S(1)}, bf16[256,512]{1,0:T(8,128)(2,1)S(1)}, u32[]{:S(2)}, u32[]{:S(2)}) collective-permute-start(bf16[256,512]{1,0:T(8,128)(2,1)S(1)} %get-tuple-element.50), channel_id=1, source_target_pairs={{0,2},{2,0},{128,130},{130,128},{1,3},{3,1},{129,131},{131,129},{4... | collective-permute-start | bytes 786440 | tf_op jit(solution)/shard_map/ppermute | solution.py:29
  227.7 15.8 %collective-permute-start.22 = (bf16[256,512]{1,0:T(8,128)(2,1)S(1)}, bf16[256,512]{1,0:T(8,128)(2,1)S(1)}, u32[]{:S(2)}, u32[]{:S(2)}) collective-permute-start(bf16[256,512]{1,0:T(8,128)(2,1)S(1)} %get-tuple-element.48), channel_id=1, source_target_pairs={{0,130},{2,128},{128,2},{130,0},{1,131},{3,129},{129,3},{131,1},{4... | collective-permute-start | bytes 786440 | tf_op jit(solution)/shard_map/ppermute | solution.py:29
  229.8 14.2 %collective-permute-start.21 = (bf16[256,512]{1,0:T(8,128)(2,1)S(1)}, bf16[256,512]{1,0:T(8,128)(2,1)S(1)}, u32[]{:S(2)}, u32[]{:S(2)}) collective-permute-start(bf16[256,512]{1,0:T(8,128)(2,1)S(1)} %get-tuple-element.49), channel_id=1, source_target_pairs={{0,128},{2,130},{128,0},{130,2},{1,129},{3,131},{129,1},{131,3},{4... | collective-permute-start | bytes 786440 | tf_op jit(solution)/shard_map/ppermute | solution.py:29
  232.2 17.8 %collective-permute-start.20 = (bf16[256,512]{1,0:T(8,128)(2,1)S(1)}, bf16[256,512]{1,0:T(8,128)(2,1)S(1)}, u32[]{:S(2)}, u32[]{:S(2)}) collective-permute-start(bf16[256,512]{1,0:T(8,128)(2,1)S(1)} %get-tuple-element.47), channel_id=1, source_target_pairs={{0,2},{2,0},{128,130},{130,128},{1,3},{3,1},{129,131},{131,129},{4... | collective-permute-start | bytes 786440 | tf_op jit(solution)/shard_map/ppermute | solution.py:29
  (3 other events, 5.8 us)
Sparse Core Ops, SparseCore 0:
  45.4 25.1 all-gather.3
  73.1 105.3 all-gather.5

commit v4 on v3

--- a/solution.py
+++ b/solution.py
@@ -60,6 +60,7 @@
             scratch_shapes=scratch,
         ),
         out_shape=out_shape,
+        compiler_params=pltpu.CompilerParams(vmem_limit_bytes=32 * 1024 * 1024),
         cost_estimate=pl.CostEstimate(flops=flops, bytes_accessed=moved, transcendentals=0),
     )
 
@@ -182,7 +183,7 @@
 def projected(left, weights, start, width):
     n, d = left.shape
     chips, runs, r = weights.shape[:3]
-    step = 512
+    step = 256
 
     def kernel(x_ref, w_ref, out_ref):
         total = 0.0
@@ -261,19 +262,21 @@
     return total
 
 
-def window_attention(queries, keys, values, first_key, part):
+def window_attention(queries, context, other_context, scalars, part):
     rows, width = queries.shape[1:]
-    span = keys.shape[1]
+    span = context.shape[1]
     count = width // HEAD_DIM
     step = rows // PARTS
     seen = WINDOW + step
     start = part * step + span - rows - WINDOW
     scale = HEAD_DIM ** (-0.5)
 
-    def kernel(first_ref, q_ref, k_ref, v_ref, out_ref):
+    def kernel(first_ref, q_ref, mine_ref, other_ref, out_ref):
         run = pl.program_id(0)
-        k = k_ref[0, start : start + seen, :]
-        v = v_ref[0, start : start + seen, :]
+        mine = mine_ref[0, start : start + seen, :]
+        other = other_ref[0, start : start + seen, :]
+        k = jnp.where(first_ref[2] == 0, mine, other)
+        v = jnp.where(first_ref[2] == 0, other, mine)
         query_pos = lax.broadcasted_iota(jnp.int32, (step, seen), 0)
         key_pos = lax.broadcasted_iota(jnp.int32, (step, seen), 1)
         distance = query_pos + WINDOW - key_pos
@@ -299,8 +302,8 @@
         pl.BlockSpec((1, step, width), lambda run, first: (run, 0, 0)),
         jax.ShapeDtypeStruct((2, step, width), jnp.bfloat16),
         flops=2 * step * width * seen * 4,
-        moved=2 * (2 * queries.size // PARTS + keys.size + values.size),
-    )(first_key, queries, keys, values)
+        moved=2 * (2 * queries.size // PARTS + 2 * context.size),
+    )(scalars, queries, context, other_context)
 
 
 def packed(parity, parts):
@@ -388,15 +391,16 @@
         came = lax.ppermute(fresh, PLANE, [(i, (i + step) % plane) for i in range(plane)])
         context.insert(0, jnp.where(place < step, came[::-1], came))
     context = jnp.concatenate(context, axis=1)
-    keys, values = ordered(core, context, other_core(context))
+    other_context = other_core(context)
 
     queries = projected(normed, attn_full, 0, heads).reshape(2, rows, heads)
     runs = jnp.stack([yl, 1 - yl])
     first_key = ((runs * plane + place - reach) * rows).astype(jnp.int32)
+    scalars = jnp.concatenate([first_key, jnp.reshape(core, (1,)).astype(jnp.int32)])
     part = rows // PARTS
     outputs = []
     for i in range(PARTS):
-        attended = window_attention(queries, keys, values, first_key, i)
+        attended = window_attention(queries, context, other_context, scalars, i)
         attn_share = column_sum(*head_terms(me, attended, out_full))
         residual = tokens[i * part : (i + 1) * part]
         if i > 0:

time: 261 us -> 252 us (0.966)
  the two profiles are of different devices: /device:TPU:1 before, /device:TPU:32 now
where the time goes in v4:
time: 252 us; the launch traced here: 251 us
  waiting for transfers between devices  118 us (47%)
  starting transfers between devices  57.3 us (23%)
  Pallas kernels  35.9 us (14%)
  local copies, waits for them, and re-layouts  20.4 us (8%)
  between operations  13.9 us (6%)
  other arithmetic  6.21 us (2%)
    ppermute x21, waiting for transfers between devices, column_partner(): return lax.ppermute(value, ('yl', 'yh'), [(i, i ^ flip) for i in range(4)])  67 us
    ppermute x21, starting transfers between devices, column_partner(): return lax.ppermute(value, ('yl', 'yh'), [(i, i ^ flip) for i in range(4)])  31.3 us
    ppermute x2, waiting for transfers between devices, per_device(): lax.ppermute(fresh, PLANE, [(i, (i + step) % plane) for i in range(plane)])  21.1 us
    all_to_all x2, waiting for transfers between devices, spread(): lax.all_to_all(jnp.broadcast_to(value[None], (length, *value.shape)), axi...  20 us
    unnamed x50, local copies, waits for them, and re-layouts  17.2 us
    pallas_call x2, Pallas kernels, unit_terms(): call(kernel, (steps + 2,), 1, [whole(mine.shape), whole(mine.shape), whol...  16.9 us
    all_to_all x2, starting transfers between devices, spread(): lax.all_to_all(jnp.broadcast_to(value[None], (length, *value.shape)), axi...  12.1 us
    pallas_call x2, Pallas kernels, window_attention(): call(kernel, (2,), 1, [pl.BlockSpec((1, step, width), lambda run, first:...  9.11 us
  transfers between devices with their start and end apart: 39, of which 25 were waited for; matrix products, arithmetic and copies ran while one was open for 3% of the time, Pallas kernels for 14%

profile of v4, /device:TPU:32, one launch (start us, length us, event | category | flops | bytes accessed | tf_op | source)
XLA Modules:
  0.0 251.5 jit_solution(14878078332326362690)
XLA Ops:
  10.3 3.0 %collective-permute-start.3 = (bf16[32,640]{1,0:T(8,128)(2,1)S(1)}, bf16[32,640]{1,0:T(8,128)(2,1)S(1)}, u32[]{:S(2)}, u32[]{:S(2)}) collective-permute-start(bf16[32,640]{1,0:T(8,128)(2,1)S(1)} %get-tuple-element.24), channel_id=1, source_target_pairs={{0,1},{1,129},{128,0},{129,128},{2,3},{3,131},{130,2},{131,130},{4... | collective-permute-start | bytes 122888 | tf_op jit(solution)/shard_map/ppermute | solution.py:38
  13.3 2.2 collective-permute-done.3
  16.5 8.6 %all-to-all-start = ((bf16[8,2,32,640]{3,2,1,0:T(8,128)(2,1)}), bf16[8,2,32,640]{3,2,1,0:T(8,128)(2,1)S(1)}, u32[]{:S(2)}, u32[]{:S(2)}) async-start(bf16[8,2,32,640]{3,2,1,0:T(8,128)(2,1)} %broadcast_in_dim.10), calls=%async_computation | async-start | bytes 1310720 | tf_op jit(solution)/shard_map/all_to_all | solution.py:19
  25.0 2.5 %collective-permute-start.6 = (bf16[512,512]{1,0:T(8,128)(2,1)S(1)}, bf16[512,512]{1,0:T(8,128)(2,1)S(1)}, u32[]{:S(2)}, u32[]{:S(2)}) collective-permute-start(bf16[512,512]{1,0:T(8,128)(2,1)S(1)} %copy-done.21), channel_id=1, source_target_pairs={{0,130},{2,128},{128,2},{130,0},{1,131},{3,129},{129,3},{131,1},{4... | collective-permute-start | bytes 1572872 | tf_op jit(solution)/shard_map/ppermute | solution.py:29
  29.8 13.6 %all-to-all-done = bf16[8,2,32,640]{3,2,1,0:T(8,128)(2,1)S(1)} async-done(((bf16[8,2,32,640]{3,2,1,0:T(8,128)(2,1)}), bf16[8,2,32,640]{3,2,1,0:T(8,128)(2,1)S(1)}, u32[]{:S(2)}, u32[]{:S(2)}) %all-to-all-start) | async-done | bytes 655392 | tf_op jit(solution)/shard_map/all_to_all | solution.py:19
  44.4 7.5 %collective-permute-done.4 = bf16[512,512]{1,0:T(8,128)(2,1)S(1)} collective-permute-done((bf16[512,512]{1,0:T(8,128)(2,1)S(1)}, bf16[512,512]{1,0:T(8,128)(2,1)S(1)}, u32[]{:S(2)}, u32[]{:S(2)}) %collective-permute-start.4) | collective-permute-done | bytes 524320 | tf_op jit(solution)/shard_map/ppermute | solution.py:29
  57.0 6.2 %collective-permute-done.1 = bf16[32,2304]{1,0:T(8,128)(2,1)S(1)} collective-permute-done((bf16[32,2304]{1,0:T(8,128)(2,1)S(1)}, bf16[32,2304]{1,0:T(8,128)(2,1)S(1)}, u32[]{:S(2)}, u32[]{:S(2)}) %collective-permute-start.1) | collective-permute-done | bytes 147488 | tf_op jit(solution)/shard_map/ppermute | solution.py:38
  64.0 3.8 %shard_map.102.x_ref = bf16[1024,2048]{1,0:T(8,128)(2,1)S(1)} custom-call(s32[1]{0:T(128)} %bitcast.me_ref, bf16[4,512,512]{2,1,0:T(8,128)(2,1)S(1)} %pad_maximum_fusion.mine_ref, bf16[4,512,512]{2,1,0:T(8,128)(2,1)} %collective-permute-done.7.theirs_ref, f32[1,2048]{1,0:T(1,128)S(1)} %bitcast.51), custom_call_target="tpu_custom_call" | custom-call | flops 26214400 | bytes 8388608 | tf_op jit(solution)/shard_map/pallas_call | solution.py:92
  67.7 2.1 copy-done.2
  71.0 2.2 copy-done.3
  74.5 1.8 shard_map.104
  78.0 3.8 %collective-permute-start.8 = (bf16[2,512,128]{2,1,0:T(8,128)(2,1)S(1)}, bf16[2,512,128]{2,1,0:T(8,128)(2,1)S(1)}, u32[]{:S(2)}, u32[]{:S(2)}) collective-permute-start(bf16[2,512,128]{2,1,0:T(8,128)(2,1)S(1)} %bitcast.41), channel_id=1, source_target_pairs={{0,8},{4,12},{8,16},{12,20},{16,24},{20,28},{24,32},{28,36},{32,40... | collective-permute-start | bytes 786440 | tf_op jit(solution)/shard_map/ppermute | solution.py:391
  81.8 5.1 %collective-permute-done.9 = bf16[2,512,128]{2,1,0:T(8,128)(2,1)S(1)} collective-permute-done((bf16[2,512,128]{2,1,0:T(8,128)(2,1)S(1)}, bf16[2,512,128]{2,1,0:T(8,128)(2,1)S(1)}, u32[]{:S(2)}, u32[]{:S(2)}) %collective-permute-start.9) | collective-permute-done | bytes 262176 | tf_op jit(solution)/shard_map/ppermute | solution.py:391
  86.9 16.1 %collective-permute-done.8 = bf16[2,512,128]{2,1,0:T(8,128)(2,1)S(1)} collective-permute-done((bf16[2,512,128]{2,1,0:T(8,128)(2,1)S(1)}, bf16[2,512,128]{2,1,0:T(8,128)(2,1)S(1)}, u32[]{:S(2)}, u32[]{:S(2)}) %collective-permute-start.8) | collective-permute-done | bytes 262176 | tf_op jit(solution)/shard_map/ppermute | solution.py:391
  104.3 3.5 %all-to-all-start.1 = ((bf16[4,8,2,32,256]{4,3,2,1,0:T(8,128)(2,1)}), bf16[4,8,2,32,256]{4,3,2,1,0:T(8,128)(2,1)S(1)}, u32[]{:S(2)}, u32[]{:S(2)}) async-start(bf16[4,8,2,32,256]{4,3,2,1,0:T(8,128)(2,1)} %broadcast_in_dim.24), calls=%async_computation.1 | async-start | bytes 2097152 | tf_op jit(solution)/shard_map/all_to_all | solution.py:19
  108.0 2.2 copy-done.4
  110.2 1.9 shard_map.103
  112.1 4.6 %shard_map.105.left_ref = bf16[2,256,256]{2,1,0:T(8,128)(2,1)S(1)} custom-call(s32[3]{0:T(128)S(1)} %pad_add_fusion.first_ref, bf16[2,512,256]{2,1,0:T(8,128)(2,1)S(1)} %bitcast.43, bf16[2,1536,128]{2,1,0:T(8,128)(2,1)S(1)} %pad_maximum_fusion.3.mine_ref, bf16[2,1536,128]{2,1,0:T(8,128)(2,1)} %collective-permute-done.10.other_ref), custom_call_target="tpu_custom_call" | custom-call | flops 671088640 | bytes 2097152 | tf_op jit(solution)/shard_map/pallas_call | solution.py:297
  117.4 6.4 %all-to-all-done.1 = bf16[4,8,2,32,256]{4,3,2,1,0:T(8,128)(2,1)S(1)} async-done(((bf16[4,8,2,32,256]{4,3,2,1,0:T(8,128)(2,1)}), bf16[4,8,2,32,256]{4,3,2,1,0:T(8,128)(2,1)S(1)}, u32[]{:S(2)}, u32[]{:S(2)}) %all-to-all-start.1) | async-done | bytes 1048608 | tf_op jit(solution)/shard_map/all_to_all | solution.py:19
  126.4 4.6 %shard_map.108.left_ref = bf16[2,256,256]{2,1,0:T(8,128)(2,1)S(1)} custom-call(s32[3]{0:T(128)S(1)} %pad_add_fusion.first_ref, bf16[2,512,256]{2,1,0:T(8,128)(2,1)S(1)} %bitcast.44, bf16[2,1536,128]{2,1,0:T(8,128)(2,1)S(1)} %pad_maximum_fusion.3.mine_ref, bf16[2,1536,128]{2,1,0:T(8,128)(2,1)} %collective-permute-done.10.other_ref), custom_call_target="tpu_custom_call" | custom-call | flops 671088640 | bytes 2097152 | tf_op jit(solution)/shard_map/pallas_call | solution.py:297
  133.4 2.7 %collective-permute-start.14 = (bf16[256,512]{1,0:T(8,128)(2,1)S(1)}, bf16[256,512]{1,0:T(8,128)(2,1)S(1)}, u32[]{:S(2)}, u32[]{:S(2)}) collective-permute-start(bf16[256,512]{1,0:T(8,128)(2,1)S(1)} %get-tuple-element.52), channel_id=1, source_target_pairs={{0,130},{2,128},{128,2},{130,0},{1,131},{3,129},{129,3},{131,1},{4... | collective-permute-start | bytes 786440 | tf_op jit(solution)/shard_map/ppermute | solution.py:29
  138.7 2.7 %collective-permute-start.26 = (bf16[256,512]{1,0:T(8,128)(2,1)S(1)}, bf16[256,512]{1,0:T(8,128)(2,1)S(1)}, u32[]{:S(2)}, u32[]{:S(2)}) collective-permute-start(bf16[256,512]{1,0:T(8,128)(2,1)S(1)} %get-tuple-element.55), channel_id=1, source_target_pairs={{0,130},{2,128},{128,2},{130,0},{1,131},{3,129},{129,3},{131,1},{4... | collective-permute-start | bytes 786440 | tf_op jit(solution)/shard_map/ppermute | solution.py:29
  141.3 3.5 %collective-permute-done.14 = bf16[256,512]{1,0:T(8,128)(2,1)S(1)} collective-permute-done((bf16[256,512]{1,0:T(8,128)(2,1)S(1)}, bf16[256,512]{1,0:T(8,128)(2,1)S(1)}, u32[]{:S(2)}, u32[]{:S(2)}) %collective-permute-start.14) | collective-permute-done | bytes 262176 | tf_op jit(solution)/shard_map/ppermute | solution.py:29
  146.5 4.4 %collective-permute-done.12 = bf16[256,512]{1,0:T(8,128)(2,1)S(1)} collective-permute-done((bf16[256,512]{1,0:T(8,128)(2,1)S(1)}, bf16[256,512]{1,0:T(8,128)(2,1)S(1)}, u32[]{:S(2)}, u32[]{:S(2)}) %collective-permute-start.12) | collective-permute-done | bytes 262176 | tf_op jit(solution)/shard_map/ppermute | solution.py:29
  151.1 3.0 %collective-permute-done.26 = bf16[256,512]{1,0:T(8,128)(2,1)S(1)} collective-permute-done((bf16[256,512]{1,0:T(8,128)(2,1)S(1)}, bf16[256,512]{1,0:T(8,128)(2,1)S(1)}, u32[]{:S(2)}, u32[]{:S(2)}) %collective-permute-start.26) | collective-permute-done | bytes 262176 | tf_op jit(solution)/shard_map/ppermute | solution.py:29
  154.1 2.3 collective-permute-done.25
  156.5 4.5 %collective-permute-done.24 = bf16[256,512]{1,0:T(8,128)(2,1)S(1)} collective-permute-done((bf16[256,512]{1,0:T(8,128)(2,1)S(1)}, bf16[256,512]{1,0:T(8,128)(2,1)S(1)}, u32[]{:S(2)}, u32[]{:S(2)}) %collective-permute-start.24) | collective-permute-done | bytes 262176 | tf_op jit(solution)/shard_map/ppermute | solution.py:29
  161.2 2.7 %collective-permute-start.29 = (bf16[256,512]{1,0:T(8,128)(2,1)S(1)}, bf16[256,512]{1,0:T(8,128)(2,1)S(1)}, u32[]{:S(2)}, u32[]{:S(2)}) collective-permute-start(bf16[256,512]{1,0:T(8,128)(2,1)S(1)} %fusion.7), channel_id=1, source_target_pairs={{0,130},{2,128},{128,2},{130,0},{1,131},{3,129},{129,3},{131,1},{4... | collective-permute-start | bytes 786440 | tf_op jit(solution)/shard_map/ppermute | solution.py:29
  163.8 2.1 collective-permute-start.27
  165.9 4.8 %collective-permute-done.29 = bf16[256,512]{1,0:T(8,128)(2,1)S(1)} collective-permute-done((bf16[256,512]{1,0:T(8,128)(2,1)S(1)}, bf16[256,512]{1,0:T(8,128)(2,1)S(1)}, u32[]{:S(2)}, u32[]{:S(2)}) %collective-permute-start.29) | collective-permute-done | bytes 262176 | tf_op jit(solution)/shard_map/ppermute | solution.py:29
  170.7 2.3 collective-permute-done.28
  173.0 3.4 %collective-permute-done.27 = bf16[256,512]{1,0:T(8,128)(2,1)S(1)} collective-permute-done((bf16[256,512]{1,0:T(8,128)(2,1)S(1)}, bf16[256,512]{1,0:T(8,128)(2,1)S(1)}, u32[]{:S(2)}, u32[]{:S(2)}) %collective-permute-start.27) | collective-permute-done | bytes 262176 | tf_op jit(solution)/shard_map/ppermute | solution.py:29
  176.6 2.7 %collective-permute-start.17 = (bf16[256,512]{1,0:T(8,128)(2,1)S(1)}, bf16[256,512]{1,0:T(8,128)(2,1)S(1)}, u32[]{:S(2)}, u32[]{:S(2)}) collective-permute-start(bf16[256,512]{1,0:T(8,128)(2,1)S(1)} %fusion.15), channel_id=1, source_target_pairs={{0,130},{2,128},{128,2},{130,0},{1,131},{3,129},{129,3},{131,1},{4... | collective-permute-start | bytes 786440 | tf_op jit(solution)/shard_map/ppermute | solution.py:29
  179.3 2.1 collective-permute-start.15
  181.4 5.1 %collective-permute-done.17 = bf16[256,512]{1,0:T(8,128)(2,1)S(1)} collective-permute-done((bf16[256,512]{1,0:T(8,128)(2,1)S(1)}, bf16[256,512]{1,0:T(8,128)(2,1)S(1)}, u32[]{:S(2)}, u32[]{:S(2)}) %collective-permute-start.17) | collective-permute-done | bytes 262176 | tf_op jit(solution)/shard_map/ppermute | solution.py:29
  186.5 1.9 collective-permute-done.16
  188.4 4.9 %collective-permute-done.15 = bf16[256,512]{1,0:T(8,128)(2,1)S(1)} collective-permute-done((bf16[256,512]{1,0:T(8,128)(2,1)S(1)}, bf16[256,512]{1,0:T(8,128)(2,1)S(1)}, u32[]{:S(2)}, u32[]{:S(2)}) %collective-permute-start.15) | collective-permute-done | bytes 262176 | tf_op jit(solution)/shard_map/ppermute | solution.py:29
  193.8 3.7 %copy-done = bf16[64,32,2304]{2,1,0:T(8,128)(2,1)S(1)} copy-done((bf16[64,32,2304]{2,1,0:T(8,128)(2,1)S(1)}, bf16[64,32,2304]{2,1,0:T(8,128)(2,1)}, u32[]{:S(2)}) %copy-start) | copy-done | bytes 9437208
  197.5 7.9 %shard_map.110 = (f32[512,1024]{1,0:T(8,128)S(1)}, bf16[512,1024]{1,0:T(8,128)(2,1)S(1)}) custom-call(s32[1]{0:T(128)} %bitcast.me_ref, bf16[4,256,512]{2,1,0:T(8,128)(2,1)S(1)} %pad_maximum_fusion.2.mine_ref, bf16[4,256,512]{2,1,0:T(8,128)(2,1)S(1)} %collective-permute-done.30.theirs_ref, f32[1,2048]{1,0:T(1,128)S(1)} %bitcast.49, ...), custom_call_target="tpu_custom_call" | custom-call | flops 4831838208 | bytes 13631488 | tf_op jit(solution)/shard_map/pallas_call | solution.py:164
  206.0 9.0 %shard_map.107 = (f32[512,1024]{1,0:T(8,128)S(1)}, bf16[512,1024]{1,0:T(8,128)(2,1)S(1)}) custom-call(s32[1]{0:T(128)} %bitcast.me_ref, bf16[4,256,512]{2,1,0:T(8,128)(2,1)S(1)} %pad_maximum_fusion.1.mine_ref, bf16[4,256,512]{2,1,0:T(8,128)(2,1)} %collective-permute-done.18.theirs_ref, f32[1,2048]{1,0:T(1,128)S(1)} %bitcast.50, ...), custom_call_target="tpu_custom_call" | custom-call | flops 4831838208 | bytes 13631488 | tf_op jit(solution)/shard_map/pallas_call | solution.py:164
  215.6 2.7 %collective-permute-start.34 = (bf16[256,512]{1,0:T(8,128)(2,1)S(1)}, bf16[256,512]{1,0:T(8,128)(2,1)S(1)}, u32[]{:S(2)}, u32[]{:S(2)}) collective-permute-start(bf16[256,512]{1,0:T(8,128)(2,1)S(1)} %get-tuple-element.49), channel_id=1, source_target_pairs={{0,130},{2,128},{128,2},{130,0},{1,131},{3,129},{129,3},{131,1},{4... | collective-permute-start | bytes 786440 | tf_op jit(solution)/shard_map/ppermute | solution.py:29
  218.2 2.1 collective-permute-start.32
  220.9 2.7 %collective-permute-start.22 = (bf16[256,512]{1,0:T(8,128)(2,1)S(1)}, bf16[256,512]{1,0:T(8,128)(2,1)S(1)}, u32[]{:S(2)}, u32[]{:S(2)}) collective-permute-start(bf16[256,512]{1,0:T(8,128)(2,1)S(1)} %get-tuple-element.46), channel_id=1, source_target_pairs={{0,130},{2,128},{128,2},{130,0},{1,131},{3,129},{129,3},{131,1},{4... | collective-permute-start | bytes 786440 | tf_op jit(solution)/shard_map/ppermute | solution.py:29
  223.6 2.6 %collective-permute-done.34 = bf16[256,512]{1,0:T(8,128)(2,1)S(1)} collective-permute-done((bf16[256,512]{1,0:T(8,128)(2,1)S(1)}, bf16[256,512]{1,0:T(8,128)(2,1)S(1)}, u32[]{:S(2)}, u32[]{:S(2)}) %collective-permute-start.34) | collective-permute-done | bytes 262176 | tf_op jit(solution)/shard_map/ppermute | solution.py:29
  227.4 5.8 %collective-permute-done.32 = bf16[256,512]{1,0:T(8,128)(2,1)S(1)} collective-permute-done((bf16[256,512]{1,0:T(8,128)(2,1)S(1)}, bf16[256,512]{1,0:T(8,128)(2,1)S(1)}, u32[]{:S(2)}, u32[]{:S(2)}) %collective-permute-start.32) | collective-permute-done | bytes 262176 | tf_op jit(solution)/shard_map/ppermute | solution.py:29
  233.4 3.4 %collective-permute-done.22 = bf16[256,512]{1,0:T(8,128)(2,1)S(1)} collective-permute-done((bf16[256,512]{1,0:T(8,128)(2,1)S(1)}, bf16[256,512]{1,0:T(8,128)(2,1)S(1)}, u32[]{:S(2)}, u32[]{:S(2)}) %collective-permute-start.22) | collective-permute-done | bytes 262176 | tf_op jit(solution)/shard_map/ppermute | solution.py:29
  236.8 1.9 collective-permute-done.21
  238.7 4.9 %collective-permute-done.20 = bf16[256,512]{1,0:T(8,128)(2,1)S(1)} collective-permute-done((bf16[256,512]{1,0:T(8,128)(2,1)S(1)}, bf16[256,512]{1,0:T(8,128)(2,1)S(1)}, u32[]{:S(2)}, u32[]{:S(2)}) %collective-permute-start.20) | collective-permute-done | bytes 262176 | tf_op jit(solution)/shard_map/ppermute | solution.py:29
  (124 shorter events, 34.7 us)
Async XLA Ops:
  9.4 15.6 %copy-start.21 = (bf16[512,512]{1,0:T(8,128)(2,1)S(1)}, bf16[512,512]{1,0:T(8,128)(2,1)}, u32[]{:S(2)}) copy-start(bf16[512,512]{1,0:T(8,128)(2,1)} %param.10) | copy-start | bytes 1572868
  9.5 3.8 %collective-permute-start.2 = (bf16[32,640]{1,0:T(8,128)(2,1)S(1)}, bf16[32,640]{1,0:T(8,128)(2,1)S(1)}, u32[]{:S(2)}, u32[]{:S(2)}) collective-permute-start(bf16[32,640]{1,0:T(8,128)(2,1)S(1)} %get-tuple-element.23), channel_id=1, source_target_pairs={{0,0},{1,128},{128,1},{129,129},{2,2},{3,130},{130,3},{131,131},{4... | collective-permute-start | bytes 122888 | tf_op jit(solution)/shard_map/ppermute | solution.py:38
  10.3 5.2 %collective-permute-start.3 = (bf16[32,640]{1,0:T(8,128)(2,1)S(1)}, bf16[32,640]{1,0:T(8,128)(2,1)S(1)}, u32[]{:S(2)}, u32[]{:S(2)}) collective-permute-start(bf16[32,640]{1,0:T(8,128)(2,1)S(1)} %get-tuple-element.24), channel_id=1, source_target_pairs={{0,1},{1,129},{128,0},{129,128},{2,3},{3,131},{130,2},{131,130},{4... | collective-permute-start | bytes 122888 | tf_op jit(solution)/shard_map/ppermute | solution.py:38
  16.5 27.0 %all-to-all-start = ((bf16[8,2,32,640]{3,2,1,0:T(8,128)(2,1)}), bf16[8,2,32,640]{3,2,1,0:T(8,128)(2,1)S(1)}, u32[]{:S(2)}, u32[]{:S(2)}) async-start(bf16[8,2,32,640]{3,2,1,0:T(8,128)(2,1)} %broadcast_in_dim.10), calls=%async_computation | async-start | bytes 1310720 | tf_op jit(solution)/shard_map/all_to_all | solution.py:19
  25.0 45.9 %all-gather.4.cloned.1.call-start = ((), (), s32[]{:S(2)}) async-start(), calls=%async_computation.2 | async-start | bytes 1966080 | tf_op jit(solution)/shard_map/all_gather | solution.py:381
  25.0 19.3 %collective-permute-start.6 = (bf16[512,512]{1,0:T(8,128)(2,1)S(1)}, bf16[512,512]{1,0:T(8,128)(2,1)S(1)}, u32[]{:S(2)}, u32[]{:S(2)}) collective-permute-start(bf16[512,512]{1,0:T(8,128)(2,1)S(1)} %copy-done.21), channel_id=1, source_target_pairs={{0,130},{2,128},{128,2},{130,0},{1,131},{3,129},{129,3},{131,1},{4... | collective-permute-start | bytes 1572872 | tf_op jit(solution)/shard_map/ppermute | solution.py:29
  27.6 16.8 %collective-permute-start.5 = (bf16[512,512]{1,0:T(8,128)(2,1)S(1)}, bf16[512,512]{1,0:T(8,128)(2,1)S(1)}, u32[]{:S(2)}, u32[]{:S(2)}) collective-permute-start(bf16[512,512]{1,0:T(8,128)(2,1)S(1)} %copy-done.21), channel_id=1, source_target_pairs={{0,128},{2,130},{128,0},{130,2},{1,129},{3,131},{129,1},{131,3},{4... | collective-permute-start | bytes 1572872 | tf_op jit(solution)/shard_map/ppermute | solution.py:29
  28.2 23.7 %collective-permute-start.4 = (bf16[512,512]{1,0:T(8,128)(2,1)S(1)}, bf16[512,512]{1,0:T(8,128)(2,1)S(1)}, u32[]{:S(2)}, u32[]{:S(2)}) collective-permute-start(bf16[512,512]{1,0:T(8,128)(2,1)S(1)} %copy-done.21), channel_id=1, source_target_pairs={{0,2},{2,0},{128,130},{130,128},{1,3},{3,1},{129,131},{131,129},{4... | collective-permute-start | bytes 1572872 | tf_op jit(solution)/shard_map/ppermute | solution.py:29
  43.4 8.4 %copy-start.18 = (bf16[8,2,32,640]{3,2,1,0:T(8,128)(2,1)}, bf16[8,2,32,640]{3,2,1,0:T(8,128)(2,1)S(1)}, u32[]{:S(2)}) copy-start(bf16[8,2,32,640]{3,2,1,0:T(8,128)(2,1)S(1)} %all-to-all-done) | copy-start | bytes 1966084
  44.3 149.5 %all-gather.6.cloned.1.call-start = ((), (), s32[]{:S(2)}) async-start(), calls=%async_computation.3 | async-start | bytes 9732096 | tf_op jit(solution)/shard_map/all_gather | solution.py:384
  44.4 7.5 %copy-start.23 = (bf16[512,512]{1,0:T(8,128)(2,1)}, bf16[512,512]{1,0:T(8,128)(2,1)S(1)}, u32[]{:S(2)}) copy-start(bf16[512,512]{1,0:T(8,128)(2,1)S(1)} %collective-permute-done.5) | copy-start | bytes 1572868
  52.7 11.3 %copy-start.15 = (f32[2048]{0:T(1024)S(1)}, f32[2048]{0:T(1024)}, u32[]{:S(2)}) copy-start(f32[2048]{0:T(1024)} %param.11) | copy-start | bytes 24580
  54.2 9.7 %collective-permute-start.7 = (bf16[4,512,512]{2,1,0:T(8,128)(2,1)S(1)}, bf16[4,512,512]{2,1,0:T(8,128)(2,1)}, u32[]{:S(2)}, u32[]{:S(2)}) collective-permute-start(bf16[4,512,512]{2,1,0:T(8,128)(2,1)S(1)} %pad_maximum_fusion.mine_ref), channel_id=1, source_target_pairs={{0,1},{1,0},{2,3},{3,2},{4,5},{5,4},{6,7},{7,6},{8,9},{9,8},{10,11... | collective-permute-start | bytes 6291464 | tf_op jit(solution)/shard_map/ppermute | solution.py:25
  54.5 2.5 collective-permute-start
  55.2 8.0 %collective-permute-start.1 = (bf16[32,2304]{1,0:T(8,128)(2,1)S(1)}, bf16[32,2304]{1,0:T(8,128)(2,1)S(1)}, u32[]{:S(2)}, u32[]{:S(2)}) collective-permute-start(bf16[32,2304]{1,0:T(8,128)(2,1)S(1)} %get-tuple-element.22), channel_id=1, source_target_pairs={{0,1},{1,129},{128,0},{129,128},{2,3},{3,131},{130,2},{131,130},{4... | collective-permute-start | bytes 442376 | tf_op jit(solution)/shard_map/ppermute | solution.py:38
  76.4 26.8 %slice-start = ((bf16[8,2,32,640]{3,2,1,0:T(8,128)(2,1)}), bf16[8,2,32,256]{3,2,1,0:T(8,128)(2,1)S(1)}, s32[]{:S(2)}) async-start(bf16[8,2,32,640]{3,2,1,0:T(8,128)(2,1)} %copy-done.18), calls=%async_computation.4 | async-start | bytes 524288 | tf_op jit(solution)/shard_map/slice | solution.py:374
  76.4 10.5 %collective-permute-start.9 = (bf16[2,512,128]{2,1,0:T(8,128)(2,1)S(1)}, bf16[2,512,128]{2,1,0:T(8,128)(2,1)S(1)}, u32[]{:S(2)}, u32[]{:S(2)}) collective-permute-start(bf16[2,512,128]{2,1,0:T(8,128)(2,1)S(1)} %bitcast.40), channel_id=1, source_target_pairs={{0,4},{4,8},{8,12},{12,16},{16,20},{20,24},{24,28},{28,32},{32,36}... | collective-permute-start | bytes 786440 | tf_op jit(solution)/shard_map/ppermute | solution.py:391
  78.0 24.9 %collective-permute-start.8 = (bf16[2,512,128]{2,1,0:T(8,128)(2,1)S(1)}, bf16[2,512,128]{2,1,0:T(8,128)(2,1)S(1)}, u32[]{:S(2)}, u32[]{:S(2)}) collective-permute-start(bf16[2,512,128]{2,1,0:T(8,128)(2,1)S(1)} %bitcast.41), channel_id=1, source_target_pairs={{0,8},{4,12},{8,16},{12,20},{16,24},{20,28},{24,32},{28,36},{32,40... | collective-permute-start | bytes 786440 | tf_op jit(solution)/shard_map/ppermute | solution.py:391
  103.1 9.0 %collective-permute-start.10 = (bf16[2,1536,128]{2,1,0:T(8,128)(2,1)S(1)}, bf16[2,1536,128]{2,1,0:T(8,128)(2,1)}, u32[]{:S(2)}, u32[]{:S(2)}) collective-permute-start(bf16[2,1536,128]{2,1,0:T(8,128)(2,1)S(1)} %pad_maximum_fusion.3.mine_ref), channel_id=1, source_target_pairs={{0,1},{1,0},{2,3},{3,2},{4,5},{5,4},{6,7},{7,6},{8,9},{9,8},{10,11... | collective-permute-start | bytes 2359304 | tf_op jit(solution)/shard_map/ppermute | solution.py:25
  104.3 19.5 %all-to-all-start.1 = ((bf16[4,8,2,32,256]{4,3,2,1,0:T(8,128)(2,1)}), bf16[4,8,2,32,256]{4,3,2,1,0:T(8,128)(2,1)S(1)}, u32[]{:S(2)}, u32[]{:S(2)}) async-start(bf16[4,8,2,32,256]{4,3,2,1,0:T(8,128)(2,1)} %broadcast_in_dim.24), calls=%async_computation.1 | async-start | bytes 2097152 | tf_op jit(solution)/shard_map/all_to_all | solution.py:19
  125.0 7.9 %collective-permute-start.11 = (bf16[512,1024]{1,0:T(8,128)(2,1)S(1)}, bf16[512,1024]{1,0:T(8,128)(2,1)S(1)}, u32[]{:S(2)}, u32[]{:S(2)}) collective-permute-start(bf16[512,1024]{1,0:T(8,128)(2,1)S(1)} %get-tuple-element.28), channel_id=1, source_target_pairs={{0,1},{1,0},{2,3},{3,2},{4,5},{5,4},{6,7},{7,6},{8,9},{9,8},{10,11... | collective-permute-start | bytes 3145736 | tf_op jit(solution)/shard_map/ppermute | solution.py:25
  132.2 6.0 %collective-permute-start.23 = (bf16[512,1024]{1,0:T(8,128)(2,1)S(1)}, bf16[512,1024]{1,0:T(8,128)(2,1)S(1)}, u32[]{:S(2)}, u32[]{:S(2)}) collective-permute-start(bf16[512,1024]{1,0:T(8,128)(2,1)S(1)} %get-tuple-element.34), channel_id=1, source_target_pairs={{0,1},{1,0},{2,3},{3,2},{4,5},{5,4},{6,7},{7,6},{8,9},{9,8},{10,11... | collective-permute-start | bytes 3145736 | tf_op jit(solution)/shard_map/ppermute | solution.py:25
  133.4 11.4 %collective-permute-start.14 = (bf16[256,512]{1,0:T(8,128)(2,1)S(1)}, bf16[256,512]{1,0:T(8,128)(2,1)S(1)}, u32[]{:S(2)}, u32[]{:S(2)}) collective-permute-start(bf16[256,512]{1,0:T(8,128)(2,1)S(1)} %get-tuple-element.52), channel_id=1, source_target_pairs={{0,130},{2,128},{128,2},{130,0},{1,131},{3,129},{129,3},{131,1},{4... | collective-permute-start | bytes 786440 | tf_op jit(solution)/shard_map/ppermute | solution.py:29
  136.0 10.5 %collective-permute-start.13 = (bf16[256,512]{1,0:T(8,128)(2,1)S(1)}, bf16[256,512]{1,0:T(8,128)(2,1)S(1)}, u32[]{:S(2)}, u32[]{:S(2)}) collective-permute-start(bf16[256,512]{1,0:T(8,128)(2,1)S(1)} %get-tuple-element.53), channel_id=1, source_target_pairs={{0,128},{2,130},{128,0},{130,2},{1,129},{3,131},{129,1},{131,3},{4... | collective-permute-start | bytes 786440 | tf_op jit(solution)/shard_map/ppermute | solution.py:29
  136.3 14.6 %collective-permute-start.12 = (bf16[256,512]{1,0:T(8,128)(2,1)S(1)}, bf16[256,512]{1,0:T(8,128)(2,1)S(1)}, u32[]{:S(2)}, u32[]{:S(2)}) collective-permute-start(bf16[256,512]{1,0:T(8,128)(2,1)S(1)} %get-tuple-element.51), channel_id=1, source_target_pairs={{0,2},{2,0},{128,130},{130,128},{1,3},{3,1},{129,131},{131,129},{4... | collective-permute-start | bytes 786440 | tf_op jit(solution)/shard_map/ppermute | solution.py:29
  138.7 15.5 %collective-permute-start.26 = (bf16[256,512]{1,0:T(8,128)(2,1)S(1)}, bf16[256,512]{1,0:T(8,128)(2,1)S(1)}, u32[]{:S(2)}, u32[]{:S(2)}) collective-permute-start(bf16[256,512]{1,0:T(8,128)(2,1)S(1)} %get-tuple-element.55), channel_id=1, source_target_pairs={{0,130},{2,128},{128,2},{130,0},{1,131},{3,129},{129,3},{131,1},{4... | collective-permute-start | bytes 786440 | tf_op jit(solution)/shard_map/ppermute | solution.py:29
  141.3 15.1 %collective-permute-start.25 = (bf16[256,512]{1,0:T(8,128)(2,1)S(1)}, bf16[256,512]{1,0:T(8,128)(2,1)S(1)}, u32[]{:S(2)}, u32[]{:S(2)}) collective-permute-start(bf16[256,512]{1,0:T(8,128)(2,1)S(1)} %get-tuple-element.56), channel_id=1, source_target_pairs={{0,128},{2,130},{128,0},{130,2},{1,129},{3,131},{129,1},{131,3},{4... | collective-permute-start | bytes 786440 | tf_op jit(solution)/shard_map/ppermute | solution.py:29
  144.8 16.2 %collective-permute-start.24 = (bf16[256,512]{1,0:T(8,128)(2,1)S(1)}, bf16[256,512]{1,0:T(8,128)(2,1)S(1)}, u32[]{:S(2)}, u32[]{:S(2)}) collective-permute-start(bf16[256,512]{1,0:T(8,128)(2,1)S(1)} %get-tuple-element.54), channel_id=1, source_target_pairs={{0,2},{2,0},{128,130},{130,128},{1,3},{3,1},{129,131},{131,129},{4... | collective-permute-start | bytes 786440 | tf_op jit(solution)/shard_map/ppermute | solution.py:29
  161.1 15.2 %copy-start.19 = (bf16[256,512]{1,0:T(8,128)(2,1)}, bf16[256,512]{1,0:T(8,128)(2,1)S(1)}, u32[]{:S(2)}) copy-start(bf16[256,512]{1,0:T(8,128)(2,1)S(1)} %fusion.7) | copy-start | bytes 786436
  161.2 9.6 %collective-permute-start.29 = (bf16[256,512]{1,0:T(8,128)(2,1)S(1)}, bf16[256,512]{1,0:T(8,128)(2,1)S(1)}, u32[]{:S(2)}, u32[]{:S(2)}) collective-permute-start(bf16[256,512]{1,0:T(8,128)(2,1)S(1)} %fusion.7), channel_id=1, source_target_pairs={{0,130},{2,128},{128,2},{130,0},{1,131},{3,129},{129,3},{131,1},{4... | collective-permute-start | bytes 786440 | tf_op jit(solution)/shard_map/ppermute | solution.py:29
  163.8 9.2 %collective-permute-start.28 = (bf16[256,512]{1,0:T(8,128)(2,1)S(1)}, bf16[256,512]{1,0:T(8,128)(2,1)S(1)}, u32[]{:S(2)}, u32[]{:S(2)}) collective-permute-start(bf16[256,512]{1,0:T(8,128)(2,1)S(1)} %fusion.7), channel_id=1, source_target_pairs={{0,128},{2,130},{128,0},{130,2},{1,129},{3,131},{129,1},{131,3},{4... | collective-permute-start | bytes 786440 | tf_op jit(solution)/shard_map/ppermute | solution.py:29
  163.8 12.5 %collective-permute-start.27 = (bf16[256,512]{1,0:T(8,128)(2,1)S(1)}, bf16[256,512]{1,0:T(8,128)(2,1)S(1)}, u32[]{:S(2)}, u32[]{:S(2)}) collective-permute-start(bf16[256,512]{1,0:T(8,128)(2,1)S(1)} %fusion.7), channel_id=1, source_target_pairs={{0,2},{2,0},{128,130},{130,128},{1,3},{3,1},{129,131},{131,129},{4... | collective-permute-start | bytes 786440 | tf_op jit(solution)/shard_map/ppermute | solution.py:29
  176.4 17.5 %copy-start.14 = (f32[2048]{0:T(1024)S(1)}, f32[2048]{0:T(1024)}, u32[]{:S(2)}) copy-start(f32[2048]{0:T(1024)} %param.16) | copy-start | bytes 24580
  176.5 17.3 %collective-permute-start.30 = (bf16[4,256,512]{2,1,0:T(8,128)(2,1)S(1)}, bf16[4,256,512]{2,1,0:T(8,128)(2,1)S(1)}, u32[]{:S(2)}, u32[]{:S(2)}) collective-permute-start(bf16[4,256,512]{2,1,0:T(8,128)(2,1)S(1)} %pad_maximum_fusion.2.mine_ref), channel_id=1, source_target_pairs={{0,1},{1,0},{2,3},{3,2},{4,5},{5,4},{6,7},{7,6},{8,9},{9,8},{10,11... | collective-permute-start | bytes 3145736 | tf_op jit(solution)/shard_map/ppermute | solution.py:25
  176.6 9.9 %collective-permute-start.17 = (bf16[256,512]{1,0:T(8,128)(2,1)S(1)}, bf16[256,512]{1,0:T(8,128)(2,1)S(1)}, u32[]{:S(2)}, u32[]{:S(2)}) collective-permute-start(bf16[256,512]{1,0:T(8,128)(2,1)S(1)} %fusion.15), channel_id=1, source_target_pairs={{0,130},{2,128},{128,2},{130,0},{1,131},{3,129},{129,3},{131,1},{4... | collective-permute-start | bytes 786440 | tf_op jit(solution)/shard_map/ppermute | solution.py:29
  179.3 9.2 %collective-permute-start.16 = (bf16[256,512]{1,0:T(8,128)(2,1)S(1)}, bf16[256,512]{1,0:T(8,128)(2,1)S(1)}, u32[]{:S(2)}, u32[]{:S(2)}) collective-permute-start(bf16[256,512]{1,0:T(8,128)(2,1)S(1)} %fusion.15), channel_id=1, source_target_pairs={{0,128},{2,130},{128,0},{130,2},{1,129},{3,131},{129,1},{131,3},{4... | collective-permute-start | bytes 786440 | tf_op jit(solution)/shard_map/ppermute | solution.py:29
  179.3 14.1 %collective-permute-start.15 = (bf16[256,512]{1,0:T(8,128)(2,1)S(1)}, bf16[256,512]{1,0:T(8,128)(2,1)S(1)}, u32[]{:S(2)}, u32[]{:S(2)}) collective-permute-start(bf16[256,512]{1,0:T(8,128)(2,1)S(1)} %fusion.15), channel_id=1, source_target_pairs={{0,2},{2,0},{128,130},{130,128},{1,3},{3,1},{129,131},{131,129},{4... | collective-permute-start | bytes 786440 | tf_op jit(solution)/shard_map/ppermute | solution.py:29
  193.5 12.5 %collective-permute-start.18 = (bf16[4,256,512]{2,1,0:T(8,128)(2,1)S(1)}, bf16[4,256,512]{2,1,0:T(8,128)(2,1)}, u32[]{:S(2)}, u32[]{:S(2)}) collective-permute-start(bf16[4,256,512]{2,1,0:T(8,128)(2,1)S(1)} %pad_maximum_fusion.1.mine_ref), channel_id=1, source_target_pairs={{0,1},{1,0},{2,3},{3,2},{4,5},{5,4},{6,7},{7,6},{8,9},{9,8},{10,11... | collective-permute-start | bytes 3145736 | tf_op jit(solution)/shard_map/ppermute | solution.py:25
  197.5 8.4 %copy-start.1 = (bf16[64,32,2304]{2,1,0:T(8,128)(2,1)S(1)}, bf16[64,32,2304]{2,1,0:T(8,128)(2,1)}, u32[]{:S(2)}) copy-start(bf16[64,32,2304]{2,1,0:T(8,128)(2,1)} %all-gather.6.cloned.1.call-done) | copy-start | bytes 28311556
  205.4 9.7 %collective-permute-start.31 = (bf16[512,1024]{1,0:T(8,128)(2,1)S(1)}, bf16[512,1024]{1,0:T(8,128)(2,1)S(1)}, u32[]{:S(2)}, u32[]{:S(2)}) collective-permute-start(bf16[512,1024]{1,0:T(8,128)(2,1)S(1)} %get-tuple-element.36), channel_id=1, source_target_pairs={{0,1},{1,0},{2,3},{3,2},{4,5},{5,4},{6,7},{7,6},{8,9},{9,8},{10,11... | collective-permute-start | bytes 3145736 | tf_op jit(solution)/shard_map/ppermute | solution.py:25
  214.9 5.4 %collective-permute-start.19 = (bf16[512,1024]{1,0:T(8,128)(2,1)S(1)}, bf16[512,1024]{1,0:T(8,128)(2,1)S(1)}, u32[]{:S(2)}, u32[]{:S(2)}) collective-permute-start(bf16[512,1024]{1,0:T(8,128)(2,1)S(1)} %get-tuple-element.31), channel_id=1, source_target_pairs={{0,1},{1,0},{2,3},{3,2},{4,5},{5,4},{6,7},{7,6},{8,9},{9,8},{10,11... | collective-permute-start | bytes 3145736 | tf_op jit(solution)/shard_map/ppermute | solution.py:25
  215.6 10.6 %collective-permute-start.34 = (bf16[256,512]{1,0:T(8,128)(2,1)S(1)}, bf16[256,512]{1,0:T(8,128)(2,1)S(1)}, u32[]{:S(2)}, u32[]{:S(2)}) collective-permute-start(bf16[256,512]{1,0:T(8,128)(2,1)S(1)} %get-tuple-element.49), channel_id=1, source_target_pairs={{0,130},{2,128},{128,2},{130,0},{1,131},{3,129},{129,3},{131,1},{4... | collective-permute-start | bytes 786440 | tf_op jit(solution)/shard_map/ppermute | solution.py:29
  218.2 9.2 %collective-permute-start.33 = (bf16[256,512]{1,0:T(8,128)(2,1)S(1)}, bf16[256,512]{1,0:T(8,128)(2,1)S(1)}, u32[]{:S(2)}, u32[]{:S(2)}) collective-permute-start(bf16[256,512]{1,0:T(8,128)(2,1)S(1)} %get-tuple-element.50), channel_id=1, source_target_pairs={{0,128},{2,130},{128,0},{130,2},{1,129},{3,131},{129,1},{131,3},{4... | collective-permute-start | bytes 786440 | tf_op jit(solution)/shard_map/ppermute | solution.py:29
  218.2 14.9 %collective-permute-start.32 = (bf16[256,512]{1,0:T(8,128)(2,1)S(1)}, bf16[256,512]{1,0:T(8,128)(2,1)S(1)}, u32[]{:S(2)}, u32[]{:S(2)}) collective-permute-start(bf16[256,512]{1,0:T(8,128)(2,1)S(1)} %get-tuple-element.48), channel_id=1, source_target_pairs={{0,2},{2,0},{128,130},{130,128},{1,3},{3,1},{129,131},{131,129},{4... | collective-permute-start | bytes 786440 | tf_op jit(solution)/shard_map/ppermute | solution.py:29
  220.4 12.8 %copy-start.20 = (bf16[256,512]{1,0:T(8,128)(2,1)S(1)}, bf16[256,512]{1,0:T(8,128)(2,1)}, u32[]{:S(2)}) copy-start(bf16[256,512]{1,0:T(8,128)(2,1)} %copy-done.19) | copy-start | bytes 786436
  220.9 15.9 %collective-permute-start.22 = (bf16[256,512]{1,0:T(8,128)(2,1)S(1)}, bf16[256,512]{1,0:T(8,128)(2,1)S(1)}, u32[]{:S(2)}, u32[]{:S(2)}) collective-permute-start(bf16[256,512]{1,0:T(8,128)(2,1)S(1)} %get-tuple-element.46), channel_id=1, source_target_pairs={{0,130},{2,128},{128,2},{130,0},{1,131},{3,129},{129,3},{131,1},{4... | collective-permute-start | bytes 786440 | tf_op jit(solution)/shard_map/ppermute | solution.py:29
  223.6 15.1 %collective-permute-start.21 = (bf16[256,512]{1,0:T(8,128)(2,1)S(1)}, bf16[256,512]{1,0:T(8,128)(2,1)S(1)}, u32[]{:S(2)}, u32[]{:S(2)}) collective-permute-start(bf16[256,512]{1,0:T(8,128)(2,1)S(1)} %get-tuple-element.47), channel_id=1, source_target_pairs={{0,128},{2,130},{128,0},{130,2},{1,129},{3,131},{129,1},{131,3},{4... | collective-permute-start | bytes 786440 | tf_op jit(solution)/shard_map/ppermute | solution.py:29
  226.2 17.4 %collective-permute-start.20 = (bf16[256,512]{1,0:T(8,128)(2,1)S(1)}, bf16[256,512]{1,0:T(8,128)(2,1)S(1)}, u32[]{:S(2)}, u32[]{:S(2)}) collective-permute-start(bf16[256,512]{1,0:T(8,128)(2,1)S(1)} %get-tuple-element.45), channel_id=1, source_target_pairs={{0,2},{2,0},{128,130},{130,128},{1,3},{3,1},{129,131},{131,129},{4... | collective-permute-start | bytes 786440 | tf_op jit(solution)/shard_map/ppermute | solution.py:29
  (17 other events, 33.6 us)
Sparse Core Ops, SparseCore 0:
  44.5 26.4 all-gather.3
  73.5 102.9 all-gather.5

commit v5 on v4

--- a/solution.py
+++ b/solution.py
@@ -49,7 +49,7 @@
     return mine, other_core(mine)
 
 
-def call(kernel, grid, scalars, in_specs, out_specs, out_shape, scratch=(), flops=0, moved=0):
+def call(kernel, grid, scalars, in_specs, out_specs, out_shape, scratch=(), flops=0, moved=0, grant=32):
     return pl.pallas_call(
         kernel,
         grid_spec=pltpu.PrefetchScalarGridSpec(
@@ -60,7 +60,7 @@
             scratch_shapes=scratch,
         ),
         out_shape=out_shape,
-        compiler_params=pltpu.CompilerParams(vmem_limit_bytes=32 * 1024 * 1024),
+        compiler_params=pltpu.CompilerParams(vmem_limit_bytes=grant * 1024 * 1024),
         cost_estimate=pl.CostEstimate(flops=flops, bytes_accessed=moved, transcendentals=0),
     )
 
@@ -205,6 +205,7 @@
         jax.ShapeDtypeStruct((n, width), jnp.bfloat16),
         flops=2 * n * d * width,
         moved=2 * (n * d + d * width + n * width),
+        grant=58,
     )(left, weights)
 
 

time: 252 us -> 250 us (level)
  local copies, waits for them, and re-layouts: 20.4 us -> 13.7 us
  Pallas kernels: 35.9 us -> 40 us
    unnamed x50 -> x42, local copies, waits for them, and re-layouts: 17.2 us -> 10.5 us
    pallas_call x2, Pallas kernels: 3.69 us -> 9.82 us  [projected(): call(kernel, (n // step,), 0, [pl.BlockSpec((step, d), lambda i: (i, 0)),...]
  transfers between devices with their start and end apart: 39 -> 39, of which waited for: 25 -> 25; matrix products, arithmetic and copies ran while one was open for 3% -> 3% of each run, Pallas kernels for 14% -> 16%
where the time goes in v5:
time: 250 us; the launch traced here: 249 us
  waiting for transfers between devices  117 us (47%)
  starting transfers between devices  57.8 us (23%)
  Pallas kernels  40 us (16%)
  between operations  13.8 us (6%)
  local copies, waits for them, and re-layouts  13.7 us (5%)
  other arithmetic  7.37 us (3%)
    ppermute x21, waiting for transfers between devices, column_partner(): return lax.ppermute(value, ('yl', 'yh'), [(i, i ^ flip) for i in range(4)])  66.5 us
    ppermute x21, starting transfers between devices, column_partner(): return lax.ppermute(value, ('yl', 'yh'), [(i, i ^ flip) for i in range(4)])  31.9 us
    ppermute x2, waiting for transfers between devices, per_device(): lax.ppermute(fresh, PLANE, [(i, (i + step) % plane) for i in range(plane)])  21.1 us
    all_to_all x2, waiting for transfers between devices, spread(): lax.all_to_all(jnp.broadcast_to(value[None], (length, *value.shape)), axi...  19.8 us
    pallas_call x2, Pallas kernels, unit_terms(): call(kernel, (steps + 2,), 1, [whole(mine.shape), whole(mine.shape), whol...  16.9 us
    all_to_all x2, starting transfers between devices, spread(): lax.all_to_all(jnp.broadcast_to(value[None], (length, *value.shape)), axi...  12.1 us
    unnamed x42, local copies, waits for them, and re-layouts  10.5 us
    pallas_call x2, Pallas kernels, projected(): call(kernel, (n // step,), 0, [pl.BlockSpec((step, d), lambda i: (i, 0)),...  9.82 us
  transfers between devices with their start and end apart: 39, of which 25 were waited for; matrix products, arithmetic and copies ran while one was open for 3% of the time, Pallas kernels for 16%

profile of v5, /device:TPU:32, one launch (start us, length us, event | category | flops | bytes accessed | tf_op | source)
XLA Modules:
  0.0 249.4 jit_solution(7054004449933391993)
XLA Ops:
  10.3 3.0 %collective-permute-start.3 = (bf16[32,640]{1,0:T(8,128)(2,1)S(1)}, bf16[32,640]{1,0:T(8,128)(2,1)S(1)}, u32[]{:S(2)}, u32[]{:S(2)}) collective-permute-start(bf16[32,640]{1,0:T(8,128)(2,1)S(1)} %get-tuple-element.24), channel_id=1, source_target_pairs={{0,1},{1,129},{128,0},{129,128},{2,3},{3,131},{130,2},{131,130},{4... | collective-permute-start | bytes 122888 | tf_op jit(solution)/shard_map/ppermute | solution.py:38
  13.3 2.2 collective-permute-done.3
  16.5 8.6 %all-to-all-start = ((bf16[8,2,32,640]{3,2,1,0:T(8,128)(2,1)}), bf16[8,2,32,640]{3,2,1,0:T(8,128)(2,1)S(1)}, u32[]{:S(2)}, u32[]{:S(2)}) async-start(bf16[8,2,32,640]{3,2,1,0:T(8,128)(2,1)} %broadcast_in_dim.10), calls=%async_computation | async-start | bytes 1310720 | tf_op jit(solution)/shard_map/all_to_all | solution.py:19
  25.0 2.5 %collective-permute-start.6 = (bf16[512,512]{1,0:T(8,128)(2,1)S(1)}, bf16[512,512]{1,0:T(8,128)(2,1)S(1)}, u32[]{:S(2)}, u32[]{:S(2)}) collective-permute-start(bf16[512,512]{1,0:T(8,128)(2,1)S(1)} %copy-done.16), channel_id=1, source_target_pairs={{0,130},{2,128},{128,2},{130,0},{1,131},{3,129},{129,3},{131,1},{4... | collective-permute-start | bytes 1572872 | tf_op jit(solution)/shard_map/ppermute | solution.py:29
  29.8 13.6 %all-to-all-done = bf16[8,2,32,640]{3,2,1,0:T(8,128)(2,1)S(1)} async-done(((bf16[8,2,32,640]{3,2,1,0:T(8,128)(2,1)}), bf16[8,2,32,640]{3,2,1,0:T(8,128)(2,1)S(1)}, u32[]{:S(2)}, u32[]{:S(2)}) %all-to-all-start) | async-done | bytes 655392 | tf_op jit(solution)/shard_map/all_to_all | solution.py:19
  44.4 7.5 %collective-permute-done.4 = bf16[512,512]{1,0:T(8,128)(2,1)S(1)} collective-permute-done((bf16[512,512]{1,0:T(8,128)(2,1)S(1)}, bf16[512,512]{1,0:T(8,128)(2,1)S(1)}, u32[]{:S(2)}, u32[]{:S(2)}) %collective-permute-start.4) | collective-permute-done | bytes 524320 | tf_op jit(solution)/shard_map/ppermute | solution.py:29
  52.7 1.7 pad_maximum_fusion.mine_ref
  55.4 1.8 collective-permute-start.1
  57.2 6.2 %collective-permute-done.1 = bf16[32,2304]{1,0:T(8,128)(2,1)S(1)} collective-permute-done((bf16[32,2304]{1,0:T(8,128)(2,1)S(1)}, bf16[32,2304]{1,0:T(8,128)(2,1)S(1)}, u32[]{:S(2)}, u32[]{:S(2)}) %collective-permute-start.1) | collective-permute-done | bytes 147488 | tf_op jit(solution)/shard_map/ppermute | solution.py:38
  64.2 3.8 %shard_map.102.x_ref = bf16[1024,2048]{1,0:T(8,128)(2,1)S(1)} custom-call(s32[1]{0:T(128)} %bitcast.me_ref, bf16[4,512,512]{2,1,0:T(8,128)(2,1)S(1)} %pad_maximum_fusion.mine_ref, bf16[4,512,512]{2,1,0:T(8,128)(2,1)} %collective-permute-done.7.theirs_ref, f32[1,2048]{1,0:T(1,128)S(1)} %bitcast.48), custom_call_target="tpu_custom_call" | custom-call | flops 26214400 | bytes 8388608 | tf_op jit(solution)/shard_map/pallas_call | solution.py:92
  67.9 2.1 copy-done.2
  70.9 4.8 %shard_map.104 = bf16[1024,128]{1,0:T(8,128)(2,1)} custom-call(bf16[1024,2048]{1,0:T(8,128)(2,1)} %copy-done.2, bf16[32,2,32,384]{3,2,1,0:T(8,128)(2,1)} %all-gather.4.cloned.1.call-done.w_ref), custom_call_target="tpu_custom_call" | custom-call | flops 536870912 | bytes 4980736 | tf_op jit(solution)/shard_map/pallas_call | solution.py:196
  77.2 3.8 %collective-permute-start.8 = (bf16[2,512,128]{2,1,0:T(8,128)(2,1)}, bf16[2,512,128]{2,1,0:T(8,128)(2,1)S(1)}, u32[]{:S(2)}, u32[]{:S(2)}) collective-permute-start(bf16[2,512,128]{2,1,0:T(8,128)(2,1)} %bitcast.53), channel_id=1, source_target_pairs={{0,8},{4,12},{8,16},{12,20},{16,24},{20,28},{24,32},{28,36},{32,40... | collective-permute-start | bytes 786440 | tf_op jit(solution)/shard_map/ppermute | solution.py:392
  81.0 5.2 %collective-permute-done.9 = bf16[2,512,128]{2,1,0:T(8,128)(2,1)S(1)} collective-permute-done((bf16[2,512,128]{2,1,0:T(8,128)(2,1)}, bf16[2,512,128]{2,1,0:T(8,128)(2,1)S(1)}, u32[]{:S(2)}, u32[]{:S(2)}) %collective-permute-start.9) | collective-permute-done | bytes 262176 | tf_op jit(solution)/shard_map/ppermute | solution.py:392
  86.3 15.8 %collective-permute-done.8 = bf16[2,512,128]{2,1,0:T(8,128)(2,1)S(1)} collective-permute-done((bf16[2,512,128]{2,1,0:T(8,128)(2,1)}, bf16[2,512,128]{2,1,0:T(8,128)(2,1)S(1)}, u32[]{:S(2)}, u32[]{:S(2)}) %collective-permute-start.8) | collective-permute-done | bytes 262176 | tf_op jit(solution)/shard_map/ppermute | solution.py:392
  104.4 3.5 %all-to-all-start.1 = ((bf16[4,8,2,32,256]{4,3,2,1,0:T(8,128)(2,1)}), bf16[4,8,2,32,256]{4,3,2,1,0:T(8,128)(2,1)S(1)}, u32[]{:S(2)}, u32[]{:S(2)}) async-start(bf16[4,8,2,32,256]{4,3,2,1,0:T(8,128)(2,1)} %broadcast_in_dim.24), calls=%async_computation.1 | async-start | bytes 2097152 | tf_op jit(solution)/shard_map/all_to_all | solution.py:19
  108.1 5.0 %shard_map.103 = bf16[1024,256]{1,0:T(8,128)(2,1)} custom-call(bf16[1024,2048]{1,0:T(8,128)(2,1)} %copy-done.2, bf16[32,2,32,384]{3,2,1,0:T(8,128)(2,1)} %all-gather.4.cloned.1.call-done.w_ref), custom_call_target="tpu_custom_call" | custom-call | flops 1073741824 | bytes 5767168 | tf_op jit(solution)/shard_map/pallas_call | solution.py:196
  114.2 3.6 %shard_map.105.left_ref = bf16[2,256,256]{2,1,0:T(8,128)(2,1)S(1)} custom-call(s32[3]{0:T(128)S(1)} %pad_add_fusion.first_ref, bf16[2,512,256]{2,1,0:T(8,128)(2,1)S(1)} %bitcast.40, bf16[2,1536,128]{2,1,0:T(8,128)(2,1)S(1)} %pad_maximum_fusion.3.mine_ref, bf16[2,1536,128]{2,1,0:T(8,128)(2,1)S(1)} %collective-permute-done.10.other_ref), custom_call_target="tpu_custom_call" | custom-call | flops 671088640 | bytes 2097152 | tf_op jit(solution)/shard_map/pallas_call | solution.py:298
  117.7 6.2 %all-to-all-done.1 = bf16[4,8,2,32,256]{4,3,2,1,0:T(8,128)(2,1)S(1)} async-done(((bf16[4,8,2,32,256]{4,3,2,1,0:T(8,128)(2,1)}), bf16[4,8,2,32,256]{4,3,2,1,0:T(8,128)(2,1)S(1)}, u32[]{:S(2)}, u32[]{:S(2)}) %all-to-all-start.1) | async-done | bytes 1048608 | tf_op jit(solution)/shard_map/all_to_all | solution.py:19
  125.4 3.6 %shard_map.108.left_ref = bf16[2,256,256]{2,1,0:T(8,128)(2,1)S(1)} custom-call(s32[3]{0:T(128)S(1)} %pad_add_fusion.first_ref, bf16[2,512,256]{2,1,0:T(8,128)(2,1)S(1)} %bitcast.41, bf16[2,1536,128]{2,1,0:T(8,128)(2,1)S(1)} %pad_maximum_fusion.3.mine_ref, bf16[2,1536,128]{2,1,0:T(8,128)(2,1)S(1)} %collective-permute-done.10.other_ref), custom_call_target="tpu_custom_call" | custom-call | flops 671088640 | bytes 2097152 | tf_op jit(solution)/shard_map/pallas_call | solution.py:298
  131.3 2.9 %collective-permute-start.14 = (bf16[256,512]{1,0:T(8,128)(2,1)S(1)}, bf16[256,512]{1,0:T(8,128)(2,1)S(1)}, u32[]{:S(2)}, u32[]{:S(2)}) collective-permute-start(bf16[256,512]{1,0:T(8,128)(2,1)S(1)} %get-tuple-element.52), channel_id=1, source_target_pairs={{0,130},{2,128},{128,2},{130,0},{1,131},{3,129},{129,3},{131,1},{4... | collective-permute-start | bytes 786440 | tf_op jit(solution)/shard_map/ppermute | solution.py:29
  136.6 2.9 %collective-permute-start.26 = (bf16[256,512]{1,0:T(8,128)(2,1)S(1)}, bf16[256,512]{1,0:T(8,128)(2,1)S(1)}, u32[]{:S(2)}, u32[]{:S(2)}) collective-permute-start(bf16[256,512]{1,0:T(8,128)(2,1)S(1)} %get-tuple-element.55), channel_id=1, source_target_pairs={{0,130},{2,128},{128,2},{130,0},{1,131},{3,129},{129,3},{131,1},{4... | collective-permute-start | bytes 786440 | tf_op jit(solution)/shard_map/ppermute | solution.py:29
  139.5 3.2 %collective-permute-done.14 = bf16[256,512]{1,0:T(8,128)(2,1)S(1)} collective-permute-done((bf16[256,512]{1,0:T(8,128)(2,1)S(1)}, bf16[256,512]{1,0:T(8,128)(2,1)S(1)}, u32[]{:S(2)}, u32[]{:S(2)}) %collective-permute-start.14) | collective-permute-done | bytes 262176 | tf_op jit(solution)/shard_map/ppermute | solution.py:29
  144.4 4.5 %collective-permute-done.12 = bf16[256,512]{1,0:T(8,128)(2,1)S(1)} collective-permute-done((bf16[256,512]{1,0:T(8,128)(2,1)S(1)}, bf16[256,512]{1,0:T(8,128)(2,1)S(1)}, u32[]{:S(2)}, u32[]{:S(2)}) %collective-permute-start.12) | collective-permute-done | bytes 262176 | tf_op jit(solution)/shard_map/ppermute | solution.py:29
  149.1 3.0 %collective-permute-done.26 = bf16[256,512]{1,0:T(8,128)(2,1)S(1)} collective-permute-done((bf16[256,512]{1,0:T(8,128)(2,1)S(1)}, bf16[256,512]{1,0:T(8,128)(2,1)S(1)}, u32[]{:S(2)}, u32[]{:S(2)}) %collective-permute-start.26) | collective-permute-done | bytes 262176 | tf_op jit(solution)/shard_map/ppermute | solution.py:29
  152.1 2.6 %collective-permute-done.25 = bf16[256,512]{1,0:T(8,128)(2,1)S(1)} collective-permute-done((bf16[256,512]{1,0:T(8,128)(2,1)S(1)}, bf16[256,512]{1,0:T(8,128)(2,1)S(1)}, u32[]{:S(2)}, u32[]{:S(2)}) %collective-permute-start.25) | collective-permute-done | bytes 262176 | tf_op jit(solution)/shard_map/ppermute | solution.py:29
  154.6 4.3 %collective-permute-done.24 = bf16[256,512]{1,0:T(8,128)(2,1)S(1)} collective-permute-done((bf16[256,512]{1,0:T(8,128)(2,1)S(1)}, bf16[256,512]{1,0:T(8,128)(2,1)S(1)}, u32[]{:S(2)}, u32[]{:S(2)}) %collective-permute-start.24) | collective-permute-done | bytes 262176 | tf_op jit(solution)/shard_map/ppermute | solution.py:29
  159.1 2.9 %collective-permute-start.29 = (bf16[256,512]{1,0:T(8,128)(2,1)S(1)}, bf16[256,512]{1,0:T(8,128)(2,1)S(1)}, u32[]{:S(2)}, u32[]{:S(2)}) collective-permute-start(bf16[256,512]{1,0:T(8,128)(2,1)S(1)} %fusion.7), channel_id=1, source_target_pairs={{0,130},{2,128},{128,2},{130,0},{1,131},{3,129},{129,3},{131,1},{4... | collective-permute-start | bytes 786440 | tf_op jit(solution)/shard_map/ppermute | solution.py:29
  162.0 1.9 collective-permute-start.27
  163.9 4.8 %collective-permute-done.29 = bf16[256,512]{1,0:T(8,128)(2,1)S(1)} collective-permute-done((bf16[256,512]{1,0:T(8,128)(2,1)S(1)}, bf16[256,512]{1,0:T(8,128)(2,1)S(1)}, u32[]{:S(2)}, u32[]{:S(2)}) %collective-permute-start.29) | collective-permute-done | bytes 262176 | tf_op jit(solution)/shard_map/ppermute | solution.py:29
  168.7 2.5 collective-permute-done.28
  171.1 3.2 %collective-permute-done.27 = bf16[256,512]{1,0:T(8,128)(2,1)S(1)} collective-permute-done((bf16[256,512]{1,0:T(8,128)(2,1)S(1)}, bf16[256,512]{1,0:T(8,128)(2,1)S(1)}, u32[]{:S(2)}, u32[]{:S(2)}) %collective-permute-start.27) | collective-permute-done | bytes 262176 | tf_op jit(solution)/shard_map/ppermute | solution.py:29
  174.5 2.9 %collective-permute-start.17 = (bf16[256,512]{1,0:T(8,128)(2,1)S(1)}, bf16[256,512]{1,0:T(8,128)(2,1)S(1)}, u32[]{:S(2)}, u32[]{:S(2)}) collective-permute-start(bf16[256,512]{1,0:T(8,128)(2,1)S(1)} %fusion.15), channel_id=1, source_target_pairs={{0,130},{2,128},{128,2},{130,0},{1,131},{3,129},{129,3},{131,1},{4... | collective-permute-start | bytes 786440 | tf_op jit(solution)/shard_map/ppermute | solution.py:29
  177.4 1.9 collective-permute-start.15
  179.3 5.1 %collective-permute-done.17 = bf16[256,512]{1,0:T(8,128)(2,1)S(1)} collective-permute-done((bf16[256,512]{1,0:T(8,128)(2,1)S(1)}, bf16[256,512]{1,0:T(8,128)(2,1)S(1)}, u32[]{:S(2)}, u32[]{:S(2)}) %collective-permute-start.17) | collective-permute-done | bytes 262176 | tf_op jit(solution)/shard_map/ppermute | solution.py:29
  184.5 2.1 collective-permute-done.16
  186.6 4.7 %collective-permute-done.15 = bf16[256,512]{1,0:T(8,128)(2,1)S(1)} collective-permute-done((bf16[256,512]{1,0:T(8,128)(2,1)S(1)}, bf16[256,512]{1,0:T(8,128)(2,1)S(1)}, u32[]{:S(2)}, u32[]{:S(2)}) %collective-permute-start.15) | collective-permute-done | bytes 262176 | tf_op jit(solution)/shard_map/ppermute | solution.py:29
  191.8 3.7 %copy-done = bf16[64,32,2304]{2,1,0:T(8,128)(2,1)S(1)} copy-done((bf16[64,32,2304]{2,1,0:T(8,128)(2,1)S(1)}, bf16[64,32,2304]{2,1,0:T(8,128)(2,1)}, u32[]{:S(2)}) %copy-start) | copy-done | bytes 9437208
  195.4 7.9 %shard_map.110 = (f32[512,1024]{1,0:T(8,128)S(1)}, bf16[512,1024]{1,0:T(8,128)(2,1)S(1)}) custom-call(s32[1]{0:T(128)} %bitcast.me_ref, bf16[4,256,512]{2,1,0:T(8,128)(2,1)S(1)} %pad_maximum_fusion.2.mine_ref, bf16[4,256,512]{2,1,0:T(8,128)(2,1)S(1)} %collective-permute-done.30.theirs_ref, f32[1,2048]{1,0:T(1,128)S(1)} %bitcast.46, ...), custom_call_target="tpu_custom_call" | custom-call | flops 4831838208 | bytes 13631488 | tf_op jit(solution)/shard_map/pallas_call | solution.py:164
  203.9 9.0 %shard_map.107 = (f32[512,1024]{1,0:T(8,128)S(1)}, bf16[512,1024]{1,0:T(8,128)(2,1)S(1)}) custom-call(s32[1]{0:T(128)} %bitcast.me_ref, bf16[4,256,512]{2,1,0:T(8,128)(2,1)S(1)} %pad_maximum_fusion.1.mine_ref, bf16[4,256,512]{2,1,0:T(8,128)(2,1)} %collective-permute-done.18.theirs_ref, f32[1,2048]{1,0:T(1,128)S(1)} %bitcast.47, ...), custom_call_target="tpu_custom_call" | custom-call | flops 4831838208 | bytes 13631488 | tf_op jit(solution)/shard_map/pallas_call | solution.py:164
  213.5 2.9 %collective-permute-start.34 = (bf16[256,512]{1,0:T(8,128)(2,1)S(1)}, bf16[256,512]{1,0:T(8,128)(2,1)S(1)}, u32[]{:S(2)}, u32[]{:S(2)}) collective-permute-start(bf16[256,512]{1,0:T(8,128)(2,1)S(1)} %get-tuple-element.49), channel_id=1, source_target_pairs={{0,130},{2,128},{128,2},{130,0},{1,131},{3,129},{129,3},{131,1},{4... | collective-permute-start | bytes 786440 | tf_op jit(solution)/shard_map/ppermute | solution.py:29
  216.4 1.9 collective-permute-start.32
  218.9 2.9 %collective-permute-start.22 = (bf16[256,512]{1,0:T(8,128)(2,1)S(1)}, bf16[256,512]{1,0:T(8,128)(2,1)S(1)}, u32[]{:S(2)}, u32[]{:S(2)}) collective-permute-start(bf16[256,512]{1,0:T(8,128)(2,1)S(1)} %get-tuple-element.46), channel_id=1, source_target_pairs={{0,130},{2,128},{128,2},{130,0},{1,131},{3,129},{129,3},{131,1},{4... | collective-permute-start | bytes 786440 | tf_op jit(solution)/shard_map/ppermute | solution.py:29
  221.7 2.4 collective-permute-done.34
  225.6 5.6 %collective-permute-done.32 = bf16[256,512]{1,0:T(8,128)(2,1)S(1)} collective-permute-done((bf16[256,512]{1,0:T(8,128)(2,1)S(1)}, bf16[256,512]{1,0:T(8,128)(2,1)S(1)}, u32[]{:S(2)}, u32[]{:S(2)}) %collective-permute-start.32) | collective-permute-done | bytes 262176 | tf_op jit(solution)/shard_map/ppermute | solution.py:29
  231.3 3.4 %collective-permute-done.22 = bf16[256,512]{1,0:T(8,128)(2,1)S(1)} collective-permute-done((bf16[256,512]{1,0:T(8,128)(2,1)S(1)}, bf16[256,512]{1,0:T(8,128)(2,1)S(1)}, u32[]{:S(2)}, u32[]{:S(2)}) %collective-permute-start.22) | collective-permute-done | bytes 262176 | tf_op jit(solution)/shard_map/ppermute | solution.py:29
  234.7 2.1 collective-permute-done.21
  236.9 4.7 %collective-permute-done.20 = bf16[256,512]{1,0:T(8,128)(2,1)S(1)} collective-permute-done((bf16[256,512]{1,0:T(8,128)(2,1)S(1)}, bf16[256,512]{1,0:T(8,128)(2,1)S(1)}, u32[]{:S(2)}, u32[]{:S(2)}) %collective-permute-start.20) | collective-permute-done | bytes 262176 | tf_op jit(solution)/shard_map/ppermute | solution.py:29
  (115 shorter events, 29.5 us)
Async XLA Ops:
  9.4 15.6 %copy-start.16 = (bf16[512,512]{1,0:T(8,128)(2,1)S(1)}, bf16[512,512]{1,0:T(8,128)(2,1)}, u32[]{:S(2)}) copy-start(bf16[512,512]{1,0:T(8,128)(2,1)} %param.10) | copy-start | bytes 1572868
  9.5 3.8 %collective-permute-start.2 = (bf16[32,640]{1,0:T(8,128)(2,1)S(1)}, bf16[32,640]{1,0:T(8,128)(2,1)S(1)}, u32[]{:S(2)}, u32[]{:S(2)}) collective-permute-start(bf16[32,640]{1,0:T(8,128)(2,1)S(1)} %get-tuple-element.23), channel_id=1, source_target_pairs={{0,0},{1,128},{128,1},{129,129},{2,2},{3,130},{130,3},{131,131},{4... | collective-permute-start | bytes 122888 | tf_op jit(solution)/shard_map/ppermute | solution.py:38
  10.3 5.2 %collective-permute-start.3 = (bf16[32,640]{1,0:T(8,128)(2,1)S(1)}, bf16[32,640]{1,0:T(8,128)(2,1)S(1)}, u32[]{:S(2)}, u32[]{:S(2)}) collective-permute-start(bf16[32,640]{1,0:T(8,128)(2,1)S(1)} %get-tuple-element.24), channel_id=1, source_target_pairs={{0,1},{1,129},{128,0},{129,128},{2,3},{3,131},{130,2},{131,130},{4... | collective-permute-start | bytes 122888 | tf_op jit(solution)/shard_map/ppermute | solution.py:38
  16.5 27.0 %all-to-all-start = ((bf16[8,2,32,640]{3,2,1,0:T(8,128)(2,1)}), bf16[8,2,32,640]{3,2,1,0:T(8,128)(2,1)S(1)}, u32[]{:S(2)}, u32[]{:S(2)}) async-start(bf16[8,2,32,640]{3,2,1,0:T(8,128)(2,1)} %broadcast_in_dim.10), calls=%async_computation | async-start | bytes 1310720 | tf_op jit(solution)/shard_map/all_to_all | solution.py:19
  25.0 45.8 %all-gather.4.cloned.1.call-start = ((), (), s32[]{:S(2)}) async-start(), calls=%async_computation.2 | async-start | bytes 1966080 | tf_op jit(solution)/shard_map/all_gather | solution.py:382
  25.0 19.3 %collective-permute-start.6 = (bf16[512,512]{1,0:T(8,128)(2,1)S(1)}, bf16[512,512]{1,0:T(8,128)(2,1)S(1)}, u32[]{:S(2)}, u32[]{:S(2)}) collective-permute-start(bf16[512,512]{1,0:T(8,128)(2,1)S(1)} %copy-done.16), channel_id=1, source_target_pairs={{0,130},{2,128},{128,2},{130,0},{1,131},{3,129},{129,3},{131,1},{4... | collective-permute-start | bytes 1572872 | tf_op jit(solution)/shard_map/ppermute | solution.py:29
  27.6 16.8 %collective-permute-start.5 = (bf16[512,512]{1,0:T(8,128)(2,1)S(1)}, bf16[512,512]{1,0:T(8,128)(2,1)S(1)}, u32[]{:S(2)}, u32[]{:S(2)}) collective-permute-start(bf16[512,512]{1,0:T(8,128)(2,1)S(1)} %copy-done.16), channel_id=1, source_target_pairs={{0,128},{2,130},{128,0},{130,2},{1,129},{3,131},{129,1},{131,3},{4... | collective-permute-start | bytes 1572872 | tf_op jit(solution)/shard_map/ppermute | solution.py:29
  28.2 23.7 %collective-permute-start.4 = (bf16[512,512]{1,0:T(8,128)(2,1)S(1)}, bf16[512,512]{1,0:T(8,128)(2,1)S(1)}, u32[]{:S(2)}, u32[]{:S(2)}) collective-permute-start(bf16[512,512]{1,0:T(8,128)(2,1)S(1)} %copy-done.16), channel_id=1, source_target_pairs={{0,2},{2,0},{128,130},{130,128},{1,3},{3,1},{129,131},{131,129},{4... | collective-permute-start | bytes 1572872 | tf_op jit(solution)/shard_map/ppermute | solution.py:29
  44.3 147.5 %all-gather.6.cloned.1.call-start = ((), (), s32[]{:S(2)}) async-start(), calls=%async_computation.3 | async-start | bytes 9732096 | tf_op jit(solution)/shard_map/all_gather | solution.py:385
  44.3 7.6 %copy-start.18 = (bf16[512,512]{1,0:T(8,128)(2,1)}, bf16[512,512]{1,0:T(8,128)(2,1)S(1)}, u32[]{:S(2)}) copy-start(bf16[512,512]{1,0:T(8,128)(2,1)S(1)} %collective-permute-done.6) | copy-start | bytes 1572868
  44.3 7.5 %copy-start.19 = (bf16[512,512]{1,0:T(8,128)(2,1)}, bf16[512,512]{1,0:T(8,128)(2,1)S(1)}, u32[]{:S(2)}) copy-start(bf16[512,512]{1,0:T(8,128)(2,1)S(1)} %collective-permute-done.5) | copy-start | bytes 1572868
  52.7 11.5 %copy-start.11 = (f32[2048]{0:T(1024)S(1)}, f32[2048]{0:T(1024)}, u32[]{:S(2)}) copy-start(f32[2048]{0:T(1024)} %param.11) | copy-start | bytes 24580
  54.4 9.7 %collective-permute-start.7 = (bf16[4,512,512]{2,1,0:T(8,128)(2,1)S(1)}, bf16[4,512,512]{2,1,0:T(8,128)(2,1)}, u32[]{:S(2)}, u32[]{:S(2)}) collective-permute-start(bf16[4,512,512]{2,1,0:T(8,128)(2,1)S(1)} %pad_maximum_fusion.mine_ref), channel_id=1, source_target_pairs={{0,1},{1,0},{2,3},{3,2},{4,5},{5,4},{6,7},{7,6},{8,9},{9,8},{10,11... | collective-permute-start | bytes 6291464 | tf_op jit(solution)/shard_map/ppermute | solution.py:25
  54.7 2.5 collective-permute-start
  55.4 8.0 %collective-permute-start.1 = (bf16[32,2304]{1,0:T(8,128)(2,1)S(1)}, bf16[32,2304]{1,0:T(8,128)(2,1)S(1)}, u32[]{:S(2)}, u32[]{:S(2)}) collective-permute-start(bf16[32,2304]{1,0:T(8,128)(2,1)S(1)} %get-tuple-element.22), channel_id=1, source_target_pairs={{0,1},{1,129},{128,0},{129,128},{2,3},{3,131},{130,2},{131,130},{4... | collective-permute-start | bytes 442376 | tf_op jit(solution)/shard_map/ppermute | solution.py:38
  75.7 10.6 %collective-permute-start.9 = (bf16[2,512,128]{2,1,0:T(8,128)(2,1)}, bf16[2,512,128]{2,1,0:T(8,128)(2,1)S(1)}, u32[]{:S(2)}, u32[]{:S(2)}) collective-permute-start(bf16[2,512,128]{2,1,0:T(8,128)(2,1)} %bitcast.52), channel_id=1, source_target_pairs={{0,4},{4,8},{8,12},{12,16},{16,20},{20,24},{24,28},{28,32},{32,36}... | collective-permute-start | bytes 786440 | tf_op jit(solution)/shard_map/ppermute | solution.py:392
  77.2 24.9 %collective-permute-start.8 = (bf16[2,512,128]{2,1,0:T(8,128)(2,1)}, bf16[2,512,128]{2,1,0:T(8,128)(2,1)S(1)}, u32[]{:S(2)}, u32[]{:S(2)}) collective-permute-start(bf16[2,512,128]{2,1,0:T(8,128)(2,1)} %bitcast.53), channel_id=1, source_target_pairs={{0,8},{4,12},{8,16},{12,20},{16,24},{20,28},{24,32},{28,36},{32,40... | collective-permute-start | bytes 786440 | tf_op jit(solution)/shard_map/ppermute | solution.py:392
  103.2 10.0 %collective-permute-start.10 = (bf16[2,1536,128]{2,1,0:T(8,128)(2,1)S(1)}, bf16[2,1536,128]{2,1,0:T(8,128)(2,1)S(1)}, u32[]{:S(2)}, u32[]{:S(2)}) collective-permute-start(bf16[2,1536,128]{2,1,0:T(8,128)(2,1)S(1)} %pad_maximum_fusion.3.mine_ref), channel_id=1, source_target_pairs={{0,1},{1,0},{2,3},{3,2},{4,5},{5,4},{6,7},{7,6},{8,9},{9,8},{10,11... | collective-permute-start | bytes 2359304 | tf_op jit(solution)/shard_map/ppermute | solution.py:25
  104.4 19.5 %all-to-all-start.1 = ((bf16[4,8,2,32,256]{4,3,2,1,0:T(8,128)(2,1)}), bf16[4,8,2,32,256]{4,3,2,1,0:T(8,128)(2,1)S(1)}, u32[]{:S(2)}, u32[]{:S(2)}) async-start(bf16[4,8,2,32,256]{4,3,2,1,0:T(8,128)(2,1)} %broadcast_in_dim.24), calls=%async_computation.1 | async-start | bytes 2097152 | tf_op jit(solution)/shard_map/all_to_all | solution.py:19
  114.2 11.2 %copy-start.4 = (bf16[1024,256]{1,0:T(8,128)(2,1)S(1)}, bf16[1024,256]{1,0:T(8,128)(2,1)}, u32[]{:S(2)}) copy-start(bf16[1024,256]{1,0:T(8,128)(2,1)} %shard_map.103) | copy-start | bytes 1572868
  125.1 5.7 %collective-permute-start.11 = (bf16[512,1024]{1,0:T(8,128)(2,1)S(1)}, bf16[512,1024]{1,0:T(8,128)(2,1)S(1)}, u32[]{:S(2)}, u32[]{:S(2)}) collective-permute-start(bf16[512,1024]{1,0:T(8,128)(2,1)S(1)} %get-tuple-element.28), channel_id=1, source_target_pairs={{0,1},{1,0},{2,3},{3,2},{4,5},{5,4},{6,7},{7,6},{8,9},{9,8},{10,11... | collective-permute-start | bytes 3145736 | tf_op jit(solution)/shard_map/ppermute | solution.py:25
  130.2 5.9 %collective-permute-start.23 = (bf16[512,1024]{1,0:T(8,128)(2,1)S(1)}, bf16[512,1024]{1,0:T(8,128)(2,1)S(1)}, u32[]{:S(2)}, u32[]{:S(2)}) collective-permute-start(bf16[512,1024]{1,0:T(8,128)(2,1)S(1)} %get-tuple-element.34), channel_id=1, source_target_pairs={{0,1},{1,0},{2,3},{3,2},{4,5},{5,4},{6,7},{7,6},{8,9},{9,8},{10,11... | collective-permute-start | bytes 3145736 | tf_op jit(solution)/shard_map/ppermute | solution.py:25
  131.3 11.4 %collective-permute-start.14 = (bf16[256,512]{1,0:T(8,128)(2,1)S(1)}, bf16[256,512]{1,0:T(8,128)(2,1)S(1)}, u32[]{:S(2)}, u32[]{:S(2)}) collective-permute-start(bf16[256,512]{1,0:T(8,128)(2,1)S(1)} %get-tuple-element.52), channel_id=1, source_target_pairs={{0,130},{2,128},{128,2},{130,0},{1,131},{3,129},{129,3},{131,1},{4... | collective-permute-start | bytes 786440 | tf_op jit(solution)/shard_map/ppermute | solution.py:29
  134.2 10.2 %collective-permute-start.13 = (bf16[256,512]{1,0:T(8,128)(2,1)S(1)}, bf16[256,512]{1,0:T(8,128)(2,1)S(1)}, u32[]{:S(2)}, u32[]{:S(2)}) collective-permute-start(bf16[256,512]{1,0:T(8,128)(2,1)S(1)} %get-tuple-element.53), channel_id=1, source_target_pairs={{0,128},{2,130},{128,0},{130,2},{1,129},{3,131},{129,1},{131,3},{4... | collective-permute-start | bytes 786440 | tf_op jit(solution)/shard_map/ppermute | solution.py:29
  134.4 14.5 %collective-permute-start.12 = (bf16[256,512]{1,0:T(8,128)(2,1)S(1)}, bf16[256,512]{1,0:T(8,128)(2,1)S(1)}, u32[]{:S(2)}, u32[]{:S(2)}) collective-permute-start(bf16[256,512]{1,0:T(8,128)(2,1)S(1)} %get-tuple-element.51), channel_id=1, source_target_pairs={{0,2},{2,0},{128,130},{130,128},{1,3},{3,1},{129,131},{131,129},{4... | collective-permute-start | bytes 786440 | tf_op jit(solution)/shard_map/ppermute | solution.py:29
  136.6 15.5 %collective-permute-start.26 = (bf16[256,512]{1,0:T(8,128)(2,1)S(1)}, bf16[256,512]{1,0:T(8,128)(2,1)S(1)}, u32[]{:S(2)}, u32[]{:S(2)}) collective-permute-start(bf16[256,512]{1,0:T(8,128)(2,1)S(1)} %get-tuple-element.55), channel_id=1, source_target_pairs={{0,130},{2,128},{128,2},{130,0},{1,131},{3,129},{129,3},{131,1},{4... | collective-permute-start | bytes 786440 | tf_op jit(solution)/shard_map/ppermute | solution.py:29
  139.5 15.1 %collective-permute-start.25 = (bf16[256,512]{1,0:T(8,128)(2,1)S(1)}, bf16[256,512]{1,0:T(8,128)(2,1)S(1)}, u32[]{:S(2)}, u32[]{:S(2)}) collective-permute-start(bf16[256,512]{1,0:T(8,128)(2,1)S(1)} %get-tuple-element.56), channel_id=1, source_target_pairs={{0,128},{2,130},{128,0},{130,2},{1,129},{3,131},{129,1},{131,3},{4... | collective-permute-start | bytes 786440 | tf_op jit(solution)/shard_map/ppermute | solution.py:29
  142.7 16.2 %collective-permute-start.24 = (bf16[256,512]{1,0:T(8,128)(2,1)S(1)}, bf16[256,512]{1,0:T(8,128)(2,1)S(1)}, u32[]{:S(2)}, u32[]{:S(2)}) collective-permute-start(bf16[256,512]{1,0:T(8,128)(2,1)S(1)} %get-tuple-element.54), channel_id=1, source_target_pairs={{0,2},{2,0},{128,130},{130,128},{1,3},{3,1},{129,131},{131,129},{4... | collective-permute-start | bytes 786440 | tf_op jit(solution)/shard_map/ppermute | solution.py:29
  159.1 15.2 %copy-start.14 = (bf16[256,512]{1,0:T(8,128)(2,1)}, bf16[256,512]{1,0:T(8,128)(2,1)S(1)}, u32[]{:S(2)}) copy-start(bf16[256,512]{1,0:T(8,128)(2,1)S(1)} %fusion.7) | copy-start | bytes 786436
  159.1 9.6 %collective-permute-start.29 = (bf16[256,512]{1,0:T(8,128)(2,1)S(1)}, bf16[256,512]{1,0:T(8,128)(2,1)S(1)}, u32[]{:S(2)}, u32[]{:S(2)}) collective-permute-start(bf16[256,512]{1,0:T(8,128)(2,1)S(1)} %fusion.7), channel_id=1, source_target_pairs={{0,130},{2,128},{128,2},{130,0},{1,131},{3,129},{129,3},{131,1},{4... | collective-permute-start | bytes 786440 | tf_op jit(solution)/shard_map/ppermute | solution.py:29
  162.0 9.2 %collective-permute-start.28 = (bf16[256,512]{1,0:T(8,128)(2,1)S(1)}, bf16[256,512]{1,0:T(8,128)(2,1)S(1)}, u32[]{:S(2)}, u32[]{:S(2)}) collective-permute-start(bf16[256,512]{1,0:T(8,128)(2,1)S(1)} %fusion.7), channel_id=1, source_target_pairs={{0,128},{2,130},{128,0},{130,2},{1,129},{3,131},{129,1},{131,3},{4... | collective-permute-start | bytes 786440 | tf_op jit(solution)/shard_map/ppermute | solution.py:29
  162.0 12.3 %collective-permute-start.27 = (bf16[256,512]{1,0:T(8,128)(2,1)S(1)}, bf16[256,512]{1,0:T(8,128)(2,1)S(1)}, u32[]{:S(2)}, u32[]{:S(2)}) collective-permute-start(bf16[256,512]{1,0:T(8,128)(2,1)S(1)} %fusion.7), channel_id=1, source_target_pairs={{0,2},{2,0},{128,130},{130,128},{1,3},{3,1},{129,131},{131,129},{4... | collective-permute-start | bytes 786440 | tf_op jit(solution)/shard_map/ppermute | solution.py:29
  174.3 17.5 %copy-start.10 = (f32[2048]{0:T(1024)S(1)}, f32[2048]{0:T(1024)}, u32[]{:S(2)}) copy-start(f32[2048]{0:T(1024)} %param.16) | copy-start | bytes 24580
  174.4 17.3 %collective-permute-start.30 = (bf16[4,256,512]{2,1,0:T(8,128)(2,1)S(1)}, bf16[4,256,512]{2,1,0:T(8,128)(2,1)S(1)}, u32[]{:S(2)}, u32[]{:S(2)}) collective-permute-start(bf16[4,256,512]{2,1,0:T(8,128)(2,1)S(1)} %pad_maximum_fusion.2.mine_ref), channel_id=1, source_target_pairs={{0,1},{1,0},{2,3},{3,2},{4,5},{5,4},{6,7},{7,6},{8,9},{9,8},{10,11... | collective-permute-start | bytes 3145736 | tf_op jit(solution)/shard_map/ppermute | solution.py:25
  174.5 9.9 %collective-permute-start.17 = (bf16[256,512]{1,0:T(8,128)(2,1)S(1)}, bf16[256,512]{1,0:T(8,128)(2,1)S(1)}, u32[]{:S(2)}, u32[]{:S(2)}) collective-permute-start(bf16[256,512]{1,0:T(8,128)(2,1)S(1)} %fusion.15), channel_id=1, source_target_pairs={{0,130},{2,128},{128,2},{130,0},{1,131},{3,129},{129,3},{131,1},{4... | collective-permute-start | bytes 786440 | tf_op jit(solution)/shard_map/ppermute | solution.py:29
  177.4 9.2 %collective-permute-start.16 = (bf16[256,512]{1,0:T(8,128)(2,1)S(1)}, bf16[256,512]{1,0:T(8,128)(2,1)S(1)}, u32[]{:S(2)}, u32[]{:S(2)}) collective-permute-start(bf16[256,512]{1,0:T(8,128)(2,1)S(1)} %fusion.15), channel_id=1, source_target_pairs={{0,128},{2,130},{128,0},{130,2},{1,129},{3,131},{129,1},{131,3},{4... | collective-permute-start | bytes 786440 | tf_op jit(solution)/shard_map/ppermute | solution.py:29
  177.4 13.8 %collective-permute-start.15 = (bf16[256,512]{1,0:T(8,128)(2,1)S(1)}, bf16[256,512]{1,0:T(8,128)(2,1)S(1)}, u32[]{:S(2)}, u32[]{:S(2)}) collective-permute-start(bf16[256,512]{1,0:T(8,128)(2,1)S(1)} %fusion.15), channel_id=1, source_target_pairs={{0,2},{2,0},{128,130},{130,128},{1,3},{3,1},{129,131},{131,129},{4... | collective-permute-start | bytes 786440 | tf_op jit(solution)/shard_map/ppermute | solution.py:29
  191.4 12.5 %collective-permute-start.18 = (bf16[4,256,512]{2,1,0:T(8,128)(2,1)S(1)}, bf16[4,256,512]{2,1,0:T(8,128)(2,1)}, u32[]{:S(2)}, u32[]{:S(2)}) collective-permute-start(bf16[4,256,512]{2,1,0:T(8,128)(2,1)S(1)} %pad_maximum_fusion.1.mine_ref), channel_id=1, source_target_pairs={{0,1},{1,0},{2,3},{3,2},{4,5},{5,4},{6,7},{7,6},{8,9},{9,8},{10,11... | collective-permute-start | bytes 3145736 | tf_op jit(solution)/shard_map/ppermute | solution.py:25
  195.4 8.4 %copy-start.1 = (bf16[64,32,2304]{2,1,0:T(8,128)(2,1)S(1)}, bf16[64,32,2304]{2,1,0:T(8,128)(2,1)}, u32[]{:S(2)}) copy-start(bf16[64,32,2304]{2,1,0:T(8,128)(2,1)} %all-gather.6.cloned.1.call-done) | copy-start | bytes 28311556
  203.3 9.7 %collective-permute-start.31 = (bf16[512,1024]{1,0:T(8,128)(2,1)S(1)}, bf16[512,1024]{1,0:T(8,128)(2,1)S(1)}, u32[]{:S(2)}, u32[]{:S(2)}) collective-permute-start(bf16[512,1024]{1,0:T(8,128)(2,1)S(1)} %get-tuple-element.36), channel_id=1, source_target_pairs={{0,1},{1,0},{2,3},{3,2},{4,5},{5,4},{6,7},{7,6},{8,9},{9,8},{10,11... | collective-permute-start | bytes 3145736 | tf_op jit(solution)/shard_map/ppermute | solution.py:25
  212.9 5.5 %collective-permute-start.19 = (bf16[512,1024]{1,0:T(8,128)(2,1)S(1)}, bf16[512,1024]{1,0:T(8,128)(2,1)S(1)}, u32[]{:S(2)}, u32[]{:S(2)}) collective-permute-start(bf16[512,1024]{1,0:T(8,128)(2,1)S(1)} %get-tuple-element.31), channel_id=1, source_target_pairs={{0,1},{1,0},{2,3},{3,2},{4,5},{5,4},{6,7},{7,6},{8,9},{9,8},{10,11... | collective-permute-start | bytes 3145736 | tf_op jit(solution)/shard_map/ppermute | solution.py:25
  213.5 10.6 %collective-permute-start.34 = (bf16[256,512]{1,0:T(8,128)(2,1)S(1)}, bf16[256,512]{1,0:T(8,128)(2,1)S(1)}, u32[]{:S(2)}, u32[]{:S(2)}) collective-permute-start(bf16[256,512]{1,0:T(8,128)(2,1)S(1)} %get-tuple-element.49), channel_id=1, source_target_pairs={{0,130},{2,128},{128,2},{130,0},{1,131},{3,129},{129,3},{131,1},{4... | collective-permute-start | bytes 786440 | tf_op jit(solution)/shard_map/ppermute | solution.py:29
  216.4 9.2 %collective-permute-start.33 = (bf16[256,512]{1,0:T(8,128)(2,1)S(1)}, bf16[256,512]{1,0:T(8,128)(2,1)S(1)}, u32[]{:S(2)}, u32[]{:S(2)}) collective-permute-start(bf16[256,512]{1,0:T(8,128)(2,1)S(1)} %get-tuple-element.50), channel_id=1, source_target_pairs={{0,128},{2,130},{128,0},{130,2},{1,129},{3,131},{129,1},{131,3},{4... | collective-permute-start | bytes 786440 | tf_op jit(solution)/shard_map/ppermute | solution.py:29
  216.4 14.7 %collective-permute-start.32 = (bf16[256,512]{1,0:T(8,128)(2,1)S(1)}, bf16[256,512]{1,0:T(8,128)(2,1)S(1)}, u32[]{:S(2)}, u32[]{:S(2)}) collective-permute-start(bf16[256,512]{1,0:T(8,128)(2,1)S(1)} %get-tuple-element.48), channel_id=1, source_target_pairs={{0,2},{2,0},{128,130},{130,128},{1,3},{3,1},{129,131},{131,129},{4... | collective-permute-start | bytes 786440 | tf_op jit(solution)/shard_map/ppermute | solution.py:29
  218.3 12.8 %copy-start.15 = (bf16[256,512]{1,0:T(8,128)(2,1)S(1)}, bf16[256,512]{1,0:T(8,128)(2,1)}, u32[]{:S(2)}) copy-start(bf16[256,512]{1,0:T(8,128)(2,1)} %copy-done.14) | copy-start | bytes 786436
  218.9 15.9 %collective-permute-start.22 = (bf16[256,512]{1,0:T(8,128)(2,1)S(1)}, bf16[256,512]{1,0:T(8,128)(2,1)S(1)}, u32[]{:S(2)}, u32[]{:S(2)}) collective-permute-start(bf16[256,512]{1,0:T(8,128)(2,1)S(1)} %get-tuple-element.46), channel_id=1, source_target_pairs={{0,130},{2,128},{128,2},{130,0},{1,131},{3,129},{129,3},{131,1},{4... | collective-permute-start | bytes 786440 | tf_op jit(solution)/shard_map/ppermute | solution.py:29
  221.7 15.1 %collective-permute-start.21 = (bf16[256,512]{1,0:T(8,128)(2,1)S(1)}, bf16[256,512]{1,0:T(8,128)(2,1)S(1)}, u32[]{:S(2)}, u32[]{:S(2)}) collective-permute-start(bf16[256,512]{1,0:T(8,128)(2,1)S(1)} %get-tuple-element.47), channel_id=1, source_target_pairs={{0,128},{2,130},{128,0},{130,2},{1,129},{3,131},{129,1},{131,3},{4... | collective-permute-start | bytes 786440 | tf_op jit(solution)/shard_map/ppermute | solution.py:29
  224.1 17.4 %collective-permute-start.20 = (bf16[256,512]{1,0:T(8,128)(2,1)S(1)}, bf16[256,512]{1,0:T(8,128)(2,1)S(1)}, u32[]{:S(2)}, u32[]{:S(2)}) collective-permute-start(bf16[256,512]{1,0:T(8,128)(2,1)S(1)} %get-tuple-element.45), channel_id=1, source_target_pairs={{0,2},{2,0},{128,130},{130,128},{1,3},{3,1},{129,131},{131,129},{4... | collective-permute-start | bytes 786440 | tf_op jit(solution)/shard_map/ppermute | solution.py:29
  (12 other events, 21.8 us)
Sparse Core Ops, SparseCore 0:
  44.4 26.4 all-gather.3
  73.4 102.5 all-gather.5
